TPU v7x, 8 devices: a whole 2x2x1 slice. The times are simulated.
8 devices in a mesh: dp: 2 (over z, y), sp: 4 (over x, core).
Axes of the slice: x: 2, y: 2, z: 1, core: 2. Of those that a mesh axis runs over, the one named last changes fastest.
Arguments:
- x_in: bfloat16 [32, 1024, 2048], P('dp', 'sp'), parts along dimension 0
- grad_y: bfloat16 [32, 1024, 2048], P('dp', 'sp'), parts along dimension 0
- positions: int32 [32, 1024], P('dp', 'sp'), parts along dimension 0
- g_norm: bfloat16 [2048], replicated
- w_query: bfloat16 [2048, 2048], replicated
- w_key: bfloat16 [2048, 2048], replicated
- w_value: bfloat16 [2048, 2048], replicated
- w_out: bfloat16 [2048, 2048], replicated
- g_query: bfloat16 [2048], replicated
- g_key: bfloat16 [2048], replicated
Outputs:
- output 1: bfloat16 [32, 1024, 2048], P('dp', 'sp'), parts along dimension 0
- output 2: bfloat16 [32, 1024, 2048], P('dp', 'sp'), parts along dimension 0
- output 3: float32 [4096], P(('dp', 'sp')), parts along dimension 0
- output 4: float32 [4096, 2048], P(('dp', 'sp')), parts along dimension 0
- output 5: float32 [4096, 2048], P(('dp', 'sp')), parts along dimension 0
- output 6: float32 [4096, 2048], P(('dp', 'sp')), parts along dimension 0
- output 7: float32 [4096, 2048], P(('dp', 'sp')), parts along dimension 0
- output 8: float32 [4096], P(('dp', 'sp')), parts along dimension 0
- output 9: float32 [4096], P(('dp', 'sp')), parts along dimension 0
There are 2 independent parts. A program takes and returns all parts, laid end to end along the dimension named above; an argument that names none is the same for every part.
All inputs are finite; a program needn't handle non-finite values.
Results may differ from a plain program's by a relative error of at most 0.0114701.
Values are sent between devices in bfloat16 or wider.
A program may use at most 1 GiB of HBM per device.

v0:
```python
import functools
import jax
import jax.numpy as jnp
from jax import lax
from jax.sharding import PartitionSpec as P

HEAD_DIM = 128
QUERY_BLOCK = 128
NORM_EPS = 1e-5
ROPE_BASE = 10000.0
NEG_BIG = -1e30


def rope_tables(positions):
    half_dim = HEAD_DIM // 2
    inv_freq = ROPE_BASE ** (-jnp.arange(half_dim, dtype=jnp.float32) * (2.0 / HEAD_DIM))
    angles = positions.astype(jnp.float32)[..., None] * inv_freq
    return jnp.cos(angles)[:, :, None, :], jnp.sin(angles)[:, :, None, :]


def rope_apply(values, cos_t, sin_t):
    half_dim = values.shape[-1] // 2
    first_half = values[..., :half_dim]
    second_half = values[..., half_dim:]
    return jnp.concatenate([first_half * cos_t - second_half * sin_t, second_half * cos_t + first_half * sin_t], axis=-1)


def rope_revert(grads_in, cos_t, sin_t):
    half_dim = grads_in.shape[-1] // 2
    first_half = grads_in[..., :half_dim]
    second_half = grads_in[..., half_dim:]
    return jnp.concatenate([first_half * cos_t + second_half * sin_t, second_half * cos_t - first_half * sin_t], axis=-1)


def rms_forward(values, gain_vec):
    inv_rms = lax.rsqrt(jnp.mean(values * values, axis=-1, keepdims=True) + NORM_EPS)
    normed = values * inv_rms
    return normed * gain_vec.astype(jnp.float32), normed, inv_rms


def rms_backward(d_out, normed, inv_rms, gain_vec):
    d_normed = d_out * gain_vec.astype(jnp.float32)
    d_in = inv_rms * (d_normed - normed * jnp.mean(d_normed * normed, axis=-1, keepdims=True))
    return d_in, d_out * normed


def project(values, weight):
    return jnp.einsum('bsd,de->bse', values, weight, preferred_element_type=jnp.float32)


def project_back(grads_in, weight):
    return jnp.einsum('bse,de->bsd', grads_in, weight, preferred_element_type=jnp.float32)


def weight_grad(values, grads_in):
    return jnp.einsum('bsd,bse->de', values, grads_in, preferred_element_type=jnp.float32)


def block_front(x_in, positions, g_norm, w_query, w_key, w_value, g_query, g_key):
    n_batch, seq_len, d_model = x_in.shape
    head_shape = (n_batch, seq_len, d_model // HEAD_DIM, HEAD_DIM)
    cos_t, sin_t = rope_tables(positions)
    x_f = x_in.astype(jnp.float32)
    hid_f, x_hat, x_inv = rms_forward(x_f, g_norm)
    hidden = hid_f.astype(jnp.bfloat16)
    q_nrm, q_hat, q_inv = rms_forward(project(hidden, w_query), g_query)
    k_nrm, k_hat, k_inv = rms_forward(project(hidden, w_key), g_key)
    q_rot = rope_apply(q_nrm.reshape(head_shape), cos_t, sin_t).astype(jnp.bfloat16)
    k_rot = rope_apply(k_nrm.reshape(head_shape), cos_t, sin_t).astype(jnp.bfloat16)
    v_val = project(hidden, w_value).astype(jnp.bfloat16).reshape(head_shape)
    saved_fwd = (x_f, x_hat, x_inv, hidden, q_hat, q_inv, k_hat, k_inv, cos_t, sin_t)
    return q_rot, k_rot, v_val, saved_fwd


def block_back(saved_fwd, d_q, d_k, d_v, grad_y, g_norm, w_query, w_key, w_value, g_query, g_key):
    x_f, x_hat, x_inv, hidden, q_hat, q_inv, k_hat, k_inv, cos_t, sin_t = saved_fwd
    flat_shape = hidden.shape
    dq_rot = rope_revert(d_q.astype(jnp.float32), cos_t, sin_t).reshape(flat_shape)
    dk_rot = rope_revert(d_k.astype(jnp.float32), cos_t, sin_t).reshape(flat_shape)
    dq_raw, q_terms = rms_backward(dq_rot, q_hat, q_inv, g_query)
    dk_raw, k_terms = rms_backward(dk_rot, k_hat, k_inv, g_key)
    dq_bf = dq_raw.astype(jnp.bfloat16)
    dk_bf = dk_raw.astype(jnp.bfloat16)
    dv_bf = d_v.reshape(flat_shape)
    d_hidden = project_back(dq_bf, w_query) + project_back(dk_bf, w_key) + project_back(dv_bf, w_value)
    dx_norm, n_terms = rms_backward(d_hidden, x_hat, x_inv, g_norm)
    grad_x = (grad_y.astype(jnp.float32) + dx_norm).astype(jnp.bfloat16)
    return grad_x, (dq_bf, dk_bf, dv_bf), (n_terms, q_terms, k_terms)


def attend_forward(q_all, k_all, v_all, q_offset):
    q_len = q_all.shape[1]
    key_pos = jnp.arange(k_all.shape[1])
    blk_len = min(QUERY_BLOCK, q_len)
    qk_scale = q_all.shape[-1] ** -0.5

    def block_step(blk_idx, loop_state):
        out_buf, lse_buf = loop_state
        q_start = blk_idx * blk_len
        q_blk = lax.dynamic_slice_in_dim(q_all, q_start, blk_len, axis=1)
        scores = jnp.einsum('bqhd,bkhd->bhqk', q_blk, k_all, preferred_element_type=jnp.float32) * qk_scale
        q_pos = q_offset + q_start + jnp.arange(blk_len)
        scores = jnp.where(q_pos[:, None] >= key_pos[None, :], scores, NEG_BIG)
        row_max = jnp.max(scores, axis=-1, keepdims=True)
        exp_scores = jnp.exp(scores - row_max)
        row_sum = jnp.sum(exp_scores, axis=-1, keepdims=True)
        prob_bf = (exp_scores / row_sum).astype(jnp.bfloat16)
        out_blk = jnp.einsum('bhqk,bkhd->bqhd', prob_bf, v_all, preferred_element_type=jnp.float32)
        lse_blk = (row_max + jnp.log(row_sum))[..., 0]
        out_buf = lax.dynamic_update_slice_in_dim(out_buf, out_blk.astype(jnp.bfloat16), q_start, axis=1)
        lse_buf = lax.dynamic_update_slice_in_dim(lse_buf, lse_blk, q_start, axis=2)
        return out_buf, lse_buf

    init_state = (jnp.zeros(q_all.shape, jnp.bfloat16), jnp.zeros((q_all.shape[0], q_all.shape[2], q_len), jnp.float32))
    return lax.fori_loop(0, q_len // blk_len, block_step, init_state)


def attend_backward(q_all, k_all, v_all, lse_all, dout_all, q_offset):
    q_len = q_all.shape[1]
    key_pos = jnp.arange(k_all.shape[1])
    blk_len = min(QUERY_BLOCK, q_len)
    qk_scale = q_all.shape[-1] ** -0.5

    def block_step(blk_idx, loop_state):
        dq_buf, dk_acc, dv_acc = loop_state
        q_start = blk_idx * blk_len
        q_blk = lax.dynamic_slice_in_dim(q_all, q_start, blk_len, axis=1)
        do_blk = lax.dynamic_slice_in_dim(dout_all, q_start, blk_len, axis=1)
        lse_blk = lax.dynamic_slice_in_dim(lse_all, q_start, blk_len, axis=2)
        scores = jnp.einsum('bqhd,bkhd->bhqk', q_blk, k_all, preferred_element_type=jnp.float32) * qk_scale
        q_pos = q_offset + q_start + jnp.arange(blk_len)
        scores = jnp.where(q_pos[:, None] >= key_pos[None, :], scores, NEG_BIG)
        prob_f = jnp.exp(scores - lse_blk[..., None])
        d_prob = jnp.einsum('bqhd,bkhd->bhqk', do_blk, v_all, preferred_element_type=jnp.float32)
        row_dot = jnp.sum(prob_f * d_prob, axis=-1, keepdims=True)
        ds_bf = (prob_f * (d_prob - row_dot) * qk_scale).astype(jnp.bfloat16)
        prob_bf = prob_f.astype(jnp.bfloat16)
        dv_acc = dv_acc + jnp.einsum('bhqk,bqhd->bkhd', prob_bf, do_blk, preferred_element_type=jnp.float32)
        dk_acc = dk_acc + jnp.einsum('bhqk,bqhd->bkhd', ds_bf, q_blk, preferred_element_type=jnp.float32)
        dq_blk = jnp.einsum('bhqk,bkhd->bqhd', ds_bf, k_all, preferred_element_type=jnp.float32)
        dq_buf = lax.dynamic_update_slice_in_dim(dq_buf, dq_blk.astype(jnp.bfloat16), q_start, axis=1)
        return dq_buf, dk_acc, dv_acc

    init_state = (jnp.zeros(q_all.shape, jnp.bfloat16), jnp.zeros(k_all.shape, jnp.float32), jnp.zeros(v_all.shape, jnp.float32))
    return lax.fori_loop(0, q_len // blk_len, block_step, init_state)


def solution(mesh):
    to_heads = functools.partial(lax.all_to_all, axis_name='sp', split_axis=2, concat_axis=1, tiled=True)
    to_tokens = functools.partial(lax.all_to_all, axis_name='sp', split_axis=1, concat_axis=2, tiled=True)

    def sum_rows(partial_sum):
        return lax.psum_scatter(partial_sum, 'sp', scatter_dimension=0, tiled=True)

    def device_step(x_loc, grad_y, positions, g_norm, w_query, w_key, w_value, w_out, g_query, g_key):
        n_batch, loc_len, d_model = x_loc.shape
        q_loc, k_loc, v_loc, saved_fwd = block_front(x_loc, positions, g_norm, w_query, w_key, w_value, g_query, g_key)
        q_all = to_heads(q_loc)
        k_all = to_heads(k_loc)
        v_all = to_heads(v_loc)
        out_all, lse_all = attend_forward(q_all, k_all, v_all, 0)
        attended = to_tokens(out_all).reshape(n_batch, loc_len, d_model)
        y_out = (saved_fwd[0] + project(attended, w_out)).astype(jnp.bfloat16)
        grad_w_out = weight_grad(attended, grad_y)
        d_attn = project_back(grad_y, w_out).astype(jnp.bfloat16).reshape(q_loc.shape)
        dq_all, dk_acc, dv_acc = attend_backward(q_all, k_all, v_all, lse_all, to_heads(d_attn), 0)
        d_q = to_tokens(dq_all)
        d_k = to_tokens(dk_acc.astype(jnp.bfloat16))
        d_v = to_tokens(dv_acc.astype(jnp.bfloat16))
        grad_x, proj_grads, gain_terms = block_back(saved_fwd, d_q, d_k, d_v, grad_y, g_norm, w_query, w_key, w_value, g_query, g_key)
        hidden = saved_fwd[3]
        return (y_out, grad_x, sum_rows(jnp.sum(gain_terms[0], axis=(0, 1))), sum_rows(weight_grad(hidden, proj_grads[0])), sum_rows(weight_grad(hidden, proj_grads[1])), sum_rows(weight_grad(hidden, proj_grads[2])), sum_rows(grad_w_out), sum_rows(jnp.sum(gain_terms[1], axis=(0, 1))), sum_rows(jnp.sum(gain_terms[2], axis=(0, 1))))

    seq_spec = P('dp', 'sp', None)
    mat_rep = P(None, None)
    vec_rep = P(None)
    row_spec = P(('dp', 'sp'), None)
    vec_spec = P(('dp', 'sp'))
    return jax.shard_map(device_step, mesh=mesh, in_specs=(seq_spec, seq_spec, P('dp', 'sp'), vec_rep, mat_rep, mat_rep, mat_rep, mat_rep, vec_rep, vec_rep), out_specs=(seq_spec, seq_spec, vec_spec, row_spec, row_spec, row_spec, row_spec, vec_spec, vec_spec), check_vma=False)
```

profile of v0, /device:TPU:0, one launch (start us, length us, event | category | flops | bytes accessed | tf_op | source)
XLA Modules:
  0.0 4964.8 jit_solution(15280457813292223524)
XLA Ops:
  155.7 88.4 %fusion.103 = (f32[16,256,16,64]{3,2,1,0:T(8,128)}, f32[16,256,16,64]{3,2,1,0:T(8,128)}, f32[16,256,16,64]{3,2,1,0:T(8,128)}, f32[16,256,16,64]{3,2,1,0:T(8,128)}) fusion(f32[16,256,16,128]{3,2,1,0:T(8,128)} %bitcast.161, f32[16,256,16,128]{3,2,1,0:T(8,128)} %bitcast.158), kind=kLoop, calls=%fused_computation.137 | loop fusion | bytes 134217728 | tf_op jit(solution)/shard_map/slice | solution.py:23
  252.8 92.2 %subtract_convert_fusion = (bf16[16,256,16,64]{3,1,0,2:T(8,128)(2,1)}, bf16[16,256,16,64]{3,1,0,2:T(8,128)(2,1)}, bf16[16,256,16,64]{3,1,0,2:T(8,128)(2,1)}, bf16[16,256,16,64]{3,1,0,2:T(8,128)(2,1)}) fusion(f32[16,256,16,64]{3,2,1,0:T(8,128)} %get-tuple-element.406, f32[16,256,16,64]{3,2,1,0:T(8,128)} %get-tuple-element.405, ...), kind=kLoop, calls=%fused_computation.97 | loop fusion | flops 67108864 | bytes 102760448 | tf_op jit(solution)/shard_map/convert.6
  393.6 163.0 %all-to-all-done.1 = bf16[16,256,16,128]{3,1,0,2:T(8,128)(2,1)} async-done(((bf16[16,256,16,128]{3,1,0,2:T(8,128)(2,1)}), bf16[16,256,16,128]{3,1,0,2:T(8,128)(2,1)}, u32[]{:S(2)}, u32[]{:S(2)}) %all-to-all-start.1) | async-done | bytes 16777248 | tf_op jit(solution)/shard_map/all_to_all | solution.py:159
  612.6 133.7 %all-to-all-done = bf16[16,256,16,128]{3,1,0,2:T(8,128)(2,1)} async-done(((bf16[16,256,16,128]{3,1,0,2:T(8,128)(2,1)}), bf16[16,256,16,128]{3,1,0,2:T(8,128)(2,1)}, u32[]{:S(2)}, u32[]{:S(2)}) %all-to-all-start) | async-done | bytes 16777248 | tf_op jit(solution)/shard_map/all_to_all | solution.py:158
  830.3 105.8 %all-to-all-done.2 = bf16[16,256,16,128]{3,1,0,2:T(8,128)(2,1)} async-done(((bf16[16,256,16,128]{3,1,0,2:T(8,128)(2,1)}), bf16[16,256,16,128]{3,1,0,2:T(8,128)(2,1)}, u32[]{:S(2)}, u32[]{:S(2)}) %all-to-all-start.2) | async-done | bytes 16777248 | tf_op jit(solution)/shard_map/all_to_all | solution.py:160
  966.8 455.2 %while.34 = (s32[]{:T(128)}, bf16[16,1024,4,128]{3,2,0,1:T(4,128)(2,1)}, f32[16,4,1024]{2,1,0:T(4,128)S(1)}, bf16[16,1024,4,128]{3,1,2,0:T(8,128)(2,1)}, bf16[16...) while((s32[]{:T(128)}, ...), condition=%wide.region_6.7_spmd.clone, body=%wide.region_3.6_spmd.clone.sunk | while | flops 4396802048 | bytes 143393952 | solution.py:115
  1445.2 1784.5 %while.35 = (s32[]{:T(128)}, bf16[16,1024,4,128]{3,2,0,1:T(4,128)(2,1)}, f32[16,1024,4,128]{1,3,2,0:T(8,128)}, f32[16,1024,4,128]{1,3,2,0:T(8,128)}, bf16[16,102...) while((s32[]{:T(128)}, ...), condition=%wide.region_9.10_spmd.clone, body=%wide.region_7.9_spmd.clone.sunk | while | flops 10990274560 | bytes 504169696 | solution.py:145
  1482.3 67.2 %bitcast_add_fusion.4 = f32[16,1024,4,128]{1,3,2,0:T(8,128)} fusion(f32[16,1024,4,128]{1,3,2,0:T(8,128)} %get-tuple-element.563, pred[]{:T(512)S(6)} %compare.3, f32[16,4,128,1024]{3,2,1,0:T(8,128)} %fusion.156, f32[16,4,128,1024]{3,2,1,0:T(8,128)} %fusion.157, f32[16,4,128]{2,1,0:T(4,128)S(1)} %constant_dynamic-slice_fusion.2, ...), kind=kOutput, calls=%fused_computation.20.clone.3 | convolution fusion | flops 2256544768 | bytes 203751424 | tf_op jit(solution)/shard_map/while/body/eval_jaxpr/bhqk,bqhd->bkhd/dot_general | solution.py:139
  1549.5 72.2 %convert_bitcast_fusion.7 = bf16[16,128,4,128]{3,1,2,0:T(8,128)(2,1)S(1)} fusion(bf16[16,1024,4,128]{3,1,2,0:T(8,128)(2,1)} %get-tuple-element.579, f32[16,4,128,1024]{3,2,1,0:T(8,128)} %fusion.156, f32[16,4,128,1024]{3,2,1,0:T(8,128)} %fusion.157, f32[16,4,128]{2,1,0:T(4,128)S(1)} %constant_dynamic-slice_fusion.2, ...), kind=kOutput, calls=%fused_computation.41.clone.1 | convolution fusion | flops 2240816128 | bytes 86147072 | tf_op jit(solution)/shard_map/while/body/eval_jaxpr/bhqk,bkhd->bqhd/dot_general | solution.py:140
  1687.4 77.4 %bitcast_add_fusion.4 = f32[16,1024,4,128]{1,3,2,0:T(8,128)} fusion(f32[16,1024,4,128]{1,3,2,0:T(8,128)} %get-tuple-element.563, pred[]{:T(512)S(6)} %compare.3, f32[16,4,128,1024]{3,2,1,0:T(8,128)} %fusion.156, f32[16,4,128,1024]{3,2,1,0:T(8,128)} %fusion.157, f32[16,4,128]{2,1,0:T(4,128)S(1)} %constant_dynamic-slice_fusion.2, ...), kind=kOutput, calls=%fused_computation.20.clone.3 | convolution fusion | flops 2256544768 | bytes 203751424 | tf_op jit(solution)/shard_map/while/body/eval_jaxpr/bhqk,bqhd->bkhd/dot_general | solution.py:139
  1764.8 72.2 %convert_bitcast_fusion.7 = bf16[16,128,4,128]{3,1,2,0:T(8,128)(2,1)S(1)} fusion(bf16[16,1024,4,128]{3,1,2,0:T(8,128)(2,1)} %get-tuple-element.579, f32[16,4,128,1024]{3,2,1,0:T(8,128)} %fusion.156, f32[16,4,128,1024]{3,2,1,0:T(8,128)} %fusion.157, f32[16,4,128]{2,1,0:T(4,128)S(1)} %constant_dynamic-slice_fusion.2, ...), kind=kOutput, calls=%fused_computation.41.clone.1 | convolution fusion | flops 2240816128 | bytes 86147072 | tf_op jit(solution)/shard_map/while/body/eval_jaxpr/bhqk,bkhd->bqhd/dot_general | solution.py:140
  1912.0 77.5 %bitcast_add_fusion.4 = f32[16,1024,4,128]{1,3,2,0:T(8,128)} fusion(f32[16,1024,4,128]{1,3,2,0:T(8,128)} %get-tuple-element.563, pred[]{:T(512)S(6)} %compare.3, f32[16,4,128,1024]{3,2,1,0:T(8,128)} %fusion.156, f32[16,4,128,1024]{3,2,1,0:T(8,128)} %fusion.157, f32[16,4,128]{2,1,0:T(4,128)S(1)} %constant_dynamic-slice_fusion.2, ...), kind=kOutput, calls=%fused_computation.20.clone.3 | convolution fusion | flops 2256544768 | bytes 203751424 | tf_op jit(solution)/shard_map/while/body/eval_jaxpr/bhqk,bqhd->bkhd/dot_general | solution.py:139
  1989.5 72.2 %convert_bitcast_fusion.7 = bf16[16,128,4,128]{3,1,2,0:T(8,128)(2,1)S(1)} fusion(bf16[16,1024,4,128]{3,1,2,0:T(8,128)(2,1)} %get-tuple-element.579, f32[16,4,128,1024]{3,2,1,0:T(8,128)} %fusion.156, f32[16,4,128,1024]{3,2,1,0:T(8,128)} %fusion.157, f32[16,4,128]{2,1,0:T(4,128)S(1)} %constant_dynamic-slice_fusion.2, ...), kind=kOutput, calls=%fused_computation.41.clone.1 | convolution fusion | flops 2240816128 | bytes 86147072 | tf_op jit(solution)/shard_map/while/body/eval_jaxpr/bhqk,bkhd->bqhd/dot_general | solution.py:140
  2136.8 77.4 %bitcast_add_fusion.4 = f32[16,1024,4,128]{1,3,2,0:T(8,128)} fusion(f32[16,1024,4,128]{1,3,2,0:T(8,128)} %get-tuple-element.563, pred[]{:T(512)S(6)} %compare.3, f32[16,4,128,1024]{3,2,1,0:T(8,128)} %fusion.156, f32[16,4,128,1024]{3,2,1,0:T(8,128)} %fusion.157, f32[16,4,128]{2,1,0:T(4,128)S(1)} %constant_dynamic-slice_fusion.2, ...), kind=kOutput, calls=%fused_computation.20.clone.3 | convolution fusion | flops 2256544768 | bytes 203751424 | tf_op jit(solution)/shard_map/while/body/eval_jaxpr/bhqk,bqhd->bkhd/dot_general | solution.py:139
  2214.2 78.1 %convert_bitcast_fusion.7 = bf16[16,128,4,128]{3,1,2,0:T(8,128)(2,1)S(1)} fusion(bf16[16,1024,4,128]{3,1,2,0:T(8,128)(2,1)} %get-tuple-element.579, f32[16,4,128,1024]{3,2,1,0:T(8,128)} %fusion.156, f32[16,4,128,1024]{3,2,1,0:T(8,128)} %fusion.157, f32[16,4,128]{2,1,0:T(4,128)S(1)} %constant_dynamic-slice_fusion.2, ...), kind=kOutput, calls=%fused_computation.41.clone.1 | convolution fusion | flops 2240816128 | bytes 86147072 | tf_op jit(solution)/shard_map/while/body/eval_jaxpr/bhqk,bkhd->bqhd/dot_general | solution.py:140
  2367.4 77.3 %bitcast_add_fusion.4 = f32[16,1024,4,128]{1,3,2,0:T(8,128)} fusion(f32[16,1024,4,128]{1,3,2,0:T(8,128)} %get-tuple-element.563, pred[]{:T(512)S(6)} %compare.3, f32[16,4,128,1024]{3,2,1,0:T(8,128)} %fusion.156, f32[16,4,128,1024]{3,2,1,0:T(8,128)} %fusion.157, f32[16,4,128]{2,1,0:T(4,128)S(1)} %constant_dynamic-slice_fusion.2, ...), kind=kOutput, calls=%fused_computation.20.clone.3 | convolution fusion | flops 2256544768 | bytes 203751424 | tf_op jit(solution)/shard_map/while/body/eval_jaxpr/bhqk,bqhd->bkhd/dot_general | solution.py:139
  2444.8 72.2 %convert_bitcast_fusion.7 = bf16[16,128,4,128]{3,1,2,0:T(8,128)(2,1)S(1)} fusion(bf16[16,1024,4,128]{3,1,2,0:T(8,128)(2,1)} %get-tuple-element.579, f32[16,4,128,1024]{3,2,1,0:T(8,128)} %fusion.156, f32[16,4,128,1024]{3,2,1,0:T(8,128)} %fusion.157, f32[16,4,128]{2,1,0:T(4,128)S(1)} %constant_dynamic-slice_fusion.2, ...), kind=kOutput, calls=%fused_computation.41.clone.1 | convolution fusion | flops 2240816128 | bytes 86147072 | tf_op jit(solution)/shard_map/while/body/eval_jaxpr/bhqk,bkhd->bqhd/dot_general | solution.py:140
  2592.1 77.5 %bitcast_add_fusion.4 = f32[16,1024,4,128]{1,3,2,0:T(8,128)} fusion(f32[16,1024,4,128]{1,3,2,0:T(8,128)} %get-tuple-element.563, pred[]{:T(512)S(6)} %compare.3, f32[16,4,128,1024]{3,2,1,0:T(8,128)} %fusion.156, f32[16,4,128,1024]{3,2,1,0:T(8,128)} %fusion.157, f32[16,4,128]{2,1,0:T(4,128)S(1)} %constant_dynamic-slice_fusion.2, ...), kind=kOutput, calls=%fused_computation.20.clone.3 | convolution fusion | flops 2256544768 | bytes 203751424 | tf_op jit(solution)/shard_map/while/body/eval_jaxpr/bhqk,bqhd->bkhd/dot_general | solution.py:139
  2669.6 72.2 %convert_bitcast_fusion.7 = bf16[16,128,4,128]{3,1,2,0:T(8,128)(2,1)S(1)} fusion(bf16[16,1024,4,128]{3,1,2,0:T(8,128)(2,1)} %get-tuple-element.579, f32[16,4,128,1024]{3,2,1,0:T(8,128)} %fusion.156, f32[16,4,128,1024]{3,2,1,0:T(8,128)} %fusion.157, f32[16,4,128]{2,1,0:T(4,128)S(1)} %constant_dynamic-slice_fusion.2, ...), kind=kOutput, calls=%fused_computation.41.clone.1 | convolution fusion | flops 2240816128 | bytes 86147072 | tf_op jit(solution)/shard_map/while/body/eval_jaxpr/bhqk,bkhd->bqhd/dot_general | solution.py:140
  2816.8 77.5 %bitcast_add_fusion.4 = f32[16,1024,4,128]{1,3,2,0:T(8,128)} fusion(f32[16,1024,4,128]{1,3,2,0:T(8,128)} %get-tuple-element.563, pred[]{:T(512)S(6)} %compare.3, f32[16,4,128,1024]{3,2,1,0:T(8,128)} %fusion.156, f32[16,4,128,1024]{3,2,1,0:T(8,128)} %fusion.157, f32[16,4,128]{2,1,0:T(4,128)S(1)} %constant_dynamic-slice_fusion.2, ...), kind=kOutput, calls=%fused_computation.20.clone.3 | convolution fusion | flops 2256544768 | bytes 203751424 | tf_op jit(solution)/shard_map/while/body/eval_jaxpr/bhqk,bqhd->bkhd/dot_general | solution.py:139
  2894.3 72.2 %convert_bitcast_fusion.7 = bf16[16,128,4,128]{3,1,2,0:T(8,128)(2,1)S(1)} fusion(bf16[16,1024,4,128]{3,1,2,0:T(8,128)(2,1)} %get-tuple-element.579, f32[16,4,128,1024]{3,2,1,0:T(8,128)} %fusion.156, f32[16,4,128,1024]{3,2,1,0:T(8,128)} %fusion.157, f32[16,4,128]{2,1,0:T(4,128)S(1)} %constant_dynamic-slice_fusion.2, ...), kind=kOutput, calls=%fused_computation.41.clone.1 | convolution fusion | flops 2240816128 | bytes 86147072 | tf_op jit(solution)/shard_map/while/body/eval_jaxpr/bhqk,bkhd->bqhd/dot_general | solution.py:140
  3041.6 77.4 %bitcast_add_fusion.4 = f32[16,1024,4,128]{1,3,2,0:T(8,128)} fusion(f32[16,1024,4,128]{1,3,2,0:T(8,128)} %get-tuple-element.563, pred[]{:T(512)S(6)} %compare.3, f32[16,4,128,1024]{3,2,1,0:T(8,128)} %fusion.156, f32[16,4,128,1024]{3,2,1,0:T(8,128)} %fusion.157, f32[16,4,128]{2,1,0:T(4,128)S(1)} %constant_dynamic-slice_fusion.2, ...), kind=kOutput, calls=%fused_computation.20.clone.3 | convolution fusion | flops 2256544768 | bytes 203751424 | tf_op jit(solution)/shard_map/while/body/eval_jaxpr/bhqk,bqhd->bkhd/dot_general | solution.py:139
  3119.0 72.2 %convert_bitcast_fusion.7 = bf16[16,128,4,128]{3,1,2,0:T(8,128)(2,1)S(1)} fusion(bf16[16,1024,4,128]{3,1,2,0:T(8,128)(2,1)} %get-tuple-element.579, f32[16,4,128,1024]{3,2,1,0:T(8,128)} %fusion.156, f32[16,4,128,1024]{3,2,1,0:T(8,128)} %fusion.157, f32[16,4,128]{2,1,0:T(4,128)S(1)} %constant_dynamic-slice_fusion.2, ...), kind=kOutput, calls=%fused_computation.41.clone.1 | convolution fusion | flops 2240816128 | bytes 86147072 | tf_op jit(solution)/shard_map/while/body/eval_jaxpr/bhqk,bkhd->bqhd/dot_general | solution.py:140
  3262.0 193.8 %all_to_all.120 = bf16[16,1024,4,128]{3,2,0,1:T(4,128)(2,1)} all-to-all(bf16[16,1024,4,128]{3,2,0,1:T(4,128)(2,1)} %copy.50), channel_id=1, replica_groups=mesh['dp'=2,'sp'=4] {'sp'}, dimensions={1} | all-to-all | bytes 33554432 | tf_op jit(solution)/shard_map/all_to_all | solution.py:168
  3482.9 162.7 %all-to-all-done.5 = bf16[16,1024,4,128]{3,2,0,1:T(4,128)(2,1)} async-done(((bf16[16,1024,4,128]{3,2,0,1:T(4,128)(2,1)}), bf16[16,1024,4,128]{3,2,0,1:T(4,128)(2,1)}, u32[]{:S(2)}, u32[]{:S(2)}) %all-to-all-start.5) | async-done | bytes 16777248 | tf_op jit(solution)/shard_map/all_to_all | solution.py:167
  3665.5 87.9 %multiply_add_fusion = (f32[16,256,16,64]{3,1,0,2:T(8,128)}, f32[16,256,16,64]{3,1,0,2:T(8,128)}, f32[16,256,16,64]{3,1,0,2:T(8,128)}, f32[16,256,16,64]{3,1,0,2:T(8,128)}) fusion(f32[16,256,16,128]{3,1,0,2:T(8,128)} %bitcast.159, f32[16,256,64]{2,1,0:T(8,128)} %get-tuple-element.414, f32[16,256,64]{2,1,0:T(8,128)S(1)} %copy-done.1, ...), kind=kLoop, calls=%fused_computation.91 | loop fusion | flops 50331648 | bytes 136314880 | tf_op jit(solution)/shard_map/add | solution.py:32
  3824.4 45.2 convolution_bitcast_fusion.2
  3940.8 45.2 convolution_bitcast_fusion.3
  4018.4 271.2 %all_to_all.121 = bf16[16,1024,4,128]{3,2,0,1:T(4,128)(2,1)S(1)} all-to-all(bf16[16,1024,4,128]{3,2,0,1:T(4,128)(2,1)} %copy.53), channel_id=1, replica_groups=mesh['dp'=2,'sp'=4] {'sp'}, dimensions={1} | all-to-all | bytes 33554432 | tf_op jit(solution)/shard_map/all_to_all | solution.py:169
  4327.8 45.1 convolution_bitcast_fusion.1
  4372.9 277.5 %all_to_all.122 = bf16[16,1024,4,128]{3,2,0,1:T(4,128)(2,1)S(1)} all-to-all(bf16[16,1024,4,128]{3,2,0,1:T(4,128)(2,1)} %get-tuple-element.305), channel_id=1, replica_groups=mesh['dp'=2,'sp'=4] {'sp'}, dimensions={1} | all-to-all | bytes 33554432 | tf_op jit(solution)/shard_map/all_to_all | solution.py:162
  4820.7 53.6 %fusion.80 = (f32[2048]{0:T(1024)S(1)}, f32[16,256]{1,0:T(8,128)S(1)}, f32[16,256,2048]{2,1,0:T(8,128)}) fusion(bf16[16,256,2048]{2,1,0:T(8,128)(2,1)} %param.14, f32[16,256]{1,0:T(8,128)S(1)} %copy-done.15, f32[2048]{0:T(1024)S(1)} %copy-done.21, bf16[16,256,2048]{2,1,0:T(8,128)(2,1)} %reshape.126, bf16[2048,2048]{1,0:T(8,128)(2,1)} %param.20, ...), kind=kOutput, calls=%fused_computation.76 | convolution fusion | flops 34435231744 | bytes 142655488 | tf_op jit(solution)/shard_map/bse,de->bsd/dot_general | solution.py:52
  (268 shorter events, 1990.7 us)
Async XLA Ops:
  14.9 70.7 %copy-start.12 = (f32[16,256]{1,0:T(8,128)}, f32[16,256]{1,0:T(8,128)S(1)}, u32[]{:S(2)}) copy-start(f32[16,256]{1,0:T(8,128)S(1)} %add_rsqrt_fusion.2) | copy-start | bytes 49156
  15.6 70.0 %copy-start.18 = (f32[2048]{0:T(1024)}, f32[2048]{0:T(1024)S(1)}, u32[]{:S(2)}) copy-start(f32[2048]{0:T(1024)S(1)} %convert_element_type.116) | copy-start | bytes 24580
  15.6 43.8 copy-start.23
  85.5 44.0 copy-start.24
  155.7 88.4 %copy-start.25 = (f32[64]{0:T(128)S(1)}, f32[64]{0:T(128)}, u32[]{:S(2)}) copy-start(f32[64]{0:T(128)} %multiply_power_fusion) | copy-start | bytes 772
  252.8 92.2 %copy-start = (f32[16,256,64]{2,1,0:T(8,128)}, f32[16,256,64]{2,1,0:T(8,128)S(1)}, u32[]{:S(2)}) copy-start(f32[16,256,64]{2,1,0:T(8,128)S(1)} %get-tuple-element.413) | copy-start | bytes 3145732
  365.8 190.7 %all-to-all-start.1 = ((bf16[16,256,16,128]{3,1,0,2:T(8,128)(2,1)}), bf16[16,256,16,128]{3,1,0,2:T(8,128)(2,1)}, u32[]{:S(2)}, u32[]{:S(2)}) async-start(bf16[16,256,16,128]{3,1,0,2:T(8,128)(2,1)} %pad_maximum_fusion.1), calls=%async_computation.1 | async-start | bytes 33554432 | tf_op jit(solution)/shard_map/all_to_all | solution.py:159
  372.8 190.8 %copy-start.13 = (f32[16,256]{1,0:T(8,128)S(1)}, f32[16,256]{1,0:T(8,128)}, u32[]{:S(2)}) copy-start(f32[16,256]{1,0:T(8,128)} %copy-done.12) | copy-start | bytes 49156
  372.9 190.8 %copy-start.19 = (f32[2048]{0:T(1024)S(1)}, f32[2048]{0:T(1024)}, u32[]{:S(2)}) copy-start(f32[2048]{0:T(1024)} %copy-done.18) | copy-start | bytes 24580
  556.6 189.8 %all-to-all-start = ((bf16[16,256,16,128]{3,1,0,2:T(8,128)(2,1)}), bf16[16,256,16,128]{3,1,0,2:T(8,128)(2,1)}, u32[]{:S(2)}, u32[]{:S(2)}) async-start(bf16[16,256,16,128]{3,1,0,2:T(8,128)(2,1)} %pad_maximum_fusion), calls=%async_computation | async-start | bytes 33554432 | tf_op jit(solution)/shard_map/all_to_all | solution.py:158
  746.4 189.7 %all-to-all-start.2 = ((bf16[16,256,16,128]{3,1,0,2:T(8,128)(2,1)}), bf16[16,256,16,128]{3,1,0,2:T(8,128)(2,1)}, u32[]{:S(2)}, u32[]{:S(2)}) async-start(bf16[16,256,16,128]{3,1,0,2:T(8,128)(2,1)} %bitcast.168), calls=%async_computation.2 | async-start | bytes 33554432 | tf_op jit(solution)/shard_map/all_to_all | solution.py:160
  936.0 485.9 %all-to-all-start.4 = ((bf16[16,256,16,128]{3,1,0,2:T(8,128)(2,1)}), bf16[16,256,16,128]{3,1,0,2:T(8,128)(2,1)}, u32[]{:S(2)}, u32[]{:S(2)}) async-start(bf16[16,256,16,128]{3,1,0,2:T(8,128)(2,1)} %bitcast.167), calls=%async_computation.4 | async-start | bytes 33554432 | tf_op jit(solution)/shard_map/all_to_all | solution.py:166
  1445.3 36.8 copy-start.2
  1650.4 36.8 copy-start.2
  1875.1 36.8 copy-start.2
  3455.8 189.7 %all-to-all-start.5 = ((bf16[16,1024,4,128]{3,2,0,1:T(4,128)(2,1)}), bf16[16,1024,4,128]{3,2,0,1:T(4,128)(2,1)}, u32[]{:S(2)}, u32[]{:S(2)}) async-start(bf16[16,1024,4,128]{3,2,0,1:T(4,128)(2,1)} %get-tuple-element.307), calls=%async_computation.5 | async-start | bytes 33554432 | tf_op jit(solution)/shard_map/all_to_all | solution.py:167
  3462.8 1494.9 %reduce-scatter.7.cloned.1.call-start = ((), (), s32[]{:S(2)}) async-start(), calls=%async_computation.13 | async-start | bytes 20971520 | tf_op jit(solution)/shard_map/reduce_scatter | solution.py:153
  3482.9 182.6 %copy-start.1 = (f32[16,256,64]{2,1,0:T(8,128)S(1)}, f32[16,256,64]{2,1,0:T(8,128)}, u32[]{:S(2)}) copy-start(f32[16,256,64]{2,1,0:T(8,128)} %copy-done) | copy-start | bytes 3145732
  3665.5 87.9 %copy-start.7 = (f32[16,256]{1,0:T(8,128)S(1)}, f32[16,256]{1,0:T(8,128)}, u32[]{:S(2)}) copy-start(f32[16,256]{1,0:T(8,128)} %copy-done.6) | copy-start | bytes 49156
  3665.5 87.9 %copy-start.11 = (f32[2048]{0:T(1024)S(1)}, f32[2048]{0:T(1024)}, u32[]{:S(2)}) copy-start(f32[2048]{0:T(1024)} %copy-done.10) | copy-start | bytes 24580
  3786.0 38.4 copy-start.14
  3786.0 38.4 copy-start.20
  3824.4 45.3 copy-start.5
  3824.4 45.3 copy-start.9
  3869.7 1088.1 %reduce-scatter.5.cloned.1.call-start = ((), (), s32[]{:S(2)}) async-start(), calls=%async_computation.12 | async-start | bytes 20971520 | tf_op jit(solution)/shard_map/reduce_scatter | solution.py:153
  3986.0 971.7 %reduce-scatter.9.cloned.1.call-start = ((), (), s32[]{:S(2)}) async-start(), calls=%async_computation.14 | async-start | bytes 20971520 | tf_op jit(solution)/shard_map/reduce_scatter | solution.py:153
  4372.9 584.9 %reduce-scatter.11.cloned.1.call-start = ((), (), s32[]{:S(2)}) async-start(), calls=%async_computation.15 | async-start | bytes 20971520 | tf_op jit(solution)/shard_map/reduce_scatter | solution.py:153
  4688.6 43.7 copy-start.26
  4777.1 43.6 copy-start.15
  4777.1 43.6 copy-start.21
  4820.7 53.6 %copy-start.16 = (f32[2048]{0:T(1024)S(1)}, f32[2048]{0:T(1024)}, u32[]{:S(2)}) copy-start(f32[2048]{0:T(1024)} %get-tuple-element.356) | copy-start | bytes 24580
  4820.7 53.6 %copy-start.17 = (f32[2048]{0:T(1024)S(1)}, f32[2048]{0:T(1024)}, u32[]{:S(2)}) copy-start(f32[2048]{0:T(1024)} %get-tuple-element.358) | copy-start | bytes 24580
  (18 other events, 519.7 us)
Sparse Core Ops, SparseCore 0:
  3869.8 119.6 reduce-scatter.6
  3992.6 202.3 reduce-scatter.4
  4373.0 212.2 reduce-scatter.8
  4732.4 118.7 reduce-scatter.10
where the time goes:
time: 4980 us; the launch traced here: 4960 us
  matrix products  2600 us (52%)
  blocking collectives  753 us (15%)
  waiting for transfers between devices  565 us (11%)
  other arithmetic  557 us (11%)
  local copies, waits for them, and re-layouts  438 us (9%)
    dot_general x8, matrix products, block_step(): jnp.einsum('bhqk,bqhd->bkhd', ds_bf, q_blk, preferred_element_type=jnp.fl...  609 us
    dot_general x8, matrix products, block_step(): jnp.einsum('bhqk,bkhd->bqhd', ds_bf, k_all, preferred_element_type=jnp.fl...  583 us
    dot_general x16, matrix products, block_step(): jnp.einsum('bqhd,bkhd->bhqk', q_blk, k_all, preferred_element_type=jnp.fl...  298 us
    all_to_all x1, blocking collectives, device_step(): attended = to_tokens(out_all).reshape(n_batch, loc_len, d_model)  278 us
    dot_general x8, matrix products, block_step(): jnp.einsum('bhqk,bqhd->bkhd', prob_bf, do_blk, preferred_element_type=jnp...  272 us
    all_to_all x1, blocking collectives, device_step(): d_v = to_tokens(dv_acc.astype(jnp.bfloat16))  271 us
    all_to_all x1, blocking collectives, device_step(): d_k = to_tokens(dk_acc.astype(jnp.bfloat16))  194 us
    dot_general x4, matrix products, project_back(): jnp.einsum('bse,de->bsd', grads_in, weight, preferred_element_type=jnp.fl...  181 us
  transfers between devices with their start and end apart: 9, of which 4 were waited for; matrix products, arithmetic and copies ran while one was open for 24% of the time, Pallas kernels for 0%

commit v1 on v0

v1 whole, which is shorter than its diff:
```python
import math
import jax
import jax.numpy as jnp
from jax import lax
from jax.experimental import pallas as pl
from jax.experimental.pallas import tpu as pltpu
from jax.sharding import PartitionSpec as P


HEAD = 128
EPS = 1e-5
ROPE_BASE = 10000.0
NEG_BIG = -1e30
SCALE = HEAD ** -0.5
SCALE2 = SCALE * math.log2(math.e)
N_CHUNK = 2
VMEM = 66_000_000
F32 = jnp.float32
BF16 = jnp.bfloat16


def dot_nn(a, b):
    return lax.dot_general(a, b, (((1,), (0,)), ((), ())), preferred_element_type=F32)


def dot_nt(a, b):
    return lax.dot_general(a, b, (((1,), (1,)), ((), ())), preferred_element_type=F32)


def dot_tn(a, b):
    return lax.dot_general(a, b, (((0,), (0,)), ((), ())), preferred_element_type=F32)


def head_cols(idx):
    return slice(idx * HEAD, (idx + 1) * HEAD)


def row_sum(part):
    return jnp.sum(part, axis=-1, keepdims=True)


ANY = pl.BlockSpec(memory_space=pl.ANY)


def place(bits):
    return jnp.where((bits == 0) | (bits == 3), 3 - bits, bits)


def front_kernel(me_ref, xa_ref, xb_ref, cos_ref, sin_ref, gn_ref, gq_ref, gk_ref, wq_ref, wk_ref, wv_ref, *refs):
    x_ref, h_ref, q_ref, k_ref, v_ref, q1_ref, k1_ref = refs[-7:]
    d_model = x_ref.shape[-1]
    n_heads = d_model // HEAD

    @pl.when(pl.program_id(0) == 0)
    def _():
        x_ref[...] = xa_ref[...]

    @pl.when(pl.program_id(0) == 1)
    def _():
        x_ref[...] = xb_ref[...]

    x_f = x_ref[...].astype(F32)
    inv_x = lax.rsqrt(jnp.mean(x_f * x_f, axis=-1, keepdims=True) + EPS)
    hidden = (x_f * inv_x * gn_ref[...]).astype(BF16)
    blk = d_model // 4
    for b in range(4):
        h_ref[:, pl.ds(pl.multiple_of(place(me_ref[0] ^ b) * blk, blk), blk)] = hidden[:, b * blk:(b + 1) * blk]
    cos_t = cos_ref[...]
    sin_t = sin_ref[...]
    n_col = 512
    for w_ref, g_ref, raw_ref, out_ref in ((wq_ref, gq_ref, q1_ref, q_ref), (wk_ref, gk_ref, k1_ref, k_ref)):
        sq = jnp.zeros((x_ref.shape[0], HEAD), F32)
        for c0 in range(0, d_model, n_col):
            raw = dot_nn(hidden, w_ref[:, c0:c0 + n_col])
            raw_ref[:, c0:c0 + n_col] = raw
            for j in range(n_col // HEAD):
                piece = raw[:, head_cols(j)]
                sq = sq + piece * piece
        inv = lax.rsqrt(row_sum(sq) * (1.0 / d_model) + EPS)
        for j in range(n_heads):
            u = raw_ref[:, head_cols(j)] * inv * g_ref[:, head_cols(j)]
            rot = u * cos_t + pltpu.roll(u, HEAD // 2, 1) * sin_t
            out_ref[:, head_cols(j)] = rot.astype(BF16)
    for c0 in range(0, d_model, n_col):
        v_ref[:, c0:c0 + n_col] = dot_nn(hidden, wv_ref[:, c0:c0 + n_col]).astype(BF16)


def front(me, x_a, x_b, own, bits, seq0, n_seq, cos_t, sin_t, g_norm, g_query, g_key, w_query, w_key, w_value, filled):
    n_piece, n_all, rows, d_model = cos_t.shape[:3] + x_a.shape[-1:]
    first = lambda i, s: jnp.where(i == 0, s, n_seq - 1)
    second = lambda i, s: jnp.where(i == 0, 0, s)
    x_block = (None, rows, d_model)
    a_map = (lambda i, s, m: (m[0] * n_all + first(i, s), 0, 0)) if own else (lambda i, s, m: (first(i, s), 0, 0))
    spot = lambda i, s, m: (m[0] ^ jnp.where(i == 0, bits[0], bits[1]), seq0 + s, 0, 0)
    table = pl.BlockSpec((None, None, rows, HEAD), spot)
    out = pl.BlockSpec((None, None, rows, d_model), spot)
    vec = pl.BlockSpec((1, d_model), lambda i, s, m: (0, 0))
    mat = pl.BlockSpec((d_model, d_model), lambda i, s, m: (0, 0), pipeline_mode=pl.Buffered(1))
    big = lambda dt: jax.ShapeDtypeStruct((n_piece, n_all, rows, d_model), dt)
    row = lambda g: g.astype(F32).reshape(1, d_model)
    n_tok = 2 * n_seq * rows
    return pl.pallas_call(
        front_kernel,
        grid_spec=pltpu.PrefetchScalarGridSpec(
            num_scalar_prefetch=1,
            grid=(2, n_seq),
            in_specs=[pl.BlockSpec(x_block, a_map), pl.BlockSpec(x_block, lambda i, s, m: (second(i, s), 0, 0)), table, table, vec, vec, vec, mat, mat, mat] + [ANY] * len(filled),
            out_specs=[out] * 7,
        ),
        out_shape=[big(BF16)] * 5 + [big(F32)] * 2,
        input_output_aliases={11 + n: n for n in range(len(filled))},
        compiler_params=pltpu.CompilerParams(vmem_limit_bytes=VMEM, dimension_semantics=("arbitrary", "arbitrary")),
        cost_estimate=pl.CostEstimate(flops=6 * n_tok * d_model * d_model, bytes_accessed=n_tok * d_model * 20 + 6 * d_model * d_model, transcendentals=0),
        name="front",
    )(me, x_a, x_b, cos_t, sin_t, row(g_norm), row(g_query), row(g_key), w_query, w_key, w_value, *filled)


def attend_kernel(me_ref, q_ref, k_ref, v_ref, *refs):
    o_ref, rel_ref, lse_ref = refs[-3:]
    n_piece, _, rows, width = q_ref.shape
    keep = lax.broadcasted_iota(jnp.int32, (rows, rows), 0) >= lax.broadcasted_iota(jnp.int32, (rows, rows), 1)
    for hd in range(width // HEAD):
        cols = head_cols(hd)
        for i in range(n_piece):
            q_i = q_ref[i, 0, :, cols]
            scores = [dot_nt(q_i, k_ref[j, 0, :, cols]) for j in range(i + 1)]
            scores[i] = jnp.where(keep, scores[i], NEG_BIG)
            top = scores[0]
            for j in range(1, i + 1):
                top = jnp.maximum(top, scores[j])
            top = jnp.max(top, axis=-1, keepdims=True) * SCALE2
            total = None
            out = None
            for j in range(i + 1):
                prob = jnp.exp2(scores[j] * SCALE2 - top)
                total = prob if total is None else total + prob
                term = dot_nn(prob.astype(BF16), v_ref[j, 0, :, cols])
                out = term if out is None else out + term
            total = row_sum(total)
            out = (out * (1.0 / total)).astype(BF16)
            o_ref[i, 0, :, cols] = out
            rel_ref[i, 0, :, cols] = out
            lse = top + jnp.log2(total)
            lse_ref[0, hd, :, i * rows:(i + 1) * rows] = jnp.broadcast_to(lse, (rows, HEAD)).T[0:1, :]


def attend(me, q_all, k_all, v_all, seq0, n_seq, filled, heads=2):
    n_piece, n_all, rows, d_model = q_all.shape
    n_heads = d_model // HEAD
    per = n_heads // heads // 4
    shape = (n_piece, 1, rows, heads * HEAD)
    blk = pl.BlockSpec(shape, lambda s, h, m: (0, seq0 + s, 0, h))
    rel = pl.BlockSpec(shape, lambda s, h, m: (0, seq0 + s, 0, place(m[0] ^ (h // per)) * per + h % per))
    seq = n_piece * rows
    big = jax.ShapeDtypeStruct(q_all.shape, BF16)
    return pl.pallas_call(
        attend_kernel,
        grid_spec=pltpu.PrefetchScalarGridSpec(
            num_scalar_prefetch=1,
            grid=(n_seq, n_heads // heads),
            in_specs=[blk] * 3 + [ANY] * len(filled),
            out_specs=[blk, rel, pl.BlockSpec((1, heads, 1, seq), lambda s, h, m: (seq0 + s, h, 0, 0))],
        ),
        out_shape=[big, big, jax.ShapeDtypeStruct((n_all, n_heads, 1, seq), F32)],
        input_output_aliases={4 + n: n for n in range(len(filled))},
        compiler_params=pltpu.CompilerParams(vmem_limit_bytes=VMEM, dimension_semantics=("arbitrary", "arbitrary")),
        cost_estimate=pl.CostEstimate(flops=6 * n_seq * seq * seq * d_model, bytes_accessed=10 * n_seq * seq * d_model, transcendentals=0),
        name="attend",
    )(me, q_all, k_all, v_all, *filled)


def attend_back_kernel(q_ref, k_ref, v_ref, do_ref, lse_ref, dq_ref, dk_ref, dv_ref, dk_acc, dv_acc):
    n_piece, _, rows, width = q_ref.shape
    keep = lax.broadcasted_iota(jnp.int32, (rows, rows), 0) <= lax.broadcasted_iota(jnp.int32, (rows, rows), 1)
    for hd in range(width // HEAD):
        cols = head_cols(hd)
        k_t = [k_ref[j, 0, :, cols].T for j in range(n_piece)]
        for i in range(n_piece):
            q_i = q_ref[i, 0, :, cols]
            do_i = do_ref[i, 0, :, cols]
            lse = lse_ref[0, hd, :, i * rows:(i + 1) * rows]
            probs, d_probs = [], []
            row_dot = None
            for j in range(i + 1):
                prob = jnp.exp2(dot_nt(k_ref[j, 0, :, cols], q_i) * SCALE2 - lse)
                if j == i:
                    prob = jnp.where(keep, prob, 0.0)
                d_prob = dot_nt(v_ref[j, 0, :, cols], do_i)
                part = jnp.sum(prob * d_prob, axis=0, keepdims=True)
                row_dot = part if row_dot is None else row_dot + part
                probs.append(prob)
                d_probs.append(d_prob)
            dq_t = None
            for j in range(i + 1):
                d_s = (probs[j] * (d_probs[j] - row_dot) * SCALE).astype(BF16)
                dv_term = dot_nn(probs[j].astype(BF16), do_i)
                dk_term = dot_nn(d_s, q_i)
                dq_term = dot_nn(k_t[j], d_s)
                dq_t = dq_term if dq_t is None else dq_t + dq_term
                if i == j:
                    dv_acc[hd, j] = dv_term
                    dk_acc[hd, j] = dk_term
                else:
                    dv_acc[hd, j] += dv_term
                    dk_acc[hd, j] += dk_term
            dq_ref[i, 0, :, cols] = dq_t.T.astype(BF16)
        for j in range(n_piece):
            dk_ref[j, 0, :, cols] = dk_acc[hd, j].astype(BF16)
            dv_ref[j, 0, :, cols] = dv_acc[hd, j].astype(BF16)


def attend_back(q_all, k_all, v_all, d_out, lse, heads=2):
    n_piece, n_seq, rows, d_model = q_all.shape
    n_heads = d_model // HEAD
    blk = pl.BlockSpec((n_piece, 1, rows, heads * HEAD), lambda s, h: (0, s, 0, h))
    seq = n_piece * rows
    return pl.pallas_call(
        attend_back_kernel,
        grid=(n_seq, n_heads // heads),
        in_specs=[blk] * 4 + [pl.BlockSpec((1, heads, 1, seq), lambda s, h: (s, h, 0, 0))],
        out_specs=[blk] * 3,
        out_shape=[jax.ShapeDtypeStruct(q_all.shape, BF16)] * 3,
        scratch_shapes=[pltpu.VMEM((heads, n_piece, rows, HEAD), F32)] * 2,
        compiler_params=pltpu.CompilerParams(vmem_limit_bytes=VMEM, dimension_semantics=("arbitrary", "arbitrary")),
        cost_estimate=pl.CostEstimate(flops=14 * n_seq * seq * seq * d_model, bytes_accessed=14 * n_seq * seq * d_model, transcendentals=0),
        name="attend_back",
    )(q_all, k_all, v_all, d_out, lse)


def tail_kernel(dq_ref, dk_ref, dv_ref, q1_ref, k1_ref, x_ref, dy_ref, cos_ref, sin_ref, gn_ref, gq_ref, gk_ref, wq_ref, wk_ref, wv_ref, *refs):
    dqr_ref, dkr_ref, gx_ref, ggn_ref, ggq_ref, ggk_ref, dh_ref, rot_ref = refs[-8:]
    rows, d_model = x_ref.shape
    n_heads = d_model // HEAD
    n_col = 512
    cos_t = cos_ref[...]
    sin_t = sin_ref[...]

    @pl.when((pl.program_id(0) == 0) & (pl.program_id(1) == 0))
    def _():
        for ref in (ggn_ref, ggq_ref, ggk_ref):
            ref[...] = jnp.zeros_like(ref)

    dv_b = dv_ref[...]
    for c0 in range(0, d_model, n_col):
        dh_ref[:, c0:c0 + n_col] = dot_nt(dv_b, wv_ref[c0:c0 + n_col, :])
    for d_ref, raw_ref, g_ref, w_ref, dr_ref, gg_ref in ((dq_ref, q1_ref, gq_ref, wq_ref, dqr_ref, ggq_ref), (dk_ref, k1_ref, gk_ref, wk_ref, dkr_ref, ggk_ref)):
        sq = jnp.zeros((rows, HEAD), F32)
        cross = jnp.zeros((rows, HEAD), F32)
        for j in range(n_heads):
            u = raw_ref[:, head_cols(j)]
            d = d_ref[:, head_cols(j)].astype(F32)
            d = d * cos_t - pltpu.roll(d, HEAD // 2, 1) * sin_t
            rot_ref[:, head_cols(j)] = d
            sq = sq + u * u
            cross = cross + d * g_ref[:, head_cols(j)] * u
        inv = lax.rsqrt(row_sum(sq) * (1.0 / d_model) + EPS)
        coef = row_sum(cross) * (1.0 / d_model) * inv * inv
        for j in range(n_heads):
            u = raw_ref[:, head_cols(j)]
            d = rot_ref[:, head_cols(j)]
            gg_ref[:, head_cols(j)] += jnp.sum(d * (u * inv), axis=0, keepdims=True)
            dr_ref[:, head_cols(j)] = (inv * (d * g_ref[:, head_cols(j)] - u * coef)).astype(BF16)
        d_b = dr_ref[...]
        for c0 in range(0, d_model, n_col):
            dh_ref[:, c0:c0 + n_col] += dot_nt(d_b, w_ref[c0:c0 + n_col, :])
    sq = jnp.zeros((rows, HEAD), F32)
    cross = jnp.zeros((rows, HEAD), F32)
    for j in range(n_heads):
        u = x_ref[:, head_cols(j)].astype(F32)
        sq = sq + u * u
        cross = cross + dh_ref[:, head_cols(j)] * gn_ref[:, head_cols(j)] * u
    inv = lax.rsqrt(row_sum(sq) * (1.0 / d_model) + EPS)
    coef = row_sum(cross) * (1.0 / d_model) * inv * inv
    for j in range(n_heads):
        u = x_ref[:, head_cols(j)].astype(F32)
        d = dh_ref[:, head_cols(j)]
        ggn_ref[:, head_cols(j)] += jnp.sum(d * (u * inv), axis=0, keepdims=True)
        g_x = dy_ref[:, head_cols(j)].astype(F32) + inv * (d * gn_ref[:, head_cols(j)] - u * coef)
        gx_ref[:, head_cols(j)] = g_x.astype(BF16)


def tail(dq, dk, dv, q1, k1, x_all, dy_all, cos_t, sin_t, g_norm, g_query, g_key, w_query, w_key, w_value, seq0, n_seq, filled):
    n_piece, _, rows, d_model = x_all.shape
    spot = lambda i, s: (i, seq0 + s, 0, 0)
    tok = pl.BlockSpec((None, None, rows, d_model), spot)
    table = pl.BlockSpec((None, None, rows, HEAD), spot)
    vec = pl.BlockSpec((1, d_model), lambda i, s: (0, 0))
    mat = pl.BlockSpec((d_model, d_model), lambda i, s: (0, 0), pipeline_mode=pl.Buffered(1))
    big = jax.ShapeDtypeStruct(x_all.shape, BF16)
    small = jax.ShapeDtypeStruct((1, d_model), F32)
    row = lambda g: g.astype(F32).reshape(1, d_model)
    n_tok = n_piece * n_seq * rows
    return pl.pallas_call(
        tail_kernel,
        grid=(n_piece, n_seq),
        in_specs=[tok] * 7 + [table] * 2 + [vec] * 3 + [mat] * 3 + [ANY] * len(filled),
        out_specs=[tok] * 3 + [vec] * 3,
        out_shape=[big] * 3 + [small] * 3,
        input_output_aliases={15 + n: n for n in range(len(filled))},
        scratch_shapes=[pltpu.VMEM((rows, d_model), F32)] * 2,
        compiler_params=pltpu.CompilerParams(vmem_limit_bytes=VMEM, dimension_semantics=("arbitrary", "arbitrary")),
        cost_estimate=pl.CostEstimate(flops=6 * n_tok * d_model * d_model, bytes_accessed=n_tok * d_model * 24 + 6 * d_model * d_model, transcendentals=0),
        name="tail",
    )(dq, dk, dv, q1, k1, x_all, dy_all, cos_t, sin_t, row(g_norm), row(g_query), row(g_key), w_query, w_key, w_value, *filled)


def rope_tables(positions):
    half = HEAD // 2
    inv_freq = ROPE_BASE ** (-jnp.arange(half, dtype=F32) * (2.0 / HEAD))
    angles = positions.astype(F32)[..., None] * inv_freq
    cos_t = jnp.cos(angles)
    sin_t = jnp.sin(angles)
    return jnp.concatenate([cos_t, cos_t], axis=-1), jnp.concatenate([-sin_t, sin_t], axis=-1)


def after(value, *earlier):
    return lax.optimization_barrier((value,) + earlier)[0]


def solution(mesh):
    n_sp = mesh.shape['sp']

    def to_peer(value, bits):
        return lax.ppermute(value, 'sp', [(i, i ^ bits) for i in range(n_sp)])

    def device_step(x_loc, grad_y, positions, g_norm, w_query, w_key, w_value, w_out, g_query, g_key):
        n_batch, rows, d_model = x_loc.shape
        n_seq = n_batch // n_sp
        step = n_seq // N_CHUNK
        me = lax.axis_index('sp')
        me_vec = jnp.reshape(me, (1,)).astype(jnp.int32)
        shape4 = (n_sp, n_seq, rows, d_model)
        flat = lambda arr: arr.reshape(-1, d_model)
        far_bits = (2, 3, 1)

        def piece(arr, bits, seq0, count):
            return lax.dynamic_slice(arr, (me ^ bits, seq0, 0, 0), (1, count, rows, d_model))

        def pieces(arr, seq0, count):
            cut = lax.optimization_barrier((arr,) + tuple(piece(arr, bits, seq0, count) for bits in far_bits))
            return cut[0], cut[1:]

        def send(parts):
            return [to_peer(p, bits) for p, bits in zip(parts, far_bits)]

        def put(buf, got, bits, seq0):
            return lax.dynamic_update_slice(buf, got, (me ^ bits, seq0, 0, 0))

        def grad_rows(rel, right):
            half = d_model // 2
            out = to_peer(dot_tn(rel[:, :half], right), 1)
            keep = dot_tn(rel[:, half:], right)
            far = keep[:half // 2] + out[:half // 2]
            got = to_peer(far, 2)
            return (keep[half // 2:], out[half // 2:], got), far

        pos = lax.all_to_all(positions.reshape(n_sp, n_seq, rows), 'sp', split_axis=0, concat_axis=0, tiled=True)
        x4 = x_loc.reshape(shape4)
        x_parts = [piece(x4, 1, 0, n_seq)[0]] + [piece(x4, bits, c * step, step)[0] for c in range(N_CHUNK) for bits in (2, 3)]
        x_near = to_peer(x_parts[0], 1)
        x_far = [[to_peer(x_parts[2 * c + bits - 1], bits) for bits in (2, 3)] for c in range(N_CHUNK)]
        dy4 = after(grad_y.reshape(shape4), *x_parts)
        dy4, dy_parts = pieces(dy4, 0, n_seq)
        dy_got = send(dy_parts)
        cos_t, sin_t = rope_tables(pos)
        gains_in = (g_norm, g_query, g_key)
        weights = (w_query, w_key, w_value)
        filled = front(me_vec, x_loc, x_near, True, (0, 1), 0, n_seq, cos_t, sin_t, *gains_in, *weights, ())
        attn = ()
        prev = cos_t
        for c in range(N_CHUNK):
            filled = front(me_vec, x_far[c][0], x_far[c][1], False, (2, 3), c * step, step, after(cos_t, prev), sin_t, *gains_in, *weights, tuple(filled))
            attn = attend(me_vec, filled[2], filled[3], filled[4], c * step, step, tuple(attn))
            prev = attn[2]
        x_all, h_rel, q, k, v, q1, k1 = filled
        attn, attn_rel, lse = attn
        y = (flat(x_all).astype(F32) + dot_nn(flat(attn), w_out)).astype(BF16).reshape(shape4)
        y, y_parts = pieces(y, 0, n_seq)
        y_got = send(y_parts)
        dy_all = jnp.where(after(me, *x_parts) >= 0, dy4, jnp.zeros_like(dy4))
        for bits, got in zip(far_bits, dy_got):
            dy_all = put(dy_all, after(got, y), bits, 0)
        w_o, far_o = grad_rows(flat(attn_rel), flat(dy_all))
        d_attn = dot_nt(flat(dy_all), w_out).astype(BF16).reshape(shape4)
        dq, dk, dv = attend_back(q, k, v, d_attn, after(lse, far_o))
        w_v, prev = grad_rows(flat(h_rel), flat(dv))
        tails = ()
        gains = 0.0
        gx_got = []
        for c in range(N_CHUNK):
            *tails, ggn, ggq, ggk = tail(dq, dk, dv, q1, k1, x_all, dy_all, after(cos_t, prev), sin_t, *gains_in, *weights, c * step, step, tuple(tails))
            tails[2], gx_parts = pieces(tails[2], c * step, step)
            gx_got.append(send(gx_parts))
            prev = gx_parts[0]
            gains = gains + jnp.concatenate([ggn, ggq, ggk], axis=0)
        dqr, dkr, gx = tails
        w_q, prev = grad_rows(flat(h_rel), flat(after(dqr, prev)))
        w_k, prev = grad_rows(flat(h_rel), flat(after(dkr, prev)))
        for bits, got in zip(far_bits, y_got):
            y = put(y, got, bits, 0)
        for c in range(N_CHUNK):
            for bits, got in zip(far_bits, gx_got[c]):
                gx = put(gx, got, bits, c * step)
        gains = gains + to_peer(gains, 1)
        gains = gains + to_peer(gains, 2)
        gains = lax.dynamic_slice_in_dim(gains, me * (d_model // n_sp), d_model // n_sp, axis=1)
        total = lambda terms: terms[0] + terms[1] + terms[2]
        join = lambda arr: arr.reshape(x_loc.shape)
        return (join(y), join(gx), gains[0], total(w_q), total(w_k), total(w_v), total(w_o), gains[1], gains[2])

    seq_spec = P('dp', 'sp', None)
    mat_rep = P(None, None)
    vec_rep = P(None)
    row_spec = P(('dp', 'sp'), None)
    vec_spec = P(('dp', 'sp'))
    return jax.shard_map(device_step, mesh=mesh, in_specs=(seq_spec, seq_spec, P('dp', 'sp'), vec_rep, mat_rep, mat_rep, mat_rep, mat_rep, vec_rep, vec_rep), out_specs=(seq_spec, seq_spec, vec_spec, row_spec, row_spec, row_spec, row_spec, vec_spec, vec_spec), check_vma=False)
```

time: 4980 us -> 1650 us (0.33)
  matrix products: 2600 us -> 267 us
  blocking collectives: 753 us -> 0 us
  Pallas kernels: 0 us -> 603 us
  other arithmetic: 557 us -> 78.4 us
  local copies, waits for them, and re-layouts: 438 us -> 93.6 us
    dot_general x68 -> x10, matrix products: 2600 us -> 267 us  [the longest x8 182 us: dot_tn(): lax.dot_general(a, b, (((0,), (0,)), ((), ())), preferred_element_type=F32)]
    all_to_all x3 -> x0, blocking collectives: 743 us -> none  [the longest x1 278 us: device_step(): attended = to_tokens(out_all).reshape(n_batch, loc_len, d_model)]
    pallas_call x0 -> x8, Pallas kernels: none -> 603 us  [the longest x2 168 us: tail(): pl.pallas_call(tail_kernel, grid=(n_piece, n_seq), in_specs=[tok] * 7 + [...]
    ppermute x0 -> x27, waiting for transfers between devices: none -> 571 us  [to_peer(): return lax.ppermute(value, 'sp', [(i, i ^ bits) for i in range(n_sp)])]
    all_to_all x5 -> x1, waiting for transfers between devices: 565 us -> 0.01 us  [device_step(): lax.all_to_all(positions.reshape(n_sp, n_seq, rows), 'sp', split_axis=0,...]
    reduce_sum x11 -> x0, other arithmetic: 193 us -> none  [the longest x8 121 us: block_step(): row_sum = jnp.sum(exp_scores, axis=-1, keepdims=True)]
    convert_element_type x7 -> x1, other arithmetic: 105 us -> 0.01 us  [rope_tables(): angles = positions.astype(F32)[..., None] * inv_freq]
    another operation x1 -> x0, other arithmetic: 92.2 us -> none
  transfers between devices with their start and end apart: 9 -> 28, of which waited for: 4 -> 7; matrix products, arithmetic and copies ran while one was open for 24% -> 19% of each run, Pallas kernels for 0% -> 17%
where the time goes in v1:
time: 1650 us; the launch traced here: 1640 us
  Pallas kernels  603 us (37%)
  waiting for transfers between devices  571 us (35%)
  matrix products  267 us (16%)
  local copies, waits for them, and re-layouts  93.6 us (6%)
  other arithmetic  78.4 us (5%)
  starting transfers between devices  25.9 us (2%)
    ppermute x27, waiting for transfers between devices, to_peer(): return lax.ppermute(value, 'sp', [(i, i ^ bits) for i in range(n_sp)])  571 us
    dot_general x8, matrix products, dot_tn(): lax.dot_general(a, b, (((0,), (0,)), ((), ())), preferred_element_type=F32)  182 us
    pallas_call x2, Pallas kernels, tail(): pl.pallas_call(tail_kernel, grid=(n_piece, n_seq), in_specs=[tok] * 7 + [...  168 us
    pallas_call x1, Pallas kernels, attend_back(): pl.pallas_call(attend_back_kernel, grid=(n_seq, n_heads // heads), in_spe...  162 us
    pallas_call x3, Pallas kernels, front(): pl.pallas_call(front_kernel, grid_spec=pltpu.PrefetchScalarGridSpec(num_s...  153 us
    pallas_call x2, Pallas kernels, attend(): pl.pallas_call(attend_kernel, grid_spec=pltpu.PrefetchScalarGridSpec(num_...  120 us
    dot_general x1, matrix products, dot_nn(): lax.dot_general(a, b, (((1,), (0,)), ((), ())), preferred_element_type=F32)  43 us
    dynamic_update_slice x12, local copies, waits for them, and re-layouts, put(): return lax.dynamic_update_slice(buf, got, (me ^ bits, seq0, 0, 0))  42.4 us
  transfers between devices with their start and end apart: 28, of which 7 were waited for; matrix products, arithmetic and copies ran while one was open for 19% of the time, Pallas kernels for 17%

profile of v1, /device:TPU:0, one launch (start us, length us, event | category | flops | bytes accessed | tf_op | source)
XLA Modules:
  0.0 1640.7 jit_solution(8851481485445797199)
XLA Ops:
  10.8 8.0 dynamic-slice_bitcast_fusion.1
  27.4 13.8 broadcast_select_fusion
  43.0 7.5 fusion.21
  56.1 70.9 %front.3 = (bf16[4,4,256,2048]{3,2,1,0:T(8,128)(2,1)}, bf16[4,4,256,2048]{3,2,1,0:T(8,128)(2,1)}, bf16[4,4,256,2048]{3,2,1,0:T(8,128)(2,1)}, bf16[4,4,256,2048]{...) custom-call(s32[1]{0:T(128)} %bitcast.me_ref, ...), custom_call_target="tpu_custom_call" | custom-call | flops 51539607552 | bytes 109051904 | tf_op jit(solution)/shard_map/front/pallas_call | solution.py:102
  127.5 40.9 %front.4 = (bf16[4,4,256,2048]{3,2,1,0:T(8,128)(2,1)}, bf16[4,4,256,2048]{3,2,1,0:T(8,128)(2,1)}, bf16[4,4,256,2048]{3,2,1,0:T(8,128)(2,1)}, bf16[4,4,256,2048]{...) custom-call(s32[1]{0:T(128)} %bitcast.me_ref, ...), custom_call_target="tpu_custom_call", output_to_operand_aliasing={{0}: (11, {}), {1}: (12, {}), {2}: (13, {}), {3}: (14, {}),... | custom-call | flops 25769803776 | bytes 67108864 | tf_op jit(solution)/shard_map/front/pallas_call | solution.py:102
  168.4 59.9 %attend.2 = (bf16[4,4,256,2048]{3,2,1,0:T(8,128)(2,1)}, bf16[4,4,256,2048]{3,2,1,0:T(8,128)(2,1)}, f32[4,16,1,1024]{3,2,1,0:T(1,128)}) custom-call(s32[1]{0:T(128)} %bitcast.me_ref, bf16[4,4,256,2048]{3,2,1,0:T(8,128)(2,1)} %get-tuple-element.87.q_ref.refs_2_, bf16[4,4,256,2048]{3,2,1,0:T(8,128)(2,1)} %get-tuple-element.88.k_ref.refs_3_, ...), custom_call_target="tpu_custom_call" | custom-call | flops 25769803776 | bytes 41943040 | tf_op jit(solution)/shard_map/attend/pallas_call | solution.py:156
  228.3 40.9 %front.5 = (bf16[4,4,256,2048]{3,2,1,0:T(8,128)(2,1)}, bf16[4,4,256,2048]{3,2,1,0:T(8,128)(2,1)}, bf16[4,4,256,2048]{3,2,1,0:T(8,128)(2,1)}, bf16[4,4,256,2048]{...) custom-call(s32[1]{0:T(128)} %bitcast.me_ref, ...), custom_call_target="tpu_custom_call", output_to_operand_aliasing={{0}: (11, {}), {1}: (12, {}), {2}: (13, {}), {3}: (14, {}),... | custom-call | flops 25769803776 | bytes 67108864 | tf_op jit(solution)/shard_map/front/pallas_call | solution.py:102
  269.2 59.9 %attend.3 = (bf16[4,4,256,2048]{3,2,1,0:T(8,128)(2,1)}, bf16[4,4,256,2048]{3,2,1,0:T(8,128)(2,1)}, f32[4,16,1,1024]{3,2,1,0:T(1,128)}) custom-call(s32[1]{0:T(128)} %bitcast.me_ref, bf16[4,4,256,2048]{3,2,1,0:T(8,128)(2,1)} %get-tuple-element.97.q_ref, ...), custom_call_target="tpu_custom_call", output_to_operand_aliasing={{0}: (4, {}), {1}: (5, {}), {2}: (6, {})} | custom-call | flops 25769803776 | bytes 41943040 | tf_op jit(solution)/shard_map/attend/pallas_call | solution.py:156
  329.1 43.0 %fusion = bf16[4096,2048]{1,0:T(8,128)(2,1)} fusion(bf16[4,4,256,2048]{3,2,1,0:T(8,128)(2,1)} %get-tuple-element.96.x_ref, bf16[4096,2048]{1,0:T(8,128)(2,1)} %bitcast.98, bf16[2048,2048]{1,0:T(8,128)(2,1)} %param.17), kind=kOutput, calls=%fused_computation.1 | convolution fusion | flops 34384904192 | bytes 58720256 | tf_op jit(solution)/shard_map/dot_general | solution.py:23
  372.1 9.5 constant_dynamic-slice_fusion.9
  394.3 22.6 %fusion.1 = f32[1024,2048]{1,0:T(8,128)} fusion(bf16[4096,2048]{1,0:T(8,128)(2,1)S(1)} %bitcast.53, bf16[4096,2048]{1,0:T(8,128)(2,1)} %bitcast.99), kind=kOutput, calls=%fused_computation.4 | convolution fusion | flops 17179869184 | bytes 33554432 | tf_op jit(solution)/shard_map/dot_general | solution.py:31
  417.3 21.2 %fusion.3 = f32[1024,2048]{1,0:T(8,128)} fusion(bf16[4096,2048]{1,0:T(8,128)(2,1)S(1)} %bitcast.54, bf16[4096,2048]{1,0:T(8,128)(2,1)} %bitcast.100), kind=kOutput, calls=%fused_computation.6 | convolution fusion | flops 17179869184 | bytes 33554432 | tf_op jit(solution)/shard_map/dot_general | solution.py:31
  438.4 42.0 %convolution_convert_fusion = bf16[4096,2048]{1,0:T(8,128)(2,1)} fusion(bf16[4096,2048]{1,0:T(8,128)(2,1)} %bitcast.55, bf16[2048,2048]{1,0:T(8,128)(2,1)} %param.17), kind=kOutput, calls=%fused_computation.3 | convolution fusion | flops 34368126976 | bytes 41943040 | tf_op jit(solution)/shard_map/dot_general | solution.py:27
  488.8 161.6 %attend_back.1 = (bf16[4,4,256,2048]{3,2,1,0:T(8,128)(2,1)}, bf16[4,4,256,2048]{3,2,1,0:T(8,128)(2,1)}, bf16[4,4,256,2048]{3,2,1,0:T(8,128)(2,1)}) custom-call(bf16[4,4,256,2048]{3,2,1,0:T(8,128)(2,1)} %get-tuple-element.97.q_ref, bf16[4,4,256,2048]{3,2,1,0:T(8,128)(2,1)} %get-tuple-element.98.k_ref, bf16[4,4,256,2048]{3,2,1,0:T(8,128)(2,1)} %get-tuple-element.99.v_ref, ...), custom_call_target="tpu_custom_call" | custom-call | flops 120259084288 | bytes 117440512 | tf_op jit(solution)/shard_map/attend_back/pallas_call | solution.py:217
  650.3 24.3 %fusion.9 = f32[1024,2048]{1,0:T(8,128)} fusion(bf16[4096,2048]{1,0:T(8,128)(2,1)} %bitcast.59, bf16[4096,2048]{1,0:T(8,128)(2,1)} %bitcast.45), kind=kOutput, calls=%fused_computation.12 | convolution fusion | flops 17179869184 | bytes 33554432 | tf_op jit(solution)/shard_map/dot_general | solution.py:31
  674.8 22.0 %fusion.15 = f32[1024,2048]{1,0:T(8,128)} fusion(bf16[4096,2048]{1,0:T(8,128)(2,1)} %bitcast.60, bf16[4096,2048]{1,0:T(8,128)(2,1)S(1)} %bitcast.48), kind=kOutput, calls=%fused_computation.18 | convolution fusion | flops 17179869184 | bytes 33554432 | tf_op jit(solution)/shard_map/dot_general | solution.py:31
  705.2 84.6 %tail.2 = (bf16[4,4,256,2048]{3,2,1,0:T(8,128)(2,1)}, bf16[4,4,256,2048]{3,2,1,0:T(8,128)(2,1)}, bf16[4,4,256,2048]{3,2,1,0:T(8,128)(2,1)}, f32[1,2048]{1,0:T(1,...) custom-call(bf16[4,4,256,2048]{3,2,1,0:T(8,128)(2,1)} %get-tuple-element.119.dq_ref, ...), custom_call_target="tpu_custom_call" | custom-call | flops 51539607552 | bytes 125829120 | tf_op jit(solution)/shard_map/tail/pallas_call | solution.py:293
  795.5 83.9 %tail.3 = (bf16[4,4,256,2048]{3,2,1,0:T(8,128)(2,1)}, bf16[4,4,256,2048]{3,2,1,0:T(8,128)(2,1)}, bf16[4,4,256,2048]{3,2,1,0:T(8,128)(2,1)}, f32[1,2048]{1,0:T(1,...) custom-call(bf16[4,4,256,2048]{3,2,1,0:T(8,128)(2,1)} %get-tuple-elemen, ...), custom_call_target="tpu_custom_call", output_to_operand_aliasing={{0}: (15, {}), {1}: (16, {}), {2}: (17, {})} | custom-call | flops 51539607552 | bytes 125829120 | tf_op jit(solution)/shard_map/tail/pallas_call | solution.py:293
  885.4 24.5 %fusion.7 = f32[1024,2048]{1,0:T(8,128)} fusion(bf16[4096,2048]{1,0:T(8,128)(2,1)} %bitcast.61, bf16[4096,2048]{1,0:T(8,128)(2,1)} %bitcast.46), kind=kOutput, calls=%fused_computation.10 | convolution fusion | flops 17179869184 | bytes 33554432 | tf_op jit(solution)/shard_map/dot_general | solution.py:31
  911.9 21.7 %fusion.13 = f32[1024,2048]{1,0:T(8,128)} fusion(bf16[4096,2048]{1,0:T(8,128)(2,1)} %bitcast.62, bf16[4096,2048]{1,0:T(8,128)(2,1)S(1)} %bitcast.51), kind=kOutput, calls=%fused_computation.16 | convolution fusion | flops 17179869184 | bytes 33554432 | tf_op jit(solution)/shard_map/dot_general | solution.py:31
  933.7 8.0 slice_add_fusion.4
  941.6 21.9 %fusion.5 = f32[1024,2048]{1,0:T(8,128)} fusion(bf16[4096,2048]{1,0:T(8,128)(2,1)} %bitcast.63, bf16[4096,2048]{1,0:T(8,128)(2,1)S(1)} %bitcast.52), kind=kOutput, calls=%fused_computation.8 | convolution fusion | flops 17179869184 | bytes 33554432 | tf_op jit(solution)/shard_map/dot_general | solution.py:31
  966.0 38.0 %collective-permute-done.5 = bf16[1,4,256,2048]{3,2,1,0:T(8,128)(2,1)} collective-permute-done((bf16[1,4,256,2048]{3,2,1,0:T(8,128)(2,1)}, bf16[1,4,256,2048]{3,2,1,0:T(8,128)(2,1)}, u32[]{:S(2)}, u32[]{:S(2)}) %collective-permute-start.5) | collective-permute-done | bytes 4194336 | tf_op jit(solution)/shard_map/ppermute | solution.py:324
  1010.6 82.5 %collective-permute-done.6 = bf16[1,4,256,2048]{3,2,1,0:T(8,128)(2,1)} collective-permute-done((bf16[1,4,256,2048]{3,2,1,0:T(8,128)(2,1)}, bf16[1,4,256,2048]{3,2,1,0:T(8,128)(2,1)}, u32[]{:S(2)}, u32[]{:S(2)}) %collective-permute-start.6) | collective-permute-done | bytes 4194336 | tf_op jit(solution)/shard_map/ppermute | solution.py:324
  1105.7 78.1 %collective-permute-done.26 = f32[512,2048]{1,0:T(8,128)} collective-permute-done((f32[512,2048]{1,0:T(8,128)}, f32[512,2048]{1,0:T(8,128)}, u32[]{:S(2)}, u32[]{:S(2)}) %collective-permute-start.26) | collective-permute-done | bytes 4194336 | tf_op jit(solution)/shard_map/ppermute | solution.py:324
  1185.4 43.9 %collective-permute-done.20 = f32[3,2048]{1,0:T(4,128)S(1)} collective-permute-done((f32[3,2048]{1,0:T(4,128)S(1)}, f32[3,2048]{1,0:T(4,128)S(1)}, u32[]{:S(2)}, u32[]{:S(2)}) %collective-permute-start.20) | collective-permute-done | bytes 24608 | tf_op jit(solution)/shard_map/ppermute | solution.py:324
  1231.1 24.1 %fusion.11 = f32[1024,2048]{1,0:T(8,128)} fusion(bf16[4096,2048]{1,0:T(8,128)(2,1)} %bitcast.64, bf16[4096,2048]{1,0:T(8,128)(2,1)} %bitcast.47), kind=kOutput, calls=%fused_computation.14 | convolution fusion | flops 17179869184 | bytes 33554432 | tf_op jit(solution)/shard_map/dot_general | solution.py:31
  1262.2 146.2 %collective-permute-done.14 = bf16[1,2,256,2048]{3,2,1,0:T(8,128)(2,1)} collective-permute-done((bf16[1,2,256,2048]{3,2,1,0:T(8,128)(2,1)}, bf16[1,2,256,2048]{3,2,1,0:T(8,128)(2,1)}, u32[]{:S(2)}, u32[]{:S(2)}) %collective-permute-start.14) | collective-permute-done | bytes 2097184 | tf_op jit(solution)/shard_map/ppermute | solution.py:324
  1430.0 113.2 %collective-permute-done.17 = bf16[1,2,256,2048]{3,2,1,0:T(8,128)(2,1)} collective-permute-done((bf16[1,2,256,2048]{3,2,1,0:T(8,128)(2,1)}, bf16[1,2,256,2048]{3,2,1,0:T(8,128)(2,1)}, u32[]{:S(2)}, u32[]{:S(2)}) %collective-permute-start.17) | collective-permute-done | bytes 2097184 | tf_op jit(solution)/shard_map/ppermute | solution.py:324
  1555.3 8.5 fusion.20
  1563.9 69.4 %collective-permute-done.24 = f32[512,2048]{1,0:T(8,128)} collective-permute-done((f32[512,2048]{1,0:T(8,128)}, f32[512,2048]{1,0:T(8,128)}, u32[]{:S(2)}, u32[]{:S(2)}) %collective-permute-start.24) | collective-permute-done | bytes 4194336 | tf_op jit(solution)/shard_map/ppermute | solution.py:324
  1633.3 6.9 fusion.19
  (154 shorter events, 135.6 us)
Async XLA Ops:
  5.5 48.9 %collective-permute-start.4 = (bf16[4,256,2048]{2,1,0:T(8,128)(2,1)}, bf16[4,256,2048]{2,1,0:T(8,128)(2,1)}, u32[]{:S(2)}, u32[]{:S(2)}) collective-permute-start(bf16[4,256,2048]{2,1,0:T(8,128)(2,1)} %dynamic-slice_bitcast_fusion), channel_id=1, source_target_pairs={{0,1},{1,0},{2,3},{3,2},{4,5},{5,4},{6,7},{7,6}} | collective-permute-start | bytes 12582920 | tf_op jit(solution)/shard_map/ppermute | solution.py:324
  6.9 36.1 %all-to-all-start = ((s32[4,4,256]{2,1,0:T(4,128)}), s32[4,4,256]{2,1,0:T(4,128)S(1)}, u32[]{:S(2)}, u32[]{:S(2)}) async-start(s32[4,4,256]{2,1,0:T(4,128)} %reshape.105), calls=%async_computation | async-start | bytes 32768 | tf_op jit(solution)/shard_map/all_to_all | solution.py:357
  18.8 108.2 %collective-permute-start.2 = (bf16[2,256,2048]{2,1,0:T(8,128)(2,1)}, bf16[2,256,2048]{2,1,0:T(8,128)(2,1)}, u32[]{:S(2)}, u32[]{:S(2)}) collective-permute-start(bf16[2,256,2048]{2,1,0:T(8,128)(2,1)} %get-tuple-element.162), channel_id=1, source_target_pairs={{0,2},{1,3},{2,0},{3,1},{4,6},{5,7},{6,4},{7,5}} | collective-permute-start | bytes 6291464 | tf_op jit(solution)/shard_map/ppermute | solution.py:324
  20.8 106.2 %collective-permute-start.3 = (bf16[2,256,2048]{2,1,0:T(8,128)(2,1)}, bf16[2,256,2048]{2,1,0:T(8,128)(2,1)}, u32[]{:S(2)}, u32[]{:S(2)}) collective-permute-start(bf16[2,256,2048]{2,1,0:T(8,128)(2,1)} %get-tuple-element.161), channel_id=1, source_target_pairs={{0,3},{1,2},{2,1},{3,0},{4,7},{5,6},{6,5},{7,4}} | collective-permute-start | bytes 6291464 | tf_op jit(solution)/shard_map/ppermute | solution.py:324
  20.8 207.4 %collective-permute-start = (bf16[2,256,2048]{2,1,0:T(8,128)(2,1)}, bf16[2,256,2048]{2,1,0:T(8,128)(2,1)}, u32[]{:S(2)}, u32[]{:S(2)}) collective-permute-start(bf16[2,256,2048]{2,1,0:T(8,128)(2,1)} %get-tuple-element.164), channel_id=1, source_target_pairs={{0,2},{1,3},{2,0},{3,1},{4,6},{5,7},{6,4},{7,5}} | collective-permute-start | bytes 6291464 | tf_op jit(solution)/shard_map/ppermute | solution.py:324
  22.6 205.7 %collective-permute-start.1 = (bf16[2,256,2048]{2,1,0:T(8,128)(2,1)}, bf16[2,256,2048]{2,1,0:T(8,128)(2,1)}, u32[]{:S(2)}, u32[]{:S(2)}) collective-permute-start(bf16[2,256,2048]{2,1,0:T(8,128)(2,1)} %get-tuple-element.163), channel_id=1, source_target_pairs={{0,3},{1,2},{2,1},{3,0},{4,7},{5,6},{6,5},{7,4}} | collective-permute-start | bytes 6291464 | tf_op jit(solution)/shard_map/ppermute | solution.py:324
  54.4 327.3 %collective-permute-start.8 = (bf16[1,4,256,2048]{3,2,1,0:T(8,128)(2,1)}, bf16[1,4,256,2048]{3,2,1,0:T(8,128)(2,1)}, u32[]{:S(2)}, u32[]{:S(2)}) collective-permute-start(bf16[1,4,256,2048]{3,2,1,0:T(8,128)(2,1)} %get-tuple-element.110), channel_id=1, source_target_pairs={{0,2},{1,3},{2,0},{3,1},{4,6},{5,7},{6,4},{7,5}} | collective-permute-start | bytes 12582920 | tf_op jit(solution)/shard_map/ppermute | solution.py:324
  127.0 254.6 %collective-permute-start.9 = (bf16[1,4,256,2048]{3,2,1,0:T(8,128)(2,1)}, bf16[1,4,256,2048]{3,2,1,0:T(8,128)(2,1)}, u32[]{:S(2)}, u32[]{:S(2)}) collective-permute-start(bf16[1,4,256,2048]{3,2,1,0:T(8,128)(2,1)} %get-tuple-element.112), channel_id=1, source_target_pairs={{0,3},{1,2},{2,1},{3,0},{4,7},{5,6},{6,5},{7,4}} | collective-permute-start | bytes 12582920 | tf_op jit(solution)/shard_map/ppermute | solution.py:324
  127.1 254.6 %collective-permute-start.10 = (bf16[1,4,256,2048]{3,2,1,0:T(8,128)(2,1)}, bf16[1,4,256,2048]{3,2,1,0:T(8,128)(2,1)}, u32[]{:S(2)}, u32[]{:S(2)}) collective-permute-start(bf16[1,4,256,2048]{3,2,1,0:T(8,128)(2,1)} %get-tuple-element.114), channel_id=1, source_target_pairs={{0,1},{1,0},{2,3},{3,2},{4,5},{5,4},{6,7},{7,6}} | collective-permute-start | bytes 12582920 | tf_op jit(solution)/shard_map/ppermute | solution.py:324
  417.0 63.5 %collective-permute-start.11 = (f32[1024,2048]{1,0:T(8,128)}, f32[1024,2048]{1,0:T(8,128)S(1)}, u32[]{:S(2)}, u32[]{:S(2)}) collective-permute-start(f32[1024,2048]{1,0:T(8,128)} %fusion.1), channel_id=1, source_target_pairs={{0,1},{1,0},{2,3},{3,2},{4,5},{5,4},{6,7},{7,6}} | collective-permute-start | bytes 25165832 | tf_op jit(solution)/shard_map/ppermute | solution.py:324
  674.6 22.3 %collective-permute-start.12 = (f32[1024,2048]{1,0:T(8,128)}, f32[1024,2048]{1,0:T(8,128)S(1)}, u32[]{:S(2)}, u32[]{:S(2)}) collective-permute-start(f32[1024,2048]{1,0:T(8,128)} %fusion.9), channel_id=1, source_target_pairs={{0,1},{1,0},{2,3},{3,2},{4,5},{5,4},{6,7},{7,6}} | collective-permute-start | bytes 25165832 | tf_op jit(solution)/shard_map/ppermute | solution.py:324
  909.9 23.7 %collective-permute-start.21 = (f32[1024,2048]{1,0:T(8,128)}, f32[1024,2048]{1,0:T(8,128)S(1)}, u32[]{:S(2)}, u32[]{:S(2)}) collective-permute-start(f32[1024,2048]{1,0:T(8,128)} %fusion.7), channel_id=1, source_target_pairs={{0,1},{1,0},{2,3},{3,2},{4,5},{5,4},{6,7},{7,6}} | collective-permute-start | bytes 25165832 | tf_op jit(solution)/shard_map/ppermute | solution.py:324
  910.2 93.8 %collective-permute-start.5 = (bf16[1,4,256,2048]{3,2,1,0:T(8,128)(2,1)}, bf16[1,4,256,2048]{3,2,1,0:T(8,128)(2,1)}, u32[]{:S(2)}, u32[]{:S(2)}) collective-permute-start(bf16[1,4,256,2048]{3,2,1,0:T(8,128)(2,1)} %get-tuple-element.104), channel_id=1, source_target_pairs={{0,2},{1,3},{2,0},{3,1},{4,6},{5,7},{6,4},{7,5}} | collective-permute-start | bytes 12582920 | tf_op jit(solution)/shard_map/ppermute | solution.py:324
  963.7 291.6 %collective-permute-start.23 = (f32[1024,2048]{1,0:T(8,128)}, f32[1024,2048]{1,0:T(8,128)}, u32[]{:S(2)}, u32[]{:S(2)}) collective-permute-start(f32[1024,2048]{1,0:T(8,128)} %fusion.5), channel_id=1, source_target_pairs={{0,1},{1,0},{2,3},{3,2},{4,5},{5,4},{6,7},{7,6}} | collective-permute-start | bytes 25165832 | tf_op jit(solution)/shard_map/ppermute | solution.py:324
  963.8 129.2 %collective-permute-start.6 = (bf16[1,4,256,2048]{3,2,1,0:T(8,128)(2,1)}, bf16[1,4,256,2048]{3,2,1,0:T(8,128)(2,1)}, u32[]{:S(2)}, u32[]{:S(2)}) collective-permute-start(bf16[1,4,256,2048]{3,2,1,0:T(8,128)(2,1)} %get-tuple-element.105), channel_id=1, source_target_pairs={{0,3},{1,2},{2,1},{3,0},{4,7},{5,6},{6,5},{7,4}} | collective-permute-start | bytes 12582920 | tf_op jit(solution)/shard_map/ppermute | solution.py:324
  964.2 136.1 %collective-permute-start.7 = (bf16[1,4,256,2048]{3,2,1,0:T(8,128)(2,1)}, bf16[1,4,256,2048]{3,2,1,0:T(8,128)(2,1)}, u32[]{:S(2)}, u32[]{:S(2)}) collective-permute-start(bf16[1,4,256,2048]{3,2,1,0:T(8,128)(2,1)} %get-tuple-element.106), channel_id=1, source_target_pairs={{0,1},{1,0},{2,3},{3,2},{4,5},{5,4},{6,7},{7,6}} | collective-permute-start | bytes 12582920 | tf_op jit(solution)/shard_map/ppermute | solution.py:324
  964.3 219.5 %collective-permute-start.26 = (f32[512,2048]{1,0:T(8,128)}, f32[512,2048]{1,0:T(8,128)}, u32[]{:S(2)}, u32[]{:S(2)}) collective-permute-start(f32[512,2048]{1,0:T(8,128)} %slice_add_fusion.7), channel_id=1, source_target_pairs={{0,2},{1,3},{2,0},{3,1},{4,6},{5,7},{6,4},{7,5}} | collective-permute-start | bytes 12582920 | tf_op jit(solution)/shard_map/ppermute | solution.py:324
  1004.0 225.8 %collective-permute-start.13 = (bf16[1,2,256,2048]{3,2,1,0:T(8,128)(2,1)}, bf16[1,2,256,2048]{3,2,1,0:T(8,128)(2,1)}, u32[]{:S(2)}, u32[]{:S(2)}) collective-permute-start(bf16[1,2,256,2048]{3,2,1,0:T(8,128)(2,1)} %get-tuple-element.127), channel_id=1, source_target_pairs={{0,2},{1,3},{2,0},{3,1},{4,6},{5,7},{6,4},{7,5}} | collective-permute-start | bytes 6291464 | tf_op jit(solution)/shard_map/ppermute | solution.py:324
  1093.1 5.4 collective-permute-start.19
  1098.5 130.8 %collective-permute-start.20 = (f32[3,2048]{1,0:T(4,128)S(1)}, f32[3,2048]{1,0:T(4,128)S(1)}, u32[]{:S(2)}, u32[]{:S(2)}) collective-permute-start(f32[3,2048]{1,0:T(4,128)S(1)} %fusion.35), channel_id=1, source_target_pairs={{0,2},{1,3},{2,0},{3,1},{4,6},{5,7},{6,4},{7,5}} | collective-permute-start | bytes 73736 | tf_op jit(solution)/shard_map/ppermute | solution.py:324
  1100.2 310.4 %slice-start.8 = ((s8[8388608]{0:T(1024)(128)(4,1)}), s8[4194304]{0:T(1024)(128)(4,1)S(1)}, s32[]{:S(2)}) async-start(s8[8388608]{0:T(1024)(128)(4,1)} %bitcast.74), calls=%async_computation.9 | async-start | bytes 8388608
  1100.2 310.4 %slice-start.10 = ((s8[8388608]{0:T(1024)(128)(4,1)}), s8[4194304]{0:T(1024)(128)(4,1)S(1)}, s32[]{:S(2)}) async-start(s8[8388608]{0:T(1024)(128)(4,1)} %bitcast.76), calls=%async_computation.11 | async-start | bytes 8388608
  1105.3 305.4 %slice-start.9 = ((s8[8388608]{0:T(1024)(128)(4,1)}), s8[4194304]{0:T(1024)(128)(4,1)S(1)}, s32[]{:S(2)}) async-start(s8[8388608]{0:T(1024)(128)(4,1)} %bitcast.74), calls=%async_computation.10 | async-start | bytes 8388608
  1105.3 305.4 %slice-start.11 = ((s8[8388608]{0:T(1024)(128)(4,1)}), s8[4194304]{0:T(1024)(128)(4,1)S(1)}, s32[]{:S(2)}) async-start(s8[8388608]{0:T(1024)(128)(4,1)} %bitcast.76), calls=%async_computation.12 | async-start | bytes 8388608
  1105.3 444.2 %collective-permute-start.25 = (f32[512,2048]{1,0:T(8,128)S(1)}, f32[512,2048]{1,0:T(8,128)}, u32[]{:S(2)}, u32[]{:S(2)}) collective-permute-start(f32[512,2048]{1,0:T(8,128)S(1)} %copy-done.7), channel_id=1, source_target_pairs={{0,2},{1,3},{2,0},{3,1},{4,6},{5,7},{6,4},{7,5}} | collective-permute-start | bytes 12582920 | tf_op jit(solution)/shard_map/ppermute | solution.py:324
  1183.8 226.5 %collective-permute-start.16 = (bf16[1,2,256,2048]{3,2,1,0:T(8,128)(2,1)}, bf16[1,2,256,2048]{3,2,1,0:T(8,128)(2,1)}, u32[]{:S(2)}, u32[]{:S(2)}) collective-permute-start(bf16[1,2,256,2048]{3,2,1,0:T(8,128)(2,1)} %get-tuple-element.136), channel_id=1, source_target_pairs={{0,2},{1,3},{2,0},{3,1},{4,6},{5,7},{6,4},{7,5}} | collective-permute-start | bytes 6291464 | tf_op jit(solution)/shard_map/ppermute | solution.py:324
  1229.3 179.1 %collective-permute-start.14 = (bf16[1,2,256,2048]{3,2,1,0:T(8,128)(2,1)}, bf16[1,2,256,2048]{3,2,1,0:T(8,128)(2,1)}, u32[]{:S(2)}, u32[]{:S(2)}) collective-permute-start(bf16[1,2,256,2048]{3,2,1,0:T(8,128)(2,1)} %get-tuple-element.134), channel_id=1, source_target_pairs={{0,3},{1,2},{2,1},{3,0},{4,7},{5,6},{6,5},{7,4}} | collective-permute-start | bytes 6291464 | tf_op jit(solution)/shard_map/ppermute | solution.py:324
  1229.8 180.5 %collective-permute-start.15 = (bf16[1,2,256,2048]{3,2,1,0:T(8,128)(2,1)S(1)}, bf16[1,2,256,2048]{3,2,1,0:T(8,128)(2,1)}, u32[]{:S(2)}, u32[]{:S(2)}) collective-permute-start(bf16[1,2,256,2048]{3,2,1,0:T(8,128)(2,1)S(1)} %copy-done.8), channel_id=1, source_target_pairs={{0,1},{1,0},{2,3},{3,2},{4,5},{5,4},{6,7},{7,6}} | collective-permute-start | bytes 6291464 | tf_op jit(solution)/shard_map/ppermute | solution.py:324
  1255.2 300.1 %collective-permute-start.22 = (f32[512,2048]{1,0:T(8,128)}, f32[512,2048]{1,0:T(8,128)}, u32[]{:S(2)}, u32[]{:S(2)}) collective-permute-start(f32[512,2048]{1,0:T(8,128)} %slice_add_fusion.4), channel_id=1, source_target_pairs={{0,2},{1,3},{2,0},{3,1},{4,6},{5,7},{6,4},{7,5}} | collective-permute-start | bytes 12582920 | tf_op jit(solution)/shard_map/ppermute | solution.py:324
  1408.4 134.8 %collective-permute-start.17 = (bf16[1,2,256,2048]{3,2,1,0:T(8,128)(2,1)}, bf16[1,2,256,2048]{3,2,1,0:T(8,128)(2,1)}, u32[]{:S(2)}, u32[]{:S(2)}) collective-permute-start(bf16[1,2,256,2048]{3,2,1,0:T(8,128)(2,1)} %get-tuple-element.137), channel_id=1, source_target_pairs={{0,3},{1,2},{2,1},{3,0},{4,7},{5,6},{6,5},{7,4}} | collective-permute-start | bytes 6291464 | tf_op jit(solution)/shard_map/ppermute | solution.py:324
  1410.3 136.1 %collective-permute-start.18 = (bf16[1,2,256,2048]{3,2,1,0:T(8,128)(2,1)}, bf16[1,2,256,2048]{3,2,1,0:T(8,128)(2,1)}, u32[]{:S(2)}, u32[]{:S(2)}) collective-permute-start(bf16[1,2,256,2048]{3,2,1,0:T(8,128)(2,1)} %get-tuple-element.138), channel_id=1, source_target_pairs={{0,1},{1,0},{2,3},{3,2},{4,5},{5,4},{6,7},{7,6}} | collective-permute-start | bytes 6291464 | tf_op jit(solution)/shard_map/ppermute | solution.py:324
  1410.3 223.0 %collective-permute-start.24 = (f32[512,2048]{1,0:T(8,128)}, f32[512,2048]{1,0:T(8,128)}, u32[]{:S(2)}, u32[]{:S(2)}) collective-permute-start(f32[512,2048]{1,0:T(8,128)} %slice_add_fusion.2), channel_id=1, source_target_pairs={{0,2},{1,3},{2,0},{3,1},{4,6},{5,7},{6,4},{7,5}} | collective-permute-start | bytes 12582920 | tf_op jit(solution)/shard_map/ppermute | solution.py:324
  (29 other events, 1528.7 us)

commit v2 on v1

--- a/solution.py
+++ b/solution.py
@@ -44,6 +44,17 @@
 
 def place(bits):
     return jnp.where((bits == 0) | (bits == 3), 3 - bits, bits)
+
+
+def front_own_kernel(*refs):
+    dy_ref, *dy_outs = refs[11], *refs[-N_CHUNK:]
+    per = pl.num_programs(1) // N_CHUNK
+    for c, out_ref in enumerate(dy_outs):
+        @pl.when((pl.program_id(0) == 0) & (pl.program_id(1) // per == c))
+        def _():
+            out_ref[...] = dy_ref[...]
+
+    front_kernel(*refs[:11], *refs[12:-N_CHUNK])
 
 
 def front_kernel(me_ref, xa_ref, xb_ref, cos_ref, sin_ref, gn_ref, gq_ref, gk_ref, wq_ref, wk_ref, wv_ref, *refs):
@@ -85,7 +96,7 @@
         v_ref[:, c0:c0 + n_col] = dot_nn(hidden, wv_ref[:, c0:c0 + n_col]).astype(BF16)
 
 
-def front(me, x_a, x_b, own, bits, seq0, n_seq, cos_t, sin_t, g_norm, g_query, g_key, w_query, w_key, w_value, filled):
+def front(me, x_a, x_b, own, bits, seq0, n_seq, cos_t, sin_t, g_norm, g_query, g_key, w_query, w_key, w_value, filled, grad_y=None):
     n_piece, n_all, rows, d_model = cos_t.shape[:3] + x_a.shape[-1:]
     first = lambda i, s: jnp.where(i == 0, s, n_seq - 1)
     second = lambda i, s: jnp.where(i == 0, 0, s)
@@ -99,49 +110,59 @@
     big = lambda dt: jax.ShapeDtypeStruct((n_piece, n_all, rows, d_model), dt)
     row = lambda g: g.astype(F32).reshape(1, d_model)
     n_tok = 2 * n_seq * rows
+    per = n_seq // N_CHUNK
+
+    def own_out(c):
+        return pl.BlockSpec((None, None, rows, d_model), lambda i, s, m: (m[0], jnp.clip(first(i, s) - c * per, 0, per - 1), 0, 0))
+
+    dy_in, dy_outs, dy_shapes = [], [], []
+    if own:
+        dy_in = [pl.BlockSpec(x_block, a_map)]
+        dy_outs = [own_out(c) for c in range(N_CHUNK)]
+        dy_shapes = [jax.ShapeDtypeStruct((n_piece, per, rows, d_model), BF16)] * N_CHUNK
     return pl.pallas_call(
-        front_kernel,
+        front_own_kernel if own else front_kernel,
         grid_spec=pltpu.PrefetchScalarGridSpec(
             num_scalar_prefetch=1,
             grid=(2, n_seq),
-            in_specs=[pl.BlockSpec(x_block, a_map), pl.BlockSpec(x_block, lambda i, s, m: (second(i, s), 0, 0)), table, table, vec, vec, vec, mat, mat, mat] + [ANY] * len(filled),
-            out_specs=[out] * 7,
+            in_specs=[pl.BlockSpec(x_block, a_map), pl.BlockSpec(x_block, lambda i, s, m: (second(i, s), 0, 0)), table, table, vec, vec, vec, mat, mat, mat] + dy_in + [ANY] * len(filled),
+            out_specs=[out] * 7 + dy_outs,
         ),
-        out_shape=[big(BF16)] * 5 + [big(F32)] * 2,
+        out_shape=[big(BF16)] * 5 + [big(F32)] * 2 + dy_shapes,
         input_output_aliases={11 + n: n for n in range(len(filled))},
         compiler_params=pltpu.CompilerParams(vmem_limit_bytes=VMEM, dimension_semantics=("arbitrary", "arbitrary")),
         cost_estimate=pl.CostEstimate(flops=6 * n_tok * d_model * d_model, bytes_accessed=n_tok * d_model * 20 + 6 * d_model * d_model, transcendentals=0),
         name="front",
-    )(me, x_a, x_b, cos_t, sin_t, row(g_norm), row(g_query), row(g_key), w_query, w_key, w_value, *filled)
+    )(me, x_a, x_b, cos_t, sin_t, row(g_norm), row(g_query), row(g_key), w_query, w_key, w_value, *([grad_y] if own else []), *filled)
 
 
 def attend_kernel(me_ref, q_ref, k_ref, v_ref, *refs):
-    o_ref, rel_ref, lse_ref = refs[-3:]
+    rel_ref, o_ref, lse_ref = refs[-3:]
     n_piece, _, rows, width = q_ref.shape
-    keep = lax.broadcasted_iota(jnp.int32, (rows, rows), 0) >= lax.broadcasted_iota(jnp.int32, (rows, rows), 1)
+    keep = lax.broadcasted_iota(jnp.int32, (rows, rows), 0) <= lax.broadcasted_iota(jnp.int32, (rows, rows), 1)
     for hd in range(width // HEAD):
         cols = head_cols(hd)
+        v_t = [v_ref[j, 0, :, cols].T for j in range(n_piece)]
         for i in range(n_piece):
             q_i = q_ref[i, 0, :, cols]
-            scores = [dot_nt(q_i, k_ref[j, 0, :, cols]) for j in range(i + 1)]
+            scores = [dot_nt(k_ref[j, 0, :, cols], q_i) for j in range(i + 1)]
             scores[i] = jnp.where(keep, scores[i], NEG_BIG)
             top = scores[0]
             for j in range(1, i + 1):
                 top = jnp.maximum(top, scores[j])
-            top = jnp.max(top, axis=-1, keepdims=True) * SCALE2
+            top = jnp.max(top, axis=0, keepdims=True) * SCALE2
             total = None
             out = None
             for j in range(i + 1):
                 prob = jnp.exp2(scores[j] * SCALE2 - top)
-                total = prob if total is None else total + prob
-                term = dot_nn(prob.astype(BF16), v_ref[j, 0, :, cols])
+                part = jnp.sum(prob, axis=0, keepdims=True)
+                total = part if total is None else total + part
+                term = dot_nn(v_t[j], prob.astype(BF16))
                 out = term if out is None else out + term
-            total = row_sum(total)
-            out = (out * (1.0 / total)).astype(BF16)
+            out = (out * (1.0 / total)).astype(BF16).T
             o_ref[i, 0, :, cols] = out
             rel_ref[i, 0, :, cols] = out
-            lse = top + jnp.log2(total)
-            lse_ref[0, hd, :, i * rows:(i + 1) * rows] = jnp.broadcast_to(lse, (rows, HEAD)).T[0:1, :]
+            lse_ref[0, hd, :, i * rows:(i + 1) * rows] = top + jnp.log2(total)
 
 
 def attend(me, q_all, k_all, v_all, seq0, n_seq, filled, heads=2):
@@ -150,7 +171,7 @@
     per = n_heads // heads // 4
     shape = (n_piece, 1, rows, heads * HEAD)
     blk = pl.BlockSpec(shape, lambda s, h, m: (0, seq0 + s, 0, h))
-    rel = pl.BlockSpec(shape, lambda s, h, m: (0, seq0 + s, 0, place(m[0] ^ (h // per)) * per + h % per))
+    rel = pl.BlockSpec(shape, lambda s, h, m: (0, s, 0, place(m[0] ^ (h // per)) * per + h % per))
     seq = n_piece * rows
     big = jax.ShapeDtypeStruct(q_all.shape, BF16)
     return pl.pallas_call(
@@ -159,17 +180,18 @@
             num_scalar_prefetch=1,
             grid=(n_seq, n_heads // heads),
             in_specs=[blk] * 3 + [ANY] * len(filled),
-            out_specs=[blk, rel, pl.BlockSpec((1, heads, 1, seq), lambda s, h, m: (seq0 + s, h, 0, 0))],
+            out_specs=[rel, blk, pl.BlockSpec((1, heads, 1, seq), lambda s, h, m: (seq0 + s, h, 0, 0))],
         ),
-        out_shape=[big, big, jax.ShapeDtypeStruct((n_all, n_heads, 1, seq), F32)],
-        input_output_aliases={4 + n: n for n in range(len(filled))},
+        out_shape=[jax.ShapeDtypeStruct((n_piece, n_seq, rows, d_model), BF16), big, jax.ShapeDtypeStruct((n_all, n_heads, 1, seq), F32)],
+        input_output_aliases={4 + n: n + 1 for n in range(len(filled))},
         compiler_params=pltpu.CompilerParams(vmem_limit_bytes=VMEM, dimension_semantics=("arbitrary", "arbitrary")),
         cost_estimate=pl.CostEstimate(flops=6 * n_seq * seq * seq * d_model, bytes_accessed=10 * n_seq * seq * d_model, transcendentals=0),
         name="attend",
     )(me, q_all, k_all, v_all, *filled)
 
 
-def attend_back_kernel(q_ref, k_ref, v_ref, do_ref, lse_ref, dq_ref, dk_ref, dv_ref, dk_acc, dv_acc):
+def attend_back_kernel(q_ref, k_ref, v_ref, do_ref, lse_ref, *refs):
+    dq_ref, dk_ref, dv_ref, dk_acc, dv_acc = refs[-5:]
     n_piece, _, rows, width = q_ref.shape
     keep = lax.broadcasted_iota(jnp.int32, (rows, rows), 0) <= lax.broadcasted_iota(jnp.int32, (rows, rows), 1)
     for hd in range(width // HEAD):
@@ -192,7 +214,7 @@
                 d_probs.append(d_prob)
             dq_t = None
             for j in range(i + 1):
-                d_s = (probs[j] * (d_probs[j] - row_dot) * SCALE).astype(BF16)
+                d_s = (probs[j] * (d_probs[j] - row_dot)).astype(BF16)
                 dv_term = dot_nn(probs[j].astype(BF16), do_i)
                 dk_term = dot_nn(d_s, q_i)
                 dq_term = dot_nn(k_t[j], d_s)
@@ -203,28 +225,31 @@
                 else:
                     dv_acc[hd, j] += dv_term
                     dk_acc[hd, j] += dk_term
-            dq_ref[i, 0, :, cols] = dq_t.T.astype(BF16)
+            dq_ref[i, 0, :, cols] = (dq_t * SCALE).astype(BF16).T
         for j in range(n_piece):
-            dk_ref[j, 0, :, cols] = dk_acc[hd, j].astype(BF16)
+            dk_ref[j, 0, :, cols] = (dk_acc[hd, j] * SCALE).astype(BF16)
             dv_ref[j, 0, :, cols] = dv_acc[hd, j].astype(BF16)
 
 
-def attend_back(q_all, k_all, v_all, d_out, lse, heads=2):
-    n_piece, n_seq, rows, d_model = q_all.shape
+def attend_back(q_all, k_all, v_all, d_out, lse, seq0, n_seq, filled, heads=2):
+    n_piece, _, rows, d_model = q_all.shape
     n_heads = d_model // HEAD
-    blk = pl.BlockSpec((n_piece, 1, rows, heads * HEAD), lambda s, h: (0, s, 0, h))
+    shape = (n_piece, 1, rows, heads * HEAD)
+    blk = pl.BlockSpec(shape, lambda s, h: (0, seq0 + s, 0, h))
+    loc = pl.BlockSpec(shape, lambda s, h: (0, s, 0, h))
     seq = n_piece * rows
     return pl.pallas_call(
         attend_back_kernel,
         grid=(n_seq, n_heads // heads),
-        in_specs=[blk] * 4 + [pl.BlockSpec((1, heads, 1, seq), lambda s, h: (s, h, 0, 0))],
-        out_specs=[blk] * 3,
-        out_shape=[jax.ShapeDtypeStruct(q_all.shape, BF16)] * 3,
+        in_specs=[blk] * 3 + [loc, pl.BlockSpec((1, heads, 1, seq), lambda s, h: (seq0 + s, h, 0, 0))] + [ANY] * len(filled),
+        out_specs=[loc, loc, blk],
+        out_shape=[jax.ShapeDtypeStruct(d_out.shape, BF16)] * 2 + [jax.ShapeDtypeStruct(q_all.shape, BF16)],
+        input_output_aliases={5: 2} if filled else {},
         scratch_shapes=[pltpu.VMEM((heads, n_piece, rows, HEAD), F32)] * 2,
         compiler_params=pltpu.CompilerParams(vmem_limit_bytes=VMEM, dimension_semantics=("arbitrary", "arbitrary")),
         cost_estimate=pl.CostEstimate(flops=14 * n_seq * seq * seq * d_model, bytes_accessed=14 * n_seq * seq * d_model, transcendentals=0),
         name="attend_back",
-    )(q_all, k_all, v_all, d_out, lse)
+    )(q_all, k_all, v_all, d_out, lse, *filled)
 
 
 def tail_kernel(dq_ref, dk_ref, dv_ref, q1_ref, k1_ref, x_ref, dy_ref, cos_ref, sin_ref, gn_ref, gq_ref, gk_ref, wq_ref, wk_ref, wv_ref, *refs):
@@ -279,10 +304,11 @@
         gx_ref[:, head_cols(j)] = g_x.astype(BF16)
 
 
-def tail(dq, dk, dv, q1, k1, x_all, dy_all, cos_t, sin_t, g_norm, g_query, g_key, w_query, w_key, w_value, seq0, n_seq, filled):
+def tail(dq, dk, dv, q1, k1, x_all, dy, cos_t, sin_t, g_norm, g_query, g_key, w_query, w_key, w_value, seq0, n_seq, filled):
     n_piece, _, rows, d_model = x_all.shape
     spot = lambda i, s: (i, seq0 + s, 0, 0)
     tok = pl.BlockSpec((None, None, rows, d_model), spot)
+    loc = pl.BlockSpec((None, None, rows, d_model), lambda i, s: (i, s, 0, 0))
     table = pl.BlockSpec((None, None, rows, HEAD), spot)
     vec = pl.BlockSpec((1, d_model), lambda i, s: (0, 0))
     mat = pl.BlockSpec((d_model, d_model), lambda i, s: (0, 0), pipeline_mode=pl.Buffered(1))
@@ -293,7 +319,7 @@
     return pl.pallas_call(
         tail_kernel,
         grid=(n_piece, n_seq),
-        in_specs=[tok] * 7 + [table] * 2 + [vec] * 3 + [mat] * 3 + [ANY] * len(filled),
+        in_specs=[loc] * 2 + [tok] * 4 + [loc] + [table] * 2 + [vec] * 3 + [mat] * 3 + [ANY] * len(filled),
         out_specs=[tok] * 3 + [vec] * 3,
         out_shape=[big] * 3 + [small] * 3,
         input_output_aliases={15 + n: n for n in range(len(filled))},
@@ -301,7 +327,7 @@
         compiler_params=pltpu.CompilerParams(vmem_limit_bytes=VMEM, dimension_semantics=("arbitrary", "arbitrary")),
         cost_estimate=pl.CostEstimate(flops=6 * n_tok * d_model * d_model, bytes_accessed=n_tok * d_model * 24 + 6 * d_model * d_model, transcendentals=0),
         name="tail",
-    )(dq, dk, dv, q1, k1, x_all, dy_all, cos_t, sin_t, row(g_norm), row(g_query), row(g_key), w_query, w_key, w_value, *filled)
+    )(dq, dk, dv, q1, k1, x_all, dy, cos_t, sin_t, row(g_norm), row(g_query), row(g_key), w_query, w_key, w_value, *filled)
 
 
 def rope_tables(positions):
@@ -346,56 +372,75 @@
         def put(buf, got, bits, seq0):
             return lax.dynamic_update_slice(buf, got, (me ^ bits, seq0, 0, 0))
 
-        def grad_rows(rel, right):
+        def grad_rows(rels, rights):
             half = d_model // 2
-            out = to_peer(dot_tn(rel[:, :half], right), 1)
-            keep = dot_tn(rel[:, half:], right)
+
+            def part(cols):
+                terms = [dot_tn(flat(r)[:, cols], flat(g)) for r, g in zip(rels, rights)]
+                return sum(terms[1:], terms[0])
+
+            out = to_peer(part(slice(0, half)), 1)
+            keep = part(slice(half, None))
             far = keep[:half // 2] + out[:half // 2]
             got = to_peer(far, 2)
             return (keep[half // 2:], out[half // 2:], got), far
 
-        pos = lax.all_to_all(positions.reshape(n_sp, n_seq, rows), 'sp', split_axis=0, concat_axis=0, tiled=True)
+        pos4 = positions.reshape(n_sp, n_seq, rows)
+        pos4, *cut = lax.optimization_barrier([pos4] + [lax.dynamic_slice_in_dim(pos4, me ^ bits, 1, axis=0) for bits in far_bits])
+        for bits, got in zip(far_bits, send(cut)):
+            pos4 = lax.dynamic_update_slice_in_dim(pos4, got, me ^ bits, axis=0)
         x4 = x_loc.reshape(shape4)
-        x_parts = [piece(x4, 1, 0, n_seq)[0]] + [piece(x4, bits, c * step, step)[0] for c in range(N_CHUNK) for bits in (2, 3)]
-        x_near = to_peer(x_parts[0], 1)
-        x_far = [[to_peer(x_parts[2 * c + bits - 1], bits) for bits in (2, 3)] for c in range(N_CHUNK)]
-        dy4 = after(grad_y.reshape(shape4), *x_parts)
-        dy4, dy_parts = pieces(dy4, 0, n_seq)
-        dy_got = send(dy_parts)
-        cos_t, sin_t = rope_tables(pos)
+        x_parts = []
+        for c in range(N_CHUNK):
+            x_parts.append([piece(x4, bits, c * step, step)[0] for bits in (2, 3)])
+            x4 = after(x4, *x_parts[-1])
+            if c == 0:
+                x_near = piece(x4, 1, 0, n_seq)[0]
+        x_far = [[to_peer(p, bits) for p, bits in zip(x_parts[c], (2, 3))] for c in range(N_CHUNK)]
+        dy4 = after(grad_y.reshape(shape4), x_near, *x_parts[1])
+        x_near = to_peer(x_near, 1)
+        dy_got = [send([piece(dy4, bits, c * step, step) for bits in far_bits]) for c in range(N_CHUNK)]
+        cos_t, sin_t = rope_tables(pos4)
         gains_in = (g_norm, g_query, g_key)
         weights = (w_query, w_key, w_value)
-        filled = front(me_vec, x_loc, x_near, True, (0, 1), 0, n_seq, cos_t, sin_t, *gains_in, *weights, ())
+        filled = front(me_vec, x_loc, x_near, True, (0, 1), 0, n_seq, cos_t, sin_t, *gains_in, *weights, (), grad_y)
+        filled, dys = filled[:7], list(filled[7:])
         attn = ()
+        rels = []
         prev = cos_t
         for c in range(N_CHUNK):
             filled = front(me_vec, x_far[c][0], x_far[c][1], False, (2, 3), c * step, step, after(cos_t, prev), sin_t, *gains_in, *weights, tuple(filled))
-            attn = attend(me_vec, filled[2], filled[3], filled[4], c * step, step, tuple(attn))
-            prev = attn[2]
+            rel, *attn = attend(me_vec, filled[2], filled[3], filled[4], c * step, step, tuple(attn))
+            rels.append(rel)
+            prev = attn[1]
         x_all, h_rel, q, k, v, q1, k1 = filled
-        attn, attn_rel, lse = attn
+        attn, lse = attn
         y = (flat(x_all).astype(F32) + dot_nn(flat(attn), w_out)).astype(BF16).reshape(shape4)
         y, y_parts = pieces(y, 0, n_seq)
         y_got = send(y_parts)
-        dy_all = jnp.where(after(me, *x_parts) >= 0, dy4, jnp.zeros_like(dy4))
-        for bits, got in zip(far_bits, dy_got):
-            dy_all = put(dy_all, after(got, y), bits, 0)
-        w_o, far_o = grad_rows(flat(attn_rel), flat(dy_all))
-        d_attn = dot_nt(flat(dy_all), w_out).astype(BF16).reshape(shape4)
-        dq, dk, dv = attend_back(q, k, v, d_attn, after(lse, far_o))
-        w_v, prev = grad_rows(flat(h_rel), flat(dv))
-        tails = ()
+        prev = y_parts[0]
+        dv, tails, gx_got = (), (), []
         gains = 0.0
-        gx_got = []
         for c in range(N_CHUNK):
-            *tails, ggn, ggq, ggk = tail(dq, dk, dv, q1, k1, x_all, dy_all, after(cos_t, prev), sin_t, *gains_in, *weights, c * step, step, tuple(tails))
+            dy = dys[c]
+            for bits, got in zip(far_bits, dy_got[c]):
+                dy = put(dy, after(got, prev), bits, 0)
+            dys[c] = dy
+            if c == N_CHUNK - 1:
+                w_o, prev = grad_rows(rels, dys)
+            d_attn = dot_nt(flat(dy), w_out).astype(BF16).reshape(dy.shape)
+            dq, dk, *dv = attend_back(q, k, v, d_attn, after(lse, prev), c * step, step, tuple(dv))
+            prev = dq
+            if c == N_CHUNK - 1:
+                w_v, prev = grad_rows([h_rel], dv)
+            *tails, ggn, ggq, ggk = tail(dq, dk, dv[0], q1, k1, x_all, dy, after(cos_t, prev), sin_t, *gains_in, *weights, c * step, step, tuple(tails))
             tails[2], gx_parts = pieces(tails[2], c * step, step)
             gx_got.append(send(gx_parts))
             prev = gx_parts[0]
             gains = gains + jnp.concatenate([ggn, ggq, ggk], axis=0)
         dqr, dkr, gx = tails
-        w_q, prev = grad_rows(flat(h_rel), flat(after(dqr, prev)))
-        w_k, prev = grad_rows(flat(h_rel), flat(after(dkr, prev)))
+        w_q, prev = grad_rows([h_rel], [after(dqr, prev)])
+        w_k, prev = grad_rows([h_rel], [after(dkr, prev)])
         for bits, got in zip(far_bits, y_got):
             y = put(y, got, bits, 0)
         for c in range(N_CHUNK):

time: 1650 us -> 1760 us (1.067)
  waiting for transfers between devices: 571 us -> 697 us
  matrix products: 267 us -> 289 us
    ppermute x27 -> x33, waiting for transfers between devices: 571 us -> 697 us  [to_peer(): return lax.ppermute(value, 'sp', [(i, i ^ bits) for i in range(n_sp)])]
    dot_general x8 -> x10, matrix products: 182 us -> 197 us  [dot_tn(): lax.dot_general(a, b, (((0,), (0,)), ((), ())), preferred_element_type=F32)]
    dot_general x1 -> x2, matrix products: 42 us -> 50.4 us  [dot_nt(): lax.dot_general(a, b, (((1,), (1,)), ((), ())), preferred_element_type=F32)]
    dynamic_update_slice x12 -> x15, local copies, waits for them, and re-layouts: 42.4 us -> 49.5 us  [put(): return lax.dynamic_update_slice(buf, got, (me ^ bits, seq0, 0, 0))]
    pallas_call x1 -> x2, Pallas kernels: 162 us -> 159 us  [attend_back(): pl.pallas_call(attend_back_kernel, grid=(n_seq, n_heads // heads), in_spe...]
  transfers between devices with their start and end apart: 28 -> 33, of which waited for: 7 -> 11; matrix products, arithmetic and copies ran while one was open for 19% -> 19% of each run, Pallas kernels for 17% -> 24%
where the time goes in v2:
time: 1760 us
  waiting for transfers between devices  697 us (40%)
  Pallas kernels  586 us (33%)
  matrix products  289 us (16%)
  local copies, waits for them, and re-layouts  104 us (6%)
  other arithmetic  62.3 us (4%)
  starting transfers between devices  20.1 us (1%)
    ppermute x33, waiting for transfers between devices, to_peer(): return lax.ppermute(value, 'sp', [(i, i ^ bits) for i in range(n_sp)])  697 us
    dot_general x10, matrix products, dot_tn(): lax.dot_general(a, b, (((0,), (0,)), ((), ())), preferred_element_type=F32)  197 us
    pallas_call x2, Pallas kernels, tail(): pl.pallas_call(tail_kernel, grid=(n_piece, n_seq), in_specs=[loc] * 2 + [...  168 us
    pallas_call x2, Pallas kernels, attend_back(): pl.pallas_call(attend_back_kernel, grid=(n_seq, n_heads // heads), in_spe...  159 us
    pallas_call x3, Pallas kernels, front(): pl.pallas_call(front_own_kernel if own else front_kernel, grid_spec=pltpu...  154 us
    pallas_call x2, Pallas kernels, attend(): pl.pallas_call(attend_kernel, grid_spec=pltpu.PrefetchScalarGridSpec(num_...  105 us
    dot_general x2, matrix products, dot_nt(): lax.dot_general(a, b, (((1,), (1,)), ((), ())), preferred_element_type=F32)  50.4 us
    dynamic_update_slice x15, local copies, waits for them, and re-layouts, put(): return lax.dynamic_update_slice(buf, got, (me ^ bits, seq0, 0, 0))  49.5 us
  transfers between devices with their start and end apart: 33, of which 11 were waited for; matrix products, arithmetic and copies ran while one was open for 19% of the time, Pallas kernels for 24%

profile of v2, /device:TPU:0, one launch (start us, length us, event | category | flops | bytes accessed | tf_op | source)
XLA Modules:
  0.0 1758.9 jit_solution(13875812264503467728)
XLA Ops:
  31.7 73.6 %collective-permute-done.2 = s32[1,4,256]{2,1,0:T(4,128)S(1)} collective-permute-done((s32[1,4,256]{2,1,0:T(4,128)S(1)}, s32[1,4,256]{2,1,0:T(4,128)S(1)}, u32[]{:S(2)}, u32[]{:S(2)}) %collective-permute-start.2) | collective-permute-done | bytes 4128 | tf_op jit(solution)/shard_map/ppermute | solution.py:350
  106.2 43.8 %collective-permute-done.3 = s32[1,4,256]{2,1,0:T(4,128)S(1)} collective-permute-done((s32[1,4,256]{2,1,0:T(4,128)S(1)}, s32[1,4,256]{2,1,0:T(4,128)S(1)}, u32[]{:S(2)}, u32[]{:S(2)}) %collective-permute-start.3) | collective-permute-done | bytes 4128 | tf_op jit(solution)/shard_map/ppermute | solution.py:350
  164.5 72.2 %front.3 = (bf16[4,4,256,2048]{3,2,1,0:T(8,128)(2,1)}, bf16[4,4,256,2048]{3,2,1,0:T(8,128)(2,1)}, bf16[4,4,256,2048]{3,2,1,0:T(8,128)(2,1)}, bf16[4,4,256,2048]{...) custom-call(s32[1]{0:T(128)} %bitcast.refs_0_.me_ref, ...), custom_call_target="tpu_custom_call" | custom-call | flops 51539607552 | bytes 109051904 | tf_op jit(solution)/shard_map/front/pallas_call | solution.py:123
  238.8 40.9 %front.4 = (bf16[4,4,256,2048]{3,2,1,0:T(8,128)(2,1)}, bf16[4,4,256,2048]{3,2,1,0:T(8,128)(2,1)}, bf16[4,4,256,2048]{3,2,1,0:T(8,128)(2,1)}, bf16[4,4,256,2048]{...) custom-call(s32[1]{0:T(128)} %bitcast.refs_0_.me_ref, ...), custom_call_target="tpu_custom_call", output_to_operand_aliasing={{0}: (11, {}), {1}: (12, {}), {2}: (13, {}), {3}: (14, {}),... | custom-call | flops 25769803776 | bytes 67108864 | tf_op jit(solution)/shard_map/front/pallas_call | solution.py:123
  279.7 52.5 %attend.2 = (bf16[4,2,256,2048]{3,2,1,0:T(8,128)(2,1)}, bf16[4,4,256,2048]{3,2,1,0:T(8,128)(2,1)}, f32[4,16,1,1024]{3,2,1,0:T(1,128)}) custom-call(s32[1]{0:T(128)} %bitcast.refs_0_.me_ref, bf16[4,4,256,2048]{3,2,1,0:T(8,128)(2,1)} %get-tuple-element.101.q_ref.refs_2_, bf16[4,4,256,2048]{3,2,1,0:T(8,128)(2,1)} %get-tuple-element.102.k_ref.refs_3_, ...), custom_call_target="tpu_custom_call" | custom-call | flops 25769803776 | bytes 41943040 | tf_op jit(solution)/shard_map/attend/pallas_call | solution.py:177
  332.6 40.9 %front.5 = (bf16[4,4,256,2048]{3,2,1,0:T(8,128)(2,1)}, bf16[4,4,256,2048]{3,2,1,0:T(8,128)(2,1)}, bf16[4,4,256,2048]{3,2,1,0:T(8,128)(2,1)}, bf16[4,4,256,2048]{...) custom-call(s32[1]{0:T(128)} %bitcast.refs_0_.me_ref, ...), custom_call_target="tpu_custom_call", output_to_operand_aliasing={{0}: (11, {}), {1}: (12, {}), {2}: (13, {}), {3}: (14, {}),... | custom-call | flops 25769803776 | bytes 67108864 | tf_op jit(solution)/shard_map/front/pallas_call | solution.py:123
  373.5 52.6 %attend.3 = (bf16[4,2,256,2048]{3,2,1,0:T(8,128)(2,1)}, bf16[4,4,256,2048]{3,2,1,0:T(8,128)(2,1)}, f32[4,16,1,1024]{3,2,1,0:T(1,128)}) custom-call(s32[1]{0:T(128)} %bitcast.refs_0_.me_ref, bf16[4,4,256,2048]{3,2,1,0:T(8,128)(2,1)} %get-tuple-element.111.q_ref, ...), custom_call_target="tpu_custom_call", output_to_operand_aliasing={{1}: (4, {}), {2}: (5, {})} | custom-call | flops 25769803776 | bytes 41943040 | tf_op jit(solution)/shard_map/attend/pallas_call | solution.py:177
  426.1 41.6 %fusion = bf16[4096,2048]{1,0:T(8,128)(2,1)S(1)} fusion(bf16[4,4,256,2048]{3,2,1,0:T(8,128)(2,1)} %get-tuple-element.110.x_ref, bf16[4096,2048]{1,0:T(8,128)(2,1)} %bitcast.110, bf16[2048,2048]{1,0:T(8,128)(2,1)} %param.17), kind=kOutput, calls=%fused_computation.1 | convolution fusion | flops 34384904192 | bytes 58720256 | tf_op jit(solution)/shard_map/dot_general | solution.py:23
  489.0 23.6 %convolution_convert_fusion.1 = bf16[2048,2048]{1,0:T(8,128)(2,1)} fusion(bf16[2048,2048]{1,0:T(8,128)(2,1)} %bitcast.105, bf16[2048,2048]{1,0:T(8,128)(2,1)} %param.17), kind=kOutput, calls=%fused_computation.3 | convolution fusion | flops 17184063488 | bytes 25165824 | tf_op jit(solution)/shard_map/dot_general | solution.py:27
  512.7 79.3 %attend_back.2 = (bf16[4,2,256,2048]{3,2,1,0:T(8,128)(2,1)}, bf16[4,2,256,2048]{3,2,1,0:T(8,128)(2,1)}, bf16[4,4,256,2048]{3,2,1,0:T(8,128)(2,1)}) custom-call(bf16[4,4,256,2048]{3,2,1,0:T(8,128)(2,1)} %get-tuple-element.111.q_ref, bf16[4,4,256,2048]{3,2,1,0:T(8,128)(2,1)} %get-tuple-element.112.k_ref, bf16[4,4,256,2048]{3,2,1,0:T(8,128)(2,1)} %get-tuple-element.113.v_ref, ...), custom_call_target="tpu_custom_call" | custom-call | flops 60129542144 | bytes 58720256 | tf_op jit(solution)/shard_map/attend_back/pallas_call | solution.py:241
  592.0 83.7 %tail.2 = (bf16[4,4,256,2048]{3,2,1,0:T(8,128)(2,1)}, bf16[4,4,256,2048]{3,2,1,0:T(8,128)(2,1)}, bf16[4,4,256,2048]{3,2,1,0:T(8,128)(2,1)}, f32[1,2048]{1,0:T(1,...) custom-call(bf16[4,2,256,2048]{3,2,1,0:T(8,128)(2,1)} %get-tuple-element.128.dq_ref, ...), custom_call_target="tpu_custom_call" | custom-call | flops 51539607552 | bytes 125829120 | tf_op jit(solution)/shard_map/tail/pallas_call | solution.py:319
  688.9 16.1 fusion.17
  705.0 14.6 fusion.28
  719.6 13.7 fusion.21
  733.2 14.5 fusion.25
  747.7 26.8 %convolution_convert_fusion = bf16[2048,2048]{1,0:T(8,128)(2,1)} fusion(bf16[2048,2048]{1,0:T(8,128)(2,1)} %bitcast.86, bf16[2048,2048]{1,0:T(8,128)(2,1)} %param.17), kind=kOutput, calls=%fused_computation.2 | convolution fusion | flops 17184063488 | bytes 25165824 | tf_op jit(solution)/shard_map/dot_general | solution.py:27
  780.6 79.4 %attend_back.3 = (bf16[4,2,256,2048]{3,2,1,0:T(8,128)(2,1)}, bf16[4,2,256,2048]{3,2,1,0:T(8,128)(2,1)}, bf16[4,4,256,2048]{3,2,1,0:T(8,128)(2,1)}) custom-call(bf16[4,4,256,2048]{3,2,1,0:T(8,128)(2,1)} %get-tuple-element.111.q_ref, bf16[4,4,256,2048]{3,2,1,0:T(8,128)(2,1)} %get-tuple-element.112.k_ref, ...), custom_call_target="tpu_custom_call", output_to_operand_aliasing={{2}: (5, {})} | custom-call | flops 60129542144 | bytes 58720256 | tf_op jit(solution)/shard_map/attend_back/pallas_call | solution.py:241
  859.9 24.5 %fusion.5 = f32[1024,2048]{1,0:T(8,128)} fusion(bf16[4096,2048]{1,0:T(8,128)(2,1)} %bitcast.65, bf16[4096,2048]{1,0:T(8,128)(2,1)} %bitcast.52), kind=kOutput, calls=%fused_computation.8 | convolution fusion | flops 17179869184 | bytes 33554432 | tf_op jit(solution)/shard_map/dot_general | solution.py:31
  884.9 21.0 %fusion.11 = f32[1024,2048]{1,0:T(8,128)} fusion(bf16[4096,2048]{1,0:T(8,128)(2,1)S(1)} %bitcast.66, bf16[4096,2048]{1,0:T(8,128)(2,1)} %bitcast.53), kind=kOutput, calls=%fused_computation.14 | convolution fusion | flops 17179869184 | bytes 33554432 | tf_op jit(solution)/shard_map/dot_general | solution.py:31
  914.2 84.1 %tail.3 = (bf16[4,4,256,2048]{3,2,1,0:T(8,128)(2,1)}, bf16[4,4,256,2048]{3,2,1,0:T(8,128)(2,1)}, bf16[4,4,256,2048]{3,2,1,0:T(8,128)(2,1)}, f32[1,2048]{1,0:T(1,...) custom-call(bf16[4,2,256,2048]{3,2,1,0:T(8,128)(2,1)} %get-tuple-elemen, ...), custom_call_target="tpu_custom_call", output_to_operand_aliasing={{0}: (15, {}), {1}: (16, {}), {2}: (17, {})} | custom-call | flops 51539607552 | bytes 125829120 | tf_op jit(solution)/shard_map/tail/pallas_call | solution.py:319
  1004.1 24.5 %fusion.3 = f32[1024,2048]{1,0:T(8,128)} fusion(bf16[4096,2048]{1,0:T(8,128)(2,1)} %bitcast.61, bf16[4096,2048]{1,0:T(8,128)(2,1)} %bitcast.54), kind=kOutput, calls=%fused_computation.6 | convolution fusion | flops 17179869184 | bytes 33554432 | tf_op jit(solution)/shard_map/dot_general | solution.py:31
  1028.8 21.7 %fusion.9 = f32[1024,2048]{1,0:T(8,128)} fusion(bf16[4096,2048]{1,0:T(8,128)(2,1)} %bitcast.62, bf16[4096,2048]{1,0:T(8,128)(2,1)S(1)} %bitcast.58), kind=kOutput, calls=%fused_computation.12 | convolution fusion | flops 17179869184 | bytes 33554432 | tf_op jit(solution)/shard_map/dot_general | solution.py:31
  1058.5 21.9 %fusion.1 = f32[1024,2048]{1,0:T(8,128)} fusion(bf16[4096,2048]{1,0:T(8,128)(2,1)} %bitcast.63, bf16[4096,2048]{1,0:T(8,128)(2,1)S(1)} %bitcast.59), kind=kOutput, calls=%fused_computation.4 | convolution fusion | flops 17179869184 | bytes 33554432 | tf_op jit(solution)/shard_map/dot_general | solution.py:31
  1082.9 39.5 %collective-permute-done.8 = bf16[1,4,256,2048]{3,2,1,0:T(8,128)(2,1)} collective-permute-done((bf16[1,4,256,2048]{3,2,1,0:T(8,128)(2,1)}, bf16[1,4,256,2048]{3,2,1,0:T(8,128)(2,1)}, u32[]{:S(2)}, u32[]{:S(2)}) %collective-permute-start.8) | collective-permute-done | bytes 4194336 | tf_op jit(solution)/shard_map/ppermute | solution.py:350
  1127.3 84.0 %collective-permute-done.9 = bf16[1,4,256,2048]{3,2,1,0:T(8,128)(2,1)} collective-permute-done((bf16[1,4,256,2048]{3,2,1,0:T(8,128)(2,1)}, bf16[1,4,256,2048]{3,2,1,0:T(8,128)(2,1)}, u32[]{:S(2)}, u32[]{:S(2)}) %collective-permute-start.9) | collective-permute-done | bytes 4194336 | tf_op jit(solution)/shard_map/ppermute | solution.py:350
  1222.4 34.8 %collective-permute-done.19 = bf16[1,2,256,2048]{3,2,1,0:T(8,128)(2,1)} collective-permute-done((bf16[1,2,256,2048]{3,2,1,0:T(8,128)(2,1)}, bf16[1,2,256,2048]{3,2,1,0:T(8,128)(2,1)}, u32[]{:S(2)}, u32[]{:S(2)}) %collective-permute-start.19) | collective-permute-done | bytes 2097184 | tf_op jit(solution)/shard_map/ppermute | solution.py:350
  1257.4 43.8 %collective-permute-done.20 = bf16[1,2,256,2048]{3,2,1,0:T(8,128)(2,1)} collective-permute-done((bf16[1,2,256,2048]{3,2,1,0:T(8,128)(2,1)}, bf16[1,2,256,2048]{3,2,1,0:T(8,128)(2,1)}, u32[]{:S(2)}, u32[]{:S(2)}) %collective-permute-start.20) | collective-permute-done | bytes 2097184 | tf_op jit(solution)/shard_map/ppermute | solution.py:350
  1301.7 24.2 %fusion.7 = f32[1024,2048]{1,0:T(8,128)} fusion(bf16[4096,2048]{1,0:T(8,128)(2,1)} %bitcast.64, bf16[4096,2048]{1,0:T(8,128)(2,1)} %bitcast.55), kind=kOutput, calls=%fused_computation.10 | convolution fusion | flops 17179869184 | bytes 33554432 | tf_op jit(solution)/shard_map/dot_general | solution.py:31
  1334.5 57.5 %collective-permute-done.32 = f32[512,2048]{1,0:T(8,128)} collective-permute-done((f32[512,2048]{1,0:T(8,128)}, f32[512,2048]{1,0:T(8,128)}, u32[]{:S(2)}, u32[]{:S(2)}) %collective-permute-start.32) | collective-permute-done | bytes 4194336 | tf_op jit(solution)/shard_map/ppermute | solution.py:350
  1392.0 135.4 %collective-permute-done.26 = f32[3,2048]{1,0:T(4,128)S(1)} collective-permute-done((f32[3,2048]{1,0:T(4,128)S(1)}, f32[3,2048]{1,0:T(4,128)S(1)}, u32[]{:S(2)}, u32[]{:S(2)}) %collective-permute-start.26) | collective-permute-done | bytes 24608 | tf_op jit(solution)/shard_map/ppermute | solution.py:350
  1547.2 114.2 %collective-permute-done.23 = bf16[1,2,256,2048]{3,2,1,0:T(8,128)(2,1)} collective-permute-done((bf16[1,2,256,2048]{3,2,1,0:T(8,128)(2,1)}, bf16[1,2,256,2048]{3,2,1,0:T(8,128)(2,1)}, u32[]{:S(2)}, u32[]{:S(2)}) %collective-permute-start.23) | collective-permute-done | bytes 2097184 | tf_op jit(solution)/shard_map/ppermute | solution.py:350
  1682.1 69.7 %collective-permute-done.30 = f32[512,2048]{1,0:T(8,128)} collective-permute-done((f32[512,2048]{1,0:T(8,128)}, f32[512,2048]{1,0:T(8,128)}, u32[]{:S(2)}, u32[]{:S(2)}) %collective-permute-start.30) | collective-permute-done | bytes 4194336 | tf_op jit(solution)/shard_map/ppermute | solution.py:350
  (182 shorter events, 187.1 us)
Async XLA Ops:
  10.3 153.9 %collective-permute-start.7 = (bf16[4,256,2048]{2,1,0:T(8,128)(2,1)}, bf16[4,256,2048]{2,1,0:T(8,128)(2,1)}, u32[]{:S(2)}, u32[]{:S(2)}) collective-permute-start(bf16[4,256,2048]{2,1,0:T(8,128)(2,1)} %dynamic-slice_bitcast_fusion), channel_id=1, source_target_pairs={{0,1},{1,0},{2,3},{3,2},{4,5},{5,4},{6,7},{7,6}} | collective-permute-start | bytes 12582920 | tf_op jit(solution)/shard_map/ppermute | solution.py:350
  11.1 225.6 %collective-permute-start.5 = (bf16[2,256,2048]{2,1,0:T(8,128)(2,1)}, bf16[2,256,2048]{2,1,0:T(8,128)(2,1)}, u32[]{:S(2)}, u32[]{:S(2)}) collective-permute-start(bf16[2,256,2048]{2,1,0:T(8,128)(2,1)} %get-tuple-element.185), channel_id=1, source_target_pairs={{0,2},{1,3},{2,0},{3,1},{4,6},{5,7},{6,4},{7,5}} | collective-permute-start | bytes 6291464 | tf_op jit(solution)/shard_map/ppermute | solution.py:350
  13.6 224.5 %collective-permute-start.6 = (bf16[2,256,2048]{2,1,0:T(8,128)(2,1)}, bf16[2,256,2048]{2,1,0:T(8,128)(2,1)}, u32[]{:S(2)}, u32[]{:S(2)}) collective-permute-start(bf16[2,256,2048]{2,1,0:T(8,128)(2,1)} %get-tuple-element.184), channel_id=1, source_target_pairs={{0,3},{1,2},{2,1},{3,0},{4,7},{5,6},{6,5},{7,4}} | collective-permute-start | bytes 6291464 | tf_op jit(solution)/shard_map/ppermute | solution.py:350
  13.7 91.6 %collective-permute-start.2 = (s32[1,4,256]{2,1,0:T(4,128)S(1)}, s32[1,4,256]{2,1,0:T(4,128)S(1)}, u32[]{:S(2)}, u32[]{:S(2)}) collective-permute-start(s32[1,4,256]{2,1,0:T(4,128)S(1)} %get-tuple-element.90), channel_id=1, source_target_pairs={{0,2},{1,3},{2,0},{3,1},{4,6},{5,7},{6,4},{7,5}} | collective-permute-start | bytes 12296 | tf_op jit(solution)/shard_map/ppermute | solution.py:350
  20.3 312.0 %collective-permute-start = (bf16[2,256,2048]{2,1,0:T(8,128)(2,1)}, bf16[2,256,2048]{2,1,0:T(8,128)(2,1)}, u32[]{:S(2)}, u32[]{:S(2)}) collective-permute-start(bf16[2,256,2048]{2,1,0:T(8,128)(2,1)} %get-tuple-element.183), channel_id=1, source_target_pairs={{0,2},{1,3},{2,0},{3,1},{4,6},{5,7},{6,4},{7,5}} | collective-permute-start | bytes 6291464 | tf_op jit(solution)/shard_map/ppermute | solution.py:350
  105.3 44.7 %collective-permute-start.3 = (s32[1,4,256]{2,1,0:T(4,128)S(1)}, s32[1,4,256]{2,1,0:T(4,128)S(1)}, u32[]{:S(2)}, u32[]{:S(2)}) collective-permute-start(s32[1,4,256]{2,1,0:T(4,128)S(1)} %get-tuple-element.91), channel_id=1, source_target_pairs={{0,3},{1,2},{2,1},{3,0},{4,7},{5,6},{6,5},{7,4}} | collective-permute-start | bytes 12296 | tf_op jit(solution)/shard_map/ppermute | solution.py:350
  151.2 181.2 %collective-permute-start.1 = (bf16[2,256,2048]{2,1,0:T(8,128)(2,1)}, bf16[2,256,2048]{2,1,0:T(8,128)(2,1)}, u32[]{:S(2)}, u32[]{:S(2)}) collective-permute-start(bf16[2,256,2048]{2,1,0:T(8,128)(2,1)} %get-tuple-element.182), channel_id=1, source_target_pairs={{0,3},{1,2},{2,1},{3,0},{4,7},{5,6},{6,5},{7,4}} | collective-permute-start | bytes 6291464 | tf_op jit(solution)/shard_map/ppermute | solution.py:350
  164.2 313.4 %collective-permute-start.12 = (bf16[1,2,256,2048]{3,2,1,0:T(8,128)(2,1)}, bf16[1,2,256,2048]{3,2,1,0:T(8,128)(2,1)}, u32[]{:S(2)}, u32[]{:S(2)}) collective-permute-start(bf16[1,2,256,2048]{3,2,1,0:T(8,128)(2,1)} %get-tuple-element.174), channel_id=1, source_target_pairs={{0,2},{1,3},{2,0},{3,1},{4,6},{5,7},{6,4},{7,5}} | collective-permute-start | bytes 6291464 | tf_op jit(solution)/shard_map/ppermute | solution.py:350
  236.7 242.8 %collective-permute-start.13 = (bf16[1,2,256,2048]{3,2,1,0:T(8,128)(2,1)}, bf16[1,2,256,2048]{3,2,1,0:T(8,128)(2,1)}, u32[]{:S(2)}, u32[]{:S(2)}) collective-permute-start(bf16[1,2,256,2048]{3,2,1,0:T(8,128)(2,1)} %get-tuple-element.173), channel_id=1, source_target_pairs={{0,3},{1,2},{2,1},{3,0},{4,7},{5,6},{6,5},{7,4}} | collective-permute-start | bytes 6291464 | tf_op jit(solution)/shard_map/ppermute | solution.py:350
  238.1 241.4 %collective-permute-start.14 = (bf16[1,2,256,2048]{3,2,1,0:T(8,128)(2,1)}, bf16[1,2,256,2048]{3,2,1,0:T(8,128)(2,1)}, u32[]{:S(2)}, u32[]{:S(2)}) collective-permute-start(bf16[1,2,256,2048]{3,2,1,0:T(8,128)(2,1)} %get-tuple-element.172), channel_id=1, source_target_pairs={{0,1},{1,0},{2,3},{3,2},{4,5},{5,4},{6,7},{7,6}} | collective-permute-start | bytes 6291464 | tf_op jit(solution)/shard_map/ppermute | solution.py:350
  332.3 349.8 %collective-permute-start.16 = (bf16[1,2,256,2048]{3,2,1,0:T(8,128)(2,1)}, bf16[1,2,256,2048]{3,2,1,0:T(8,128)(2,1)}, u32[]{:S(2)}, u32[]{:S(2)}) collective-permute-start(bf16[1,2,256,2048]{3,2,1,0:T(8,128)(2,1)} %get-tuple-element.170), channel_id=1, source_target_pairs={{0,1},{1,0},{2,3},{3,2},{4,5},{5,4},{6,7},{7,6}} | collective-permute-start | bytes 6291464 | tf_op jit(solution)/shard_map/ppermute | solution.py:350
  332.3 349.8 %collective-permute-start.15 = (bf16[1,2,256,2048]{3,2,1,0:T(8,128)(2,1)}, bf16[1,2,256,2048]{3,2,1,0:T(8,128)(2,1)}, u32[]{:S(2)}, u32[]{:S(2)}) collective-permute-start(bf16[1,2,256,2048]{3,2,1,0:T(8,128)(2,1)} %get-tuple-element.171), channel_id=1, source_target_pairs={{0,3},{1,2},{2,1},{3,0},{4,7},{5,6},{6,5},{7,4}} | collective-permute-start | bytes 6291464 | tf_op jit(solution)/shard_map/ppermute | solution.py:350
  477.6 204.5 %collective-permute-start.11 = (bf16[1,2,256,2048]{3,2,1,0:T(8,128)(2,1)}, bf16[1,2,256,2048]{3,2,1,0:T(8,128)(2,1)}, u32[]{:S(2)}, u32[]{:S(2)}) collective-permute-start(bf16[1,2,256,2048]{3,2,1,0:T(8,128)(2,1)} %get-tuple-element.175), channel_id=1, source_target_pairs={{0,2},{1,3},{2,0},{3,1},{4,6},{5,7},{6,4},{7,5}} | collective-permute-start | bytes 6291464 | tf_op jit(solution)/shard_map/ppermute | solution.py:350
  719.6 54.9 %collective-permute-start.17 = (f32[1024,2048]{1,0:T(8,128)}, f32[1024,2048]{1,0:T(8,128)S(1)}, u32[]{:S(2)}, u32[]{:S(2)}) collective-permute-start(f32[1024,2048]{1,0:T(8,128)} %fusion.28), channel_id=1, source_target_pairs={{0,1},{1,0},{2,3},{3,2},{4,5},{5,4},{6,7},{7,6}} | collective-permute-start | bytes 25165832 | tf_op jit(solution)/shard_map/ppermute | solution.py:350
  884.4 21.5 %collective-permute-start.18 = (f32[1024,2048]{1,0:T(8,128)}, f32[1024,2048]{1,0:T(8,128)S(1)}, u32[]{:S(2)}, u32[]{:S(2)}) collective-permute-start(f32[1024,2048]{1,0:T(8,128)} %fusion.5), channel_id=1, source_target_pairs={{0,1},{1,0},{2,3},{3,2},{4,5},{5,4},{6,7},{7,6}} | collective-permute-start | bytes 25165832 | tf_op jit(solution)/shard_map/ppermute | solution.py:350
  1028.6 21.9 %collective-permute-start.27 = (f32[1024,2048]{1,0:T(8,128)}, f32[1024,2048]{1,0:T(8,128)S(1)}, u32[]{:S(2)}, u32[]{:S(2)}) collective-permute-start(f32[1024,2048]{1,0:T(8,128)} %fusion.3), channel_id=1, source_target_pairs={{0,1},{1,0},{2,3},{3,2},{4,5},{5,4},{6,7},{7,6}} | collective-permute-start | bytes 25165832 | tf_op jit(solution)/shard_map/ppermute | solution.py:350
  1028.6 93.8 %collective-permute-start.8 = (bf16[1,4,256,2048]{3,2,1,0:T(8,128)(2,1)}, bf16[1,4,256,2048]{3,2,1,0:T(8,128)(2,1)}, u32[]{:S(2)}, u32[]{:S(2)}) collective-permute-start(bf16[1,4,256,2048]{3,2,1,0:T(8,128)(2,1)} %get-tuple-element.117), channel_id=1, source_target_pairs={{0,2},{1,3},{2,0},{3,1},{4,6},{5,7},{6,4},{7,5}} | collective-permute-start | bytes 12582920 | tf_op jit(solution)/shard_map/ppermute | solution.py:350
  1080.4 247.0 %collective-permute-start.29 = (f32[1024,2048]{1,0:T(8,128)}, f32[1024,2048]{1,0:T(8,128)}, u32[]{:S(2)}, u32[]{:S(2)}) collective-permute-start(f32[1024,2048]{1,0:T(8,128)} %fusion.1), channel_id=1, source_target_pairs={{0,1},{1,0},{2,3},{3,2},{4,5},{5,4},{6,7},{7,6}} | collective-permute-start | bytes 25165832 | tf_op jit(solution)/shard_map/ppermute | solution.py:350
  1080.8 130.5 %collective-permute-start.9 = (bf16[1,4,256,2048]{3,2,1,0:T(8,128)(2,1)}, bf16[1,4,256,2048]{3,2,1,0:T(8,128)(2,1)}, u32[]{:S(2)}, u32[]{:S(2)}) collective-permute-start(bf16[1,4,256,2048]{3,2,1,0:T(8,128)(2,1)} %get-tuple-element.118), channel_id=1, source_target_pairs={{0,3},{1,2},{2,1},{3,0},{4,7},{5,6},{6,5},{7,4}} | collective-permute-start | bytes 12582920 | tf_op jit(solution)/shard_map/ppermute | solution.py:350
  1082.4 134.3 %collective-permute-start.10 = (bf16[1,4,256,2048]{3,2,1,0:T(8,128)(2,1)}, bf16[1,4,256,2048]{3,2,1,0:T(8,128)(2,1)}, u32[]{:S(2)}, u32[]{:S(2)}) collective-permute-start(bf16[1,4,256,2048]{3,2,1,0:T(8,128)(2,1)} %get-tuple-element.119), channel_id=1, source_target_pairs={{0,1},{1,0},{2,3},{3,2},{4,5},{5,4},{6,7},{7,6}} | collective-permute-start | bytes 12582920 | tf_op jit(solution)/shard_map/ppermute | solution.py:350
  1082.6 174.6 %collective-permute-start.19 = (bf16[1,2,256,2048]{3,2,1,0:T(8,128)(2,1)}, bf16[1,2,256,2048]{3,2,1,0:T(8,128)(2,1)}, u32[]{:S(2)}, u32[]{:S(2)}) collective-permute-start(bf16[1,2,256,2048]{3,2,1,0:T(8,128)(2,1)} %get-tuple-element.135), channel_id=1, source_target_pairs={{0,2},{1,3},{2,0},{3,1},{4,6},{5,7},{6,4},{7,5}} | collective-permute-start | bytes 6291464 | tf_op jit(solution)/shard_map/ppermute | solution.py:350
  1122.4 178.8 %collective-permute-start.20 = (bf16[1,2,256,2048]{3,2,1,0:T(8,128)(2,1)}, bf16[1,2,256,2048]{3,2,1,0:T(8,128)(2,1)}, u32[]{:S(2)}, u32[]{:S(2)}) collective-permute-start(bf16[1,2,256,2048]{3,2,1,0:T(8,128)(2,1)} %get-tuple-element.152), channel_id=1, source_target_pairs={{0,3},{1,2},{2,1},{3,0},{4,7},{5,6},{6,5},{7,4}} | collective-permute-start | bytes 6291464 | tf_op jit(solution)/shard_map/ppermute | solution.py:350
  1216.1 176.0 %collective-permute-start.32 = (f32[512,2048]{1,0:T(8,128)}, f32[512,2048]{1,0:T(8,128)}, u32[]{:S(2)}, u32[]{:S(2)}) collective-permute-start(f32[512,2048]{1,0:T(8,128)} %slice_add_fusion.7), channel_id=1, source_target_pairs={{0,2},{1,3},{2,0},{3,1},{4,6},{5,7},{6,4},{7,5}} | collective-permute-start | bytes 12582920 | tf_op jit(solution)/shard_map/ppermute | solution.py:350
  1216.7 5.4 collective-permute-start.25
  1222.1 103.8 %collective-permute-start.21 = (bf16[1,2,256,2048]{3,2,1,0:T(8,128)(2,1)S(1)}, bf16[1,2,256,2048]{3,2,1,0:T(8,128)(2,1)}, u32[]{:S(2)}, u32[]{:S(2)}) collective-permute-start(bf16[1,2,256,2048]{3,2,1,0:T(8,128)(2,1)S(1)} %copy-done.9), channel_id=1, source_target_pairs={{0,1},{1,0},{2,3},{3,2},{4,5},{5,4},{6,7},{7,6}} | collective-permute-start | bytes 6291464 | tf_op jit(solution)/shard_map/ppermute | solution.py:350
  1257.2 410.5 %collective-permute-start.31 = (f32[512,2048]{1,0:T(8,128)S(1)}, f32[512,2048]{1,0:T(8,128)}, u32[]{:S(2)}, u32[]{:S(2)}) collective-permute-start(f32[512,2048]{1,0:T(8,128)S(1)} %copy-done.8), channel_id=1, source_target_pairs={{0,2},{1,3},{2,0},{3,1},{4,6},{5,7},{6,4},{7,5}} | collective-permute-start | bytes 12582920 | tf_op jit(solution)/shard_map/ppermute | solution.py:350
  1301.2 226.3 %collective-permute-start.22 = (bf16[1,2,256,2048]{3,2,1,0:T(8,128)(2,1)}, bf16[1,2,256,2048]{3,2,1,0:T(8,128)(2,1)}, u32[]{:S(2)}, u32[]{:S(2)}) collective-permute-start(bf16[1,2,256,2048]{3,2,1,0:T(8,128)(2,1)} %get-tuple-element.154), channel_id=1, source_target_pairs={{0,2},{1,3},{2,0},{3,1},{4,6},{5,7},{6,4},{7,5}} | collective-permute-start | bytes 6291464 | tf_op jit(solution)/shard_map/ppermute | solution.py:350
  1325.9 201.6 %collective-permute-start.26 = (f32[3,2048]{1,0:T(4,128)S(1)}, f32[3,2048]{1,0:T(4,128)S(1)}, u32[]{:S(2)}, u32[]{:S(2)}) collective-permute-start(f32[3,2048]{1,0:T(4,128)S(1)} %fusion.50), channel_id=1, source_target_pairs={{0,2},{1,3},{2,0},{3,1},{4,6},{5,7},{6,4},{7,5}} | collective-permute-start | bytes 73736 | tf_op jit(solution)/shard_map/ppermute | solution.py:350
  1327.4 346.2 %collective-permute-start.28 = (f32[512,2048]{1,0:T(8,128)}, f32[512,2048]{1,0:T(8,128)}, u32[]{:S(2)}, u32[]{:S(2)}) collective-permute-start(f32[512,2048]{1,0:T(8,128)} %slice_add_fusion.4), channel_id=1, source_target_pairs={{0,2},{1,3},{2,0},{3,1},{4,6},{5,7},{6,4},{7,5}} | collective-permute-start | bytes 12582920 | tf_op jit(solution)/shard_map/ppermute | solution.py:350
  1392.0 269.4 %collective-permute-start.23 = (bf16[1,2,256,2048]{3,2,1,0:T(8,128)(2,1)}, bf16[1,2,256,2048]{3,2,1,0:T(8,128)(2,1)}, u32[]{:S(2)}, u32[]{:S(2)}) collective-permute-start(bf16[1,2,256,2048]{3,2,1,0:T(8,128)(2,1)} %get-tuple-element.155), channel_id=1, source_target_pairs={{0,3},{1,2},{2,1},{3,0},{4,7},{5,6},{6,5},{7,4}} | collective-permute-start | bytes 6291464 | tf_op jit(solution)/shard_map/ppermute | solution.py:350
  1527.5 137.1 %collective-permute-start.24 = (bf16[1,2,256,2048]{3,2,1,0:T(8,128)(2,1)}, bf16[1,2,256,2048]{3,2,1,0:T(8,128)(2,1)}, u32[]{:S(2)}, u32[]{:S(2)}) collective-permute-start(bf16[1,2,256,2048]{3,2,1,0:T(8,128)(2,1)} %get-tuple-element.156), channel_id=1, source_target_pairs={{0,1},{1,0},{2,3},{3,2},{4,5},{5,4},{6,7},{7,6}} | collective-permute-start | bytes 6291464 | tf_op jit(solution)/shard_map/ppermute | solution.py:350
  1527.5 224.3 %collective-permute-start.30 = (f32[512,2048]{1,0:T(8,128)}, f32[512,2048]{1,0:T(8,128)}, u32[]{:S(2)}, u32[]{:S(2)}) collective-permute-start(f32[512,2048]{1,0:T(8,128)} %slice_add_fusion.2), channel_id=1, source_target_pairs={{0,2},{1,3},{2,0},{3,1},{4,6},{5,7},{6,4},{7,5}} | collective-permute-start | bytes 12582920 | tf_op jit(solution)/shard_map/ppermute | solution.py:350
  (37 other events, 3016.5 us)

commit v3 on v2

--- a/solution.py
+++ b/solution.py
@@ -379,7 +379,8 @@
                 terms = [dot_tn(flat(r)[:, cols], flat(g)) for r, g in zip(rels, rights)]
                 return sum(terms[1:], terms[0])
 
-            out = to_peer(part(slice(0, half)), 1)
+            out = part(slice(0, half))
+            out = to_peer(out, 1)
             keep = part(slice(half, None))
             far = keep[:half // 2] + out[:half // 2]
             got = to_peer(far, 2)
@@ -391,13 +392,13 @@
             pos4 = lax.dynamic_update_slice_in_dim(pos4, got, me ^ bits, axis=0)
         x4 = x_loc.reshape(shape4)
         x_parts = []
+        x_near = piece(x4, 1, 0, n_seq)[0]
+        x4 = after(x4, x_near)
         for c in range(N_CHUNK):
             x_parts.append([piece(x4, bits, c * step, step)[0] for bits in (2, 3)])
             x4 = after(x4, *x_parts[-1])
-            if c == 0:
-                x_near = piece(x4, 1, 0, n_seq)[0]
         x_far = [[to_peer(p, bits) for p, bits in zip(x_parts[c], (2, 3))] for c in range(N_CHUNK)]
-        dy4 = after(grad_y.reshape(shape4), x_near, *x_parts[1])
+        dy4 = after(grad_y.reshape(shape4), *x_parts[1])
         x_near = to_peer(x_near, 1)
         dy_got = [send([piece(dy4, bits, c * step, step) for bits in far_bits]) for c in range(N_CHUNK)]
         cos_t, sin_t = rope_tables(pos4)
@@ -419,8 +420,7 @@
         y, y_parts = pieces(y, 0, n_seq)
         y_got = send(y_parts)
         prev = y_parts[0]
-        dv, tails, gx_got = (), (), []
-        gains = 0.0
+        dv, tails, gx_got, dqk = (), (), [], []
         for c in range(N_CHUNK):
             dy = dys[c]
             for bits, got in zip(far_bits, dy_got[c]):
@@ -430,24 +430,27 @@
                 w_o, prev = grad_rows(rels, dys)
             d_attn = dot_nt(flat(dy), w_out).astype(BF16).reshape(dy.shape)
             dq, dk, *dv = attend_back(q, k, v, d_attn, after(lse, prev), c * step, step, tuple(dv))
+            dqk.append((dq, dk))
             prev = dq
+        w_v, prev = grad_rows([h_rel], dv)
+        gains = 0.0
+        for c in range(N_CHUNK):
+            *tails, ggn, ggq, ggk = tail(*dqk[c], dv[0], q1, k1, x_all, dys[c], after(cos_t, prev), sin_t, *gains_in, *weights, c * step, step, tuple(tails))
+            gains = gains + jnp.concatenate([ggn, ggq, ggk], axis=0)
+            tails[2], gx_parts = pieces(tails[2], c * step, step)
             if c == N_CHUNK - 1:
-                w_v, prev = grad_rows([h_rel], dv)
-            *tails, ggn, ggq, ggk = tail(dq, dk, dv[0], q1, k1, x_all, dy, after(cos_t, prev), sin_t, *gains_in, *weights, c * step, step, tuple(tails))
-            tails[2], gx_parts = pieces(tails[2], c * step, step)
+                gains = gains + to_peer(gains, 2)
             gx_got.append(send(gx_parts))
             prev = gx_parts[0]
-            gains = gains + jnp.concatenate([ggn, ggq, ggk], axis=0)
         dqr, dkr, gx = tails
         w_q, prev = grad_rows([h_rel], [after(dqr, prev)])
         w_k, prev = grad_rows([h_rel], [after(dkr, prev)])
         for bits, got in zip(far_bits, y_got):
-            y = put(y, got, bits, 0)
+            y = put(y, after(got, prev), bits, 0)
         for c in range(N_CHUNK):
             for bits, got in zip(far_bits, gx_got[c]):
                 gx = put(gx, got, bits, c * step)
         gains = gains + to_peer(gains, 1)
-        gains = gains + to_peer(gains, 2)
         gains = lax.dynamic_slice_in_dim(gains, me * (d_model // n_sp), d_model // n_sp, axis=1)
         total = lambda terms: terms[0] + terms[1] + terms[2]
         join = lambda arr: arr.reshape(x_loc.shape)

time: 1760 us -> 1830 us (1.040)
  waiting for transfers between devices: 697 us -> 758 us
    ppermute x33, waiting for transfers between devices: 697 us -> 758 us  [to_peer(): return lax.ppermute(value, 'sp', [(i, i ^ bits) for i in range(n_sp)])]
  transfers between devices with their start and end apart: 33 -> 33, of which waited for: 11 -> 9; matrix products, arithmetic and copies ran while one was open for 19% -> 16% of each run, Pallas kernels for 24% -> 19%
where the time goes in v3:
time: 1830 us; the launch traced here: 1820 us
  waiting for transfers between devices  758 us (41%)
  Pallas kernels  586 us (32%)
  matrix products  285 us (16%)
  local copies, waits for them, and re-layouts  95.1 us (5%)
  other arithmetic  69.1 us (4%)
  starting transfers between devices  26.9 us (1%)
    ppermute x33, waiting for transfers between devices, to_peer(): return lax.ppermute(value, 'sp', [(i, i ^ bits) for i in range(n_sp)])  758 us
    dot_general x10, matrix products, dot_tn(): lax.dot_general(a, b, (((0,), (0,)), ((), ())), preferred_element_type=F32)  193 us
    pallas_call x2, Pallas kernels, tail(): pl.pallas_call(tail_kernel, grid=(n_piece, n_seq), in_specs=[loc] * 2 + [...  168 us
    pallas_call x2, Pallas kernels, attend_back(): pl.pallas_call(attend_back_kernel, grid=(n_seq, n_heads // heads), in_spe...  159 us
    pallas_call x3, Pallas kernels, front(): pl.pallas_call(front_own_kernel if own else front_kernel, grid_spec=pltpu...  154 us
    pallas_call x2, Pallas kernels, attend(): pl.pallas_call(attend_kernel, grid_spec=pltpu.PrefetchScalarGridSpec(num_...  105 us
    dot_general x2, matrix products, dot_nt(): lax.dot_general(a, b, (((1,), (1,)), ((), ())), preferred_element_type=F32)  50.5 us
    dynamic_update_slice x15, local copies, waits for them, and re-layouts, put(): return lax.dynamic_update_slice(buf, got, (me ^ bits, seq0, 0, 0))  46.8 us
  transfers between devices with their start and end apart: 33, of which 9 were waited for; matrix products, arithmetic and copies ran while one was open for 16% of the time, Pallas kernels for 19%

profile of v3, /device:TPU:0, one launch (start us, length us, event | category | flops | bytes accessed | tf_op | source)
XLA Modules:
  0.0 1821.9 jit_solution(10320364310379175774)
XLA Ops:
  29.1 122.5 %collective-permute-done.3 = s32[1,4,256]{2,1,0:T(4,128)S(1)} collective-permute-done((s32[1,4,256]{2,1,0:T(4,128)S(1)}, s32[1,4,256]{2,1,0:T(4,128)S(1)}, u32[]{:S(2)}, u32[]{:S(2)}) %collective-permute-start.3) | collective-permute-done | bytes 4128 | tf_op jit(solution)/shard_map/ppermute | solution.py:350
  165.1 72.3 %front.3 = (bf16[4,4,256,2048]{3,2,1,0:T(8,128)(2,1)}, bf16[4,4,256,2048]{3,2,1,0:T(8,128)(2,1)}, bf16[4,4,256,2048]{3,2,1,0:T(8,128)(2,1)}, bf16[4,4,256,2048]{...) custom-call(s32[1]{0:T(128)} %bitcast.refs_0_.me_ref, ...), custom_call_target="tpu_custom_call" | custom-call | flops 51539607552 | bytes 109051904 | tf_op jit(solution)/shard_map/front/pallas_call | solution.py:123
  239.5 40.9 %front.4 = (bf16[4,4,256,2048]{3,2,1,0:T(8,128)(2,1)}, bf16[4,4,256,2048]{3,2,1,0:T(8,128)(2,1)}, bf16[4,4,256,2048]{3,2,1,0:T(8,128)(2,1)}, bf16[4,4,256,2048]{...) custom-call(s32[1]{0:T(128)} %bitcast.refs_0_.me_ref, ...), custom_call_target="tpu_custom_call", output_to_operand_aliasing={{0}: (11, {}), {1}: (12, {}), {2}: (13, {}), {3}: (14, {}),... | custom-call | flops 25769803776 | bytes 67108864 | tf_op jit(solution)/shard_map/front/pallas_call | solution.py:123
  280.4 52.7 %attend.2 = (bf16[4,2,256,2048]{3,2,1,0:T(8,128)(2,1)}, bf16[4,4,256,2048]{3,2,1,0:T(8,128)(2,1)}, f32[4,16,1,1024]{3,2,1,0:T(1,128)}) custom-call(s32[1]{0:T(128)} %bitcast.refs_0_.me_ref, bf16[4,4,256,2048]{3,2,1,0:T(8,128)(2,1)} %get-tuple-element.106.q_ref.refs_2_, bf16[4,4,256,2048]{3,2,1,0:T(8,128)(2,1)} %get-tuple-element.107.k_ref.refs_3_, ...), custom_call_target="tpu_custom_call" | custom-call | flops 25769803776 | bytes 41943040 | tf_op jit(solution)/shard_map/attend/pallas_call | solution.py:177
  334.9 41.1 %front.5 = (bf16[4,4,256,2048]{3,2,1,0:T(8,128)(2,1)}, bf16[4,4,256,2048]{3,2,1,0:T(8,128)(2,1)}, bf16[4,4,256,2048]{3,2,1,0:T(8,128)(2,1)}, bf16[4,4,256,2048]{...) custom-call(s32[1]{0:T(128)} %bitcast.refs_0_.me_ref, ...), custom_call_target="tpu_custom_call", output_to_operand_aliasing={{0}: (11, {}), {1}: (12, {}), {2}: (13, {}), {3}: (14, {}),... | custom-call | flops 25769803776 | bytes 67108864 | tf_op jit(solution)/shard_map/front/pallas_call | solution.py:123
  376.0 52.6 %attend.3 = (bf16[4,2,256,2048]{3,2,1,0:T(8,128)(2,1)}, bf16[4,4,256,2048]{3,2,1,0:T(8,128)(2,1)}, f32[4,16,1,1024]{3,2,1,0:T(1,128)}) custom-call(s32[1]{0:T(128)} %bitcast.refs_0_.me_ref, bf16[4,4,256,2048]{3,2,1,0:T(8,128)(2,1)} %get-tuple-element.116.q_ref, ...), custom_call_target="tpu_custom_call", output_to_operand_aliasing={{1}: (4, {}), {2}: (5, {})} | custom-call | flops 25769803776 | bytes 41943040 | tf_op jit(solution)/shard_map/attend/pallas_call | solution.py:177
  428.7 41.3 %fusion = bf16[4096,2048]{1,0:T(8,128)(2,1)S(1)} fusion(bf16[4,4,256,2048]{3,2,1,0:T(8,128)(2,1)} %get-tuple-element.115.x_ref, bf16[4096,2048]{1,0:T(8,128)(2,1)} %bitcast.104, bf16[2048,2048]{1,0:T(8,128)(2,1)} %param.17), kind=kOutput, calls=%fused_computation.1 | convolution fusion | flops 34384904192 | bytes 58720256 | tf_op jit(solution)/shard_map/dot_general | solution.py:23
  489.6 23.8 %convolution_convert_fusion.1 = bf16[2048,2048]{1,0:T(8,128)(2,1)} fusion(bf16[2048,2048]{1,0:T(8,128)(2,1)} %bitcast.99, bf16[2048,2048]{1,0:T(8,128)(2,1)} %param.17), kind=kOutput, calls=%fused_computation.3 | convolution fusion | flops 17184063488 | bytes 25165824 | tf_op jit(solution)/shard_map/dot_general | solution.py:27
  513.3 79.4 %attend_back.2 = (bf16[4,2,256,2048]{3,2,1,0:T(8,128)(2,1)}, bf16[4,2,256,2048]{3,2,1,0:T(8,128)(2,1)}, bf16[4,4,256,2048]{3,2,1,0:T(8,128)(2,1)}) custom-call(bf16[4,4,256,2048]{3,2,1,0:T(8,128)(2,1)} %get-tuple-element.116.q_ref, bf16[4,4,256,2048]{3,2,1,0:T(8,128)(2,1)} %get-tuple-element.117.k_ref, bf16[4,4,256,2048]{3,2,1,0:T(8,128)(2,1)} %get-tuple-element.118.v_ref, ...), custom_call_target="tpu_custom_call" | custom-call | flops 60129542144 | bytes 58720256 | tf_op jit(solution)/shard_map/attend_back/pallas_call | solution.py:241
  602.4 14.8 fusion.17
  617.2 15.1 fusion.28
  632.3 13.2 fusion.21
  645.5 14.6 fusion.25
  660.2 26.7 %convolution_convert_fusion = bf16[2048,2048]{1,0:T(8,128)(2,1)} fusion(bf16[2048,2048]{1,0:T(8,128)(2,1)} %bitcast.79, bf16[2048,2048]{1,0:T(8,128)(2,1)} %param.17), kind=kOutput, calls=%fused_computation.2 | convolution fusion | flops 17184063488 | bytes 25165824 | tf_op jit(solution)/shard_map/dot_general | solution.py:27
  693.0 79.6 %attend_back.3 = (bf16[4,2,256,2048]{3,2,1,0:T(8,128)(2,1)}, bf16[4,2,256,2048]{3,2,1,0:T(8,128)(2,1)}, bf16[4,4,256,2048]{3,2,1,0:T(8,128)(2,1)}) custom-call(bf16[4,4,256,2048]{3,2,1,0:T(8,128)(2,1)} %get-tuple-element.116.q_ref, bf16[4,4,256,2048]{3,2,1,0:T(8,128)(2,1)} %get-tuple-element.117.k_ref, ...), custom_call_target="tpu_custom_call", output_to_operand_aliasing={{2}: (5, {})} | custom-call | flops 60129542144 | bytes 58720256 | tf_op jit(solution)/shard_map/attend_back/pallas_call | solution.py:241
  772.6 24.3 %fusion.5 = f32[1024,2048]{1,0:T(8,128)} fusion(bf16[4096,2048]{1,0:T(8,128)(2,1)} %bitcast.61, bf16[4096,2048]{1,0:T(8,128)(2,1)} %bitcast.52), kind=kOutput, calls=%fused_computation.8 | convolution fusion | flops 17179869184 | bytes 33554432 | tf_op jit(solution)/shard_map/dot_general | solution.py:31
  797.3 21.4 %fusion.11 = f32[1024,2048]{1,0:T(8,128)} fusion(bf16[4096,2048]{1,0:T(8,128)(2,1)S(1)} %bitcast.62, bf16[4096,2048]{1,0:T(8,128)(2,1)} %bitcast.53), kind=kOutput, calls=%fused_computation.14 | convolution fusion | flops 17179869184 | bytes 33554432 | tf_op jit(solution)/shard_map/dot_general | solution.py:31
  827.0 83.7 %tail.2 = (bf16[4,4,256,2048]{3,2,1,0:T(8,128)(2,1)}, bf16[4,4,256,2048]{3,2,1,0:T(8,128)(2,1)}, bf16[4,4,256,2048]{3,2,1,0:T(8,128)(2,1)}, f32[1,2048]{1,0:T(1,...) custom-call(bf16[4,2,256,2048]{3,2,1,0:T(8,128)(2,1)} %get-tuple-element.132.dq_ref, ...), custom_call_target="tpu_custom_call" | custom-call | flops 51539607552 | bytes 125829120 | tf_op jit(solution)/shard_map/tail/pallas_call | solution.py:319
  916.3 83.8 %tail.3 = (bf16[4,4,256,2048]{3,2,1,0:T(8,128)(2,1)}, bf16[4,4,256,2048]{3,2,1,0:T(8,128)(2,1)}, bf16[4,4,256,2048]{3,2,1,0:T(8,128)(2,1)}, f32[1,2048]{1,0:T(1,...) custom-call(bf16[4,2,256,2048]{3,2,1,0:T(8,128)(2,1)} %get-tuple-elemen, ...), custom_call_target="tpu_custom_call", output_to_operand_aliasing={{0}: (15, {}), {1}: (16, {}), {2}: (17, {})} | custom-call | flops 51539607552 | bytes 125829120 | tf_op jit(solution)/shard_map/tail/pallas_call | solution.py:319
  1006.1 24.5 %fusion.3 = f32[1024,2048]{1,0:T(8,128)} fusion(bf16[4096,2048]{1,0:T(8,128)(2,1)} %bitcast.63, bf16[4096,2048]{1,0:T(8,128)(2,1)} %bitcast.54), kind=kOutput, calls=%fused_computation.6 | convolution fusion | flops 17179869184 | bytes 33554432 | tf_op jit(solution)/shard_map/dot_general | solution.py:31
  1030.6 21.7 %fusion.9 = f32[1024,2048]{1,0:T(8,128)} fusion(bf16[4096,2048]{1,0:T(8,128)(2,1)} %bitcast.64, bf16[4096,2048]{1,0:T(8,128)(2,1)S(1)} %bitcast.58), kind=kOutput, calls=%fused_computation.12 | convolution fusion | flops 17179869184 | bytes 33554432 | tf_op jit(solution)/shard_map/dot_general | solution.py:31
  1060.3 22.0 %fusion.1 = f32[1024,2048]{1,0:T(8,128)} fusion(bf16[4096,2048]{1,0:T(8,128)(2,1)} %bitcast.65, bf16[4096,2048]{1,0:T(8,128)(2,1)S(1)} %bitcast.59), kind=kOutput, calls=%fused_computation.4 | convolution fusion | flops 17179869184 | bytes 33554432 | tf_op jit(solution)/shard_map/dot_general | solution.py:31
  1086.6 179.6 %collective-permute-done.27 = f32[3,2048]{1,0:T(4,128)S(1)} collective-permute-done((f32[3,2048]{1,0:T(4,128)S(1)}, f32[3,2048]{1,0:T(4,128)S(1)}, u32[]{:S(2)}, u32[]{:S(2)}) %collective-permute-start.27) | collective-permute-done | bytes 24608 | tf_op jit(solution)/shard_map/ppermute | solution.py:350
  1274.4 8.4 fusion.13
  1283.4 36.1 %collective-permute-done.24 = bf16[1,2,256,2048]{3,2,1,0:T(8,128)(2,1)} collective-permute-done((bf16[1,2,256,2048]{3,2,1,0:T(8,128)(2,1)}, bf16[1,2,256,2048]{3,2,1,0:T(8,128)(2,1)}, u32[]{:S(2)}, u32[]{:S(2)}) %collective-permute-start.24) | collective-permute-done | bytes 2097184 | tf_op jit(solution)/shard_map/ppermute | solution.py:350
  1321.1 42.5 %collective-permute-done.25 = bf16[1,2,256,2048]{3,2,1,0:T(8,128)(2,1)} collective-permute-done((bf16[1,2,256,2048]{3,2,1,0:T(8,128)(2,1)}, bf16[1,2,256,2048]{3,2,1,0:T(8,128)(2,1)}, u32[]{:S(2)}, u32[]{:S(2)}) %collective-permute-start.25) | collective-permute-done | bytes 2097184 | tf_op jit(solution)/shard_map/ppermute | solution.py:350
  1365.9 21.6 %fusion.7 = f32[1024,2048]{1,0:T(8,128)S(1)} fusion(bf16[4096,2048]{1,0:T(8,128)(2,1)} %bitcast.66, bf16[4096,2048]{1,0:T(8,128)(2,1)} %bitcast.55), kind=kOutput, calls=%fused_computation.10 | convolution fusion | flops 17179869184 | bytes 33554432 | tf_op jit(solution)/shard_map/dot_general | solution.py:31
  1395.5 58.7 %collective-permute-done.31 = f32[512,2048]{1,0:T(8,128)S(1)} collective-permute-done((f32[512,2048]{1,0:T(8,128)}, f32[512,2048]{1,0:T(8,128)S(1)}, u32[]{:S(2)}, u32[]{:S(2)}) %collective-permute-start.31) | collective-permute-done | bytes 4194336 | tf_op jit(solution)/shard_map/ppermute | solution.py:350
  1482.0 241.9 %collective-permute-done.29 = f32[512,2048]{1,0:T(8,128)} collective-permute-done((f32[512,2048]{1,0:T(8,128)S(1)}, f32[512,2048]{1,0:T(8,128)}, u32[]{:S(2)}, u32[]{:S(2)}) %collective-permute-start.29) | collective-permute-done | bytes 4194336 | tf_op jit(solution)/shard_map/ppermute | solution.py:350
  1723.9 8.4 fusion.16
  1740.8 72.2 %collective-permute-done.30 = f32[512,2048]{1,0:T(8,128)} collective-permute-done((f32[512,2048]{1,0:T(8,128)}, f32[512,2048]{1,0:T(8,128)}, u32[]{:S(2)}, u32[]{:S(2)}) %collective-permute-start.30) | collective-permute-done | bytes 4194336 | tf_op jit(solution)/shard_map/ppermute | solution.py:350
  1813.0 8.4 fusion.15
  (175 shorter events, 170.6 us)
Async XLA Ops:
  5.5 159.5 %collective-permute-start.7 = (bf16[4,256,2048]{2,1,0:T(8,128)(2,1)}, bf16[4,256,2048]{2,1,0:T(8,128)(2,1)}, u32[]{:S(2)}, u32[]{:S(2)}) collective-permute-start(bf16[4,256,2048]{2,1,0:T(8,128)(2,1)} %dynamic-slice_bitcast_fusion), channel_id=1, source_target_pairs={{0,1},{1,0},{2,3},{3,2},{4,5},{5,4},{6,7},{7,6}} | collective-permute-start | bytes 12582920 | tf_op jit(solution)/shard_map/ppermute | solution.py:350
  6.3 21.3 %collective-permute-start.2 = (s32[1,4,256]{2,1,0:T(4,128)S(1)}, s32[1,4,256]{2,1,0:T(4,128)S(1)}, u32[]{:S(2)}, u32[]{:S(2)}) collective-permute-start(s32[1,4,256]{2,1,0:T(4,128)S(1)} %get-tuple-element.95), channel_id=1, source_target_pairs={{0,2},{1,3},{2,0},{3,1},{4,6},{5,7},{6,4},{7,5}} | collective-permute-start | bytes 12296 | tf_op jit(solution)/shard_map/ppermute | solution.py:350
  14.4 223.0 %collective-permute-start.5 = (bf16[2,256,2048]{2,1,0:T(8,128)(2,1)}, bf16[2,256,2048]{2,1,0:T(8,128)(2,1)}, u32[]{:S(2)}, u32[]{:S(2)}) collective-permute-start(bf16[2,256,2048]{2,1,0:T(8,128)(2,1)} %get-tuple-element.193), channel_id=1, source_target_pairs={{0,2},{1,3},{2,0},{3,1},{4,6},{5,7},{6,4},{7,5}} | collective-permute-start | bytes 6291464 | tf_op jit(solution)/shard_map/ppermute | solution.py:350
  14.4 224.7 %collective-permute-start.6 = (bf16[2,256,2048]{2,1,0:T(8,128)(2,1)}, bf16[2,256,2048]{2,1,0:T(8,128)(2,1)}, u32[]{:S(2)}, u32[]{:S(2)}) collective-permute-start(bf16[2,256,2048]{2,1,0:T(8,128)(2,1)} %get-tuple-element.192), channel_id=1, source_target_pairs={{0,3},{1,2},{2,1},{3,0},{4,7},{5,6},{6,5},{7,4}} | collective-permute-start | bytes 6291464 | tf_op jit(solution)/shard_map/ppermute | solution.py:350
  20.8 312.3 %collective-permute-start = (bf16[2,256,2048]{2,1,0:T(8,128)(2,1)}, bf16[2,256,2048]{2,1,0:T(8,128)(2,1)}, u32[]{:S(2)}, u32[]{:S(2)}) collective-permute-start(bf16[2,256,2048]{2,1,0:T(8,128)(2,1)} %get-tuple-element.191), channel_id=1, source_target_pairs={{0,2},{1,3},{2,0},{3,1},{4,6},{5,7},{6,4},{7,5}} | collective-permute-start | bytes 6291464 | tf_op jit(solution)/shard_map/ppermute | solution.py:350
  27.7 124.0 %collective-permute-start.3 = (s32[1,4,256]{2,1,0:T(4,128)S(1)}, s32[1,4,256]{2,1,0:T(4,128)S(1)}, u32[]{:S(2)}, u32[]{:S(2)}) collective-permute-start(s32[1,4,256]{2,1,0:T(4,128)S(1)} %get-tuple-element.96), channel_id=1, source_target_pairs={{0,3},{1,2},{2,1},{3,0},{4,7},{5,6},{6,5},{7,4}} | collective-permute-start | bytes 12296 | tf_op jit(solution)/shard_map/ppermute | solution.py:350
  153.4 179.8 %collective-permute-start.1 = (bf16[2,256,2048]{2,1,0:T(8,128)(2,1)}, bf16[2,256,2048]{2,1,0:T(8,128)(2,1)}, u32[]{:S(2)}, u32[]{:S(2)}) collective-permute-start(bf16[2,256,2048]{2,1,0:T(8,128)(2,1)} %get-tuple-element.190), channel_id=1, source_target_pairs={{0,3},{1,2},{2,1},{3,0},{4,7},{5,6},{6,5},{7,4}} | collective-permute-start | bytes 6291464 | tf_op jit(solution)/shard_map/ppermute | solution.py:350
  165.0 314.6 %collective-permute-start.12 = (bf16[1,2,256,2048]{3,2,1,0:T(8,128)(2,1)}, bf16[1,2,256,2048]{3,2,1,0:T(8,128)(2,1)}, u32[]{:S(2)}, u32[]{:S(2)}) collective-permute-start(bf16[1,2,256,2048]{3,2,1,0:T(8,128)(2,1)} %get-tuple-element.183), channel_id=1, source_target_pairs={{0,1},{1,0},{2,3},{3,2},{4,5},{5,4},{6,7},{7,6}} | collective-permute-start | bytes 6291464 | tf_op jit(solution)/shard_map/ppermute | solution.py:350
  237.4 242.5 %collective-permute-start.11 = (bf16[1,2,256,2048]{3,2,1,0:T(8,128)(2,1)}, bf16[1,2,256,2048]{3,2,1,0:T(8,128)(2,1)}, u32[]{:S(2)}, u32[]{:S(2)}) collective-permute-start(bf16[1,2,256,2048]{3,2,1,0:T(8,128)(2,1)} %get-tuple-element.184), channel_id=1, source_target_pairs={{0,3},{1,2},{2,1},{3,0},{4,7},{5,6},{6,5},{7,4}} | collective-permute-start | bytes 6291464 | tf_op jit(solution)/shard_map/ppermute | solution.py:350
  239.1 240.9 %collective-permute-start.10 = (bf16[1,2,256,2048]{3,2,1,0:T(8,128)(2,1)}, bf16[1,2,256,2048]{3,2,1,0:T(8,128)(2,1)}, u32[]{:S(2)}, u32[]{:S(2)}) collective-permute-start(bf16[1,2,256,2048]{3,2,1,0:T(8,128)(2,1)} %get-tuple-element.185), channel_id=1, source_target_pairs={{0,2},{1,3},{2,0},{3,1},{4,6},{5,7},{6,4},{7,5}} | collective-permute-start | bytes 6291464 | tf_op jit(solution)/shard_map/ppermute | solution.py:350
  333.1 259.6 %collective-permute-start.14 = (bf16[1,2,256,2048]{3,2,1,0:T(8,128)(2,1)}, bf16[1,2,256,2048]{3,2,1,0:T(8,128)(2,1)}, u32[]{:S(2)}, u32[]{:S(2)}) collective-permute-start(bf16[1,2,256,2048]{3,2,1,0:T(8,128)(2,1)} %get-tuple-element.181), channel_id=1, source_target_pairs={{0,1},{1,0},{2,3},{3,2},{4,5},{5,4},{6,7},{7,6}} | collective-permute-start | bytes 6291464 | tf_op jit(solution)/shard_map/ppermute | solution.py:350
  333.1 259.6 %collective-permute-start.13 = (bf16[1,2,256,2048]{3,2,1,0:T(8,128)(2,1)}, bf16[1,2,256,2048]{3,2,1,0:T(8,128)(2,1)}, u32[]{:S(2)}, u32[]{:S(2)}) collective-permute-start(bf16[1,2,256,2048]{3,2,1,0:T(8,128)(2,1)} %get-tuple-element.182), channel_id=1, source_target_pairs={{0,3},{1,2},{2,1},{3,0},{4,7},{5,6},{6,5},{7,4}} | collective-permute-start | bytes 6291464 | tf_op jit(solution)/shard_map/ppermute | solution.py:350
  479.6 113.1 %collective-permute-start.9 = (bf16[1,2,256,2048]{3,2,1,0:T(8,128)(2,1)}, bf16[1,2,256,2048]{3,2,1,0:T(8,128)(2,1)}, u32[]{:S(2)}, u32[]{:S(2)}) collective-permute-start(bf16[1,2,256,2048]{3,2,1,0:T(8,128)(2,1)} %get-tuple-element.186), channel_id=1, source_target_pairs={{0,2},{1,3},{2,0},{3,1},{4,6},{5,7},{6,4},{7,5}} | collective-permute-start | bytes 6291464 | tf_op jit(solution)/shard_map/ppermute | solution.py:350
  632.3 54.6 %collective-permute-start.15 = (f32[1024,2048]{1,0:T(8,128)}, f32[1024,2048]{1,0:T(8,128)S(1)}, u32[]{:S(2)}, u32[]{:S(2)}) collective-permute-start(f32[1024,2048]{1,0:T(8,128)} %fusion.28), channel_id=1, source_target_pairs={{0,1},{1,0},{2,3},{3,2},{4,5},{5,4},{6,7},{7,6}} | collective-permute-start | bytes 25165832 | tf_op jit(solution)/shard_map/ppermute | solution.py:350
  796.8 21.9 %collective-permute-start.16 = (f32[1024,2048]{1,0:T(8,128)}, f32[1024,2048]{1,0:T(8,128)S(1)}, u32[]{:S(2)}, u32[]{:S(2)}) collective-permute-start(f32[1024,2048]{1,0:T(8,128)} %fusion.5), channel_id=1, source_target_pairs={{0,1},{1,0},{2,3},{3,2},{4,5},{5,4},{6,7},{7,6}} | collective-permute-start | bytes 25165832 | tf_op jit(solution)/shard_map/ppermute | solution.py:350
  1030.6 21.8 %collective-permute-start.17 = (f32[1024,2048]{1,0:T(8,128)}, f32[1024,2048]{1,0:T(8,128)S(1)}, u32[]{:S(2)}, u32[]{:S(2)}) collective-permute-start(f32[1024,2048]{1,0:T(8,128)} %fusion.3), channel_id=1, source_target_pairs={{0,1},{1,0},{2,3},{3,2},{4,5},{5,4},{6,7},{7,6}} | collective-permute-start | bytes 25165832 | tf_op jit(solution)/shard_map/ppermute | solution.py:350
  1082.3 283.1 %collective-permute-start.18 = (f32[1024,2048]{1,0:T(8,128)}, f32[1024,2048]{1,0:T(8,128)}, u32[]{:S(2)}, u32[]{:S(2)}) collective-permute-start(f32[1024,2048]{1,0:T(8,128)} %fusion.1), channel_id=1, source_target_pairs={{0,1},{1,0},{2,3},{3,2},{4,5},{5,4},{6,7},{7,6}} | collective-permute-start | bytes 25165832 | tf_op jit(solution)/shard_map/ppermute | solution.py:350
  1082.8 183.4 %collective-permute-start.32 = (f32[512,2048]{1,0:T(8,128)}, f32[512,2048]{1,0:T(8,128)}, u32[]{:S(2)}, u32[]{:S(2)}) collective-permute-start(f32[512,2048]{1,0:T(8,128)} %slice_add_fusion.7), channel_id=1, source_target_pairs={{0,2},{1,3},{2,0},{3,1},{4,6},{5,7},{6,4},{7,5}} | collective-permute-start | bytes 12582920 | tf_op jit(solution)/shard_map/ppermute | solution.py:350
  1084.4 187.8 %collective-permute-start.21 = (bf16[1,2,256,2048]{3,2,1,0:T(8,128)(2,1)}, bf16[1,2,256,2048]{3,2,1,0:T(8,128)(2,1)}, u32[]{:S(2)}, u32[]{:S(2)}) collective-permute-start(bf16[1,2,256,2048]{3,2,1,0:T(8,128)(2,1)} %get-tuple-element.148), channel_id=1, source_target_pairs={{0,2},{1,3},{2,0},{3,1},{4,6},{5,7},{6,4},{7,5}} | collective-permute-start | bytes 6291464 | tf_op jit(solution)/shard_map/ppermute | solution.py:350
  1084.9 187.4 %collective-permute-start.22 = (bf16[1,2,256,2048]{3,2,1,0:T(8,128)(2,1)}, bf16[1,2,256,2048]{3,2,1,0:T(8,128)(2,1)}, u32[]{:S(2)}, u32[]{:S(2)}) collective-permute-start(bf16[1,2,256,2048]{3,2,1,0:T(8,128)(2,1)} %get-tuple-element.165), channel_id=1, source_target_pairs={{0,3},{1,2},{2,1},{3,0},{4,7},{5,6},{6,5},{7,4}} | collective-permute-start | bytes 6291464 | tf_op jit(solution)/shard_map/ppermute | solution.py:350
  1085.6 180.5 %collective-permute-start.27 = (f32[3,2048]{1,0:T(4,128)S(1)}, f32[3,2048]{1,0:T(4,128)S(1)}, u32[]{:S(2)}, u32[]{:S(2)}) collective-permute-start(f32[3,2048]{1,0:T(4,128)S(1)} %maximum_add_fusion), channel_id=1, source_target_pairs={{0,2},{1,3},{2,0},{3,1},{4,6},{5,7},{6,4},{7,5}} | collective-permute-start | bytes 73736 | tf_op jit(solution)/shard_map/ppermute | solution.py:350
  1266.1 6.7 collective-permute-start.23
  1266.2 4.4 collective-permute-start.28
  1270.7 48.8 %collective-permute-start.24 = (bf16[1,2,256,2048]{3,2,1,0:T(8,128)(2,1)}, bf16[1,2,256,2048]{3,2,1,0:T(8,128)(2,1)}, u32[]{:S(2)}, u32[]{:S(2)}) collective-permute-start(bf16[1,2,256,2048]{3,2,1,0:T(8,128)(2,1)} %get-tuple-element.156), channel_id=1, source_target_pairs={{0,2},{1,3},{2,0},{3,1},{4,6},{5,7},{6,4},{7,5}} | collective-permute-start | bytes 6291464 | tf_op jit(solution)/shard_map/ppermute | solution.py:350
  1272.2 91.3 %collective-permute-start.25 = (bf16[1,2,256,2048]{3,2,1,0:T(8,128)(2,1)}, bf16[1,2,256,2048]{3,2,1,0:T(8,128)(2,1)}, u32[]{:S(2)}, u32[]{:S(2)}) collective-permute-start(bf16[1,2,256,2048]{3,2,1,0:T(8,128)(2,1)} %get-tuple-element.167), channel_id=1, source_target_pairs={{0,3},{1,2},{2,1},{3,0},{4,7},{5,6},{6,5},{7,4}} | collective-permute-start | bytes 6291464 | tf_op jit(solution)/shard_map/ppermute | solution.py:350
  1272.3 92.0 %collective-permute-start.26 = (bf16[1,2,256,2048]{3,2,1,0:T(8,128)(2,1)}, bf16[1,2,256,2048]{3,2,1,0:T(8,128)(2,1)}, u32[]{:S(2)}, u32[]{:S(2)}) collective-permute-start(bf16[1,2,256,2048]{3,2,1,0:T(8,128)(2,1)} %get-tuple-element.168), channel_id=1, source_target_pairs={{0,1},{1,0},{2,3},{3,2},{4,5},{5,4},{6,7},{7,6}} | collective-permute-start | bytes 6291464 | tf_op jit(solution)/shard_map/ppermute | solution.py:350
  1272.8 181.4 %collective-permute-start.31 = (f32[512,2048]{1,0:T(8,128)}, f32[512,2048]{1,0:T(8,128)S(1)}, u32[]{:S(2)}, u32[]{:S(2)}) collective-permute-start(f32[512,2048]{1,0:T(8,128)} %slice_add_fusion.6), channel_id=1, source_target_pairs={{0,2},{1,3},{2,0},{3,1},{4,6},{5,7},{6,4},{7,5}} | collective-permute-start | bytes 12582920 | tf_op jit(solution)/shard_map/ppermute | solution.py:350
  1319.5 412.9 %collective-permute-start.8 = (bf16[1,4,256,2048]{3,2,1,0:T(8,128)(2,1)}, bf16[1,4,256,2048]{3,2,1,0:T(8,128)(2,1)}, u32[]{:S(2)}, u32[]{:S(2)}) collective-permute-start(bf16[1,4,256,2048]{3,2,1,0:T(8,128)(2,1)} %get-tuple-element.122), channel_id=1, source_target_pairs={{0,2},{1,3},{2,0},{3,1},{4,6},{5,7},{6,4},{7,5}} | collective-permute-start | bytes 12582920 | tf_op jit(solution)/shard_map/ppermute | solution.py:350
  1363.5 368.8 %collective-permute-start.20 = (bf16[1,4,256,2048]{3,2,1,0:T(8,128)(2,1)}, bf16[1,4,256,2048]{3,2,1,0:T(8,128)(2,1)}, u32[]{:S(2)}, u32[]{:S(2)}) collective-permute-start(bf16[1,4,256,2048]{3,2,1,0:T(8,128)(2,1)} %get-tuple-element.162), channel_id=1, source_target_pairs={{0,1},{1,0},{2,3},{3,2},{4,5},{5,4},{6,7},{7,6}} | collective-permute-start | bytes 12582920 | tf_op jit(solution)/shard_map/ppermute | solution.py:350
  1364.2 368.1 %collective-permute-start.19 = (bf16[1,4,256,2048]{3,2,1,0:T(8,128)(2,1)}, bf16[1,4,256,2048]{3,2,1,0:T(8,128)(2,1)}, u32[]{:S(2)}, u32[]{:S(2)}) collective-permute-start(bf16[1,4,256,2048]{3,2,1,0:T(8,128)(2,1)} %get-tuple-element.160), channel_id=1, source_target_pairs={{0,3},{1,2},{2,1},{3,0},{4,7},{5,6},{6,5},{7,4}} | collective-permute-start | bytes 12582920 | tf_op jit(solution)/shard_map/ppermute | solution.py:350
  1365.4 358.5 %collective-permute-start.29 = (f32[512,2048]{1,0:T(8,128)S(1)}, f32[512,2048]{1,0:T(8,128)}, u32[]{:S(2)}, u32[]{:S(2)}) collective-permute-start(f32[512,2048]{1,0:T(8,128)S(1)} %copy-done.10), channel_id=1, source_target_pairs={{0,2},{1,3},{2,0},{3,1},{4,6},{5,7},{6,4},{7,5}} | collective-permute-start | bytes 12582920 | tf_op jit(solution)/shard_map/ppermute | solution.py:350
  1454.2 358.8 %collective-permute-start.30 = (f32[512,2048]{1,0:T(8,128)}, f32[512,2048]{1,0:T(8,128)}, u32[]{:S(2)}, u32[]{:S(2)}) collective-permute-start(f32[512,2048]{1,0:T(8,128)} %slice_add_fusion.4), channel_id=1, source_target_pairs={{0,2},{1,3},{2,0},{3,1},{4,6},{5,7},{6,4},{7,5}} | collective-permute-start | bytes 12582920 | tf_op jit(solution)/shard_map/ppermute | solution.py:350
  (35 other events, 1726.3 us)

commit v4 on v3

--- a/solution.py
+++ b/solution.py
@@ -43,7 +43,7 @@
 
 
 def place(bits):
-    return jnp.where((bits == 0) | (bits == 3), 3 - bits, bits)
+    return 3 - bits
 
 
 def front_own_kernel(*refs):
@@ -373,18 +373,23 @@
             return lax.dynamic_update_slice(buf, got, (me ^ bits, seq0, 0, 0))
 
         def grad_rows(rels, rights):
-            half = d_model // 2
-
-            def part(cols):
-                terms = [dot_tn(flat(r)[:, cols], flat(g)) for r, g in zip(rels, rights)]
+            blk = d_model // n_sp
+
+            def part(n, grads):
+                terms = [dot_tn(flat(r)[:, n * blk:(n + 1) * blk], flat(g)) for r, g in zip(rels, grads)]
                 return sum(terms[1:], terms[0])
 
-            out = part(slice(0, half))
-            out = to_peer(out, 1)
-            keep = part(slice(half, None))
-            far = keep[:half // 2] + out[:half // 2]
+            given = to_peer(part(0, rights), 1)
+            far = lax.optimization_barrier(part(1, rights)) + given
             got = to_peer(far, 2)
-            return (keep[half // 2:], out[half // 2:], got), far
+
+            def rest(prev):
+                late = [after(g, prev) for g in rights]
+                given = to_peer(part(2, late), 1)
+                mine = lax.optimization_barrier(part(3, late))
+                return mine, given, got
+
+            return rest, far
 
         pos4 = positions.reshape(n_sp, n_seq, rows)
         pos4, *cut = lax.optimization_barrier([pos4] + [lax.dynamic_slice_in_dim(pos4, me ^ bits, 1, axis=0) for bits in far_bits])
@@ -445,6 +450,10 @@
         dqr, dkr, gx = tails
         w_q, prev = grad_rows([h_rel], [after(dqr, prev)])
         w_k, prev = grad_rows([h_rel], [after(dkr, prev)])
+        sums = []
+        for rest in (w_q, w_k, w_v, w_o):
+            sums.append(rest(prev))
+            prev = sums[-1][0]
         for bits, got in zip(far_bits, y_got):
             y = put(y, after(got, prev), bits, 0)
         for c in range(N_CHUNK):
@@ -454,7 +463,7 @@
         gains = lax.dynamic_slice_in_dim(gains, me * (d_model // n_sp), d_model // n_sp, axis=1)
         total = lambda terms: terms[0] + terms[1] + terms[2]
         join = lambda arr: arr.reshape(x_loc.shape)
-        return (join(y), join(gx), gains[0], total(w_q), total(w_k), total(w_v), total(w_o), gains[1], gains[2])
+        return (join(y), join(gx), gains[0], *map(total, sums), gains[1], gains[2])
 
     seq_spec = P('dp', 'sp', None)
     mat_rep = P(None, None)

time: 1830 us -> 1700 us (0.929)
  waiting for transfers between devices: 758 us -> 625 us
  matrix products: 285 us -> 306 us
    ppermute x33 -> x37, waiting for transfers between devices: 758 us -> 625 us  [to_peer(): return lax.ppermute(value, 'sp', [(i, i ^ bits) for i in range(n_sp)])]
    dot_general x10 -> x20, matrix products: 193 us -> 219 us  [dot_tn(): lax.dot_general(a, b, (((0,), (0,)), ((), ())), preferred_element_type=F32)]
  transfers between devices with their start and end apart: 33 -> 37, of which waited for: 9 -> 10; matrix products, arithmetic and copies ran while one was open for 16% -> 22% of each run, Pallas kernels for 19% -> 20%
where the time goes in v4:
time: 1700 us; the launch traced here: 1690 us
  waiting for transfers between devices  625 us (37%)
  Pallas kernels  586 us (34%)
  matrix products  306 us (18%)
  local copies, waits for them, and re-layouts  90.3 us (5%)
  other arithmetic  54.5 us (3%)
  starting transfers between devices  27.7 us (2%)
    ppermute x37, waiting for transfers between devices, to_peer(): return lax.ppermute(value, 'sp', [(i, i ^ bits) for i in range(n_sp)])  625 us
    dot_general x20, matrix products, dot_tn(): lax.dot_general(a, b, (((0,), (0,)), ((), ())), preferred_element_type=F32)  219 us
    pallas_call x2, Pallas kernels, tail(): pl.pallas_call(tail_kernel, grid=(n_piece, n_seq), in_specs=[loc] * 2 + [...  168 us
    pallas_call x2, Pallas kernels, attend_back(): pl.pallas_call(attend_back_kernel, grid=(n_seq, n_heads // heads), in_spe...  159 us
    pallas_call x3, Pallas kernels, front(): pl.pallas_call(front_own_kernel if own else front_kernel, grid_spec=pltpu...  154 us
    pallas_call x2, Pallas kernels, attend(): pl.pallas_call(attend_kernel, grid_spec=pltpu.PrefetchScalarGridSpec(num_...  105 us
    dynamic_update_slice x15, local copies, waits for them, and re-layouts, put(): return lax.dynamic_update_slice(buf, got, (me ^ bits, seq0, 0, 0))  48.5 us
    dot_general x2, matrix products, dot_nt(): lax.dot_general(a, b, (((1,), (1,)), ((), ())), preferred_element_type=F32)  45.9 us
  transfers between devices with their start and end apart: 37, of which 10 were waited for; matrix products, arithmetic and copies ran while one was open for 22% of the time, Pallas kernels for 20%

profile of v4, /device:TPU:0, one launch (start us, length us, event | category | flops | bytes accessed | tf_op | source)
XLA Modules:
  0.0 1691.5 jit_solution(7211994787805731130)
XLA Ops:
  29.1 122.5 %collective-permute-done.3 = s32[1,4,256]{2,1,0:T(4,128)S(1)} collective-permute-done((s32[1,4,256]{2,1,0:T(4,128)S(1)}, s32[1,4,256]{2,1,0:T(4,128)S(1)}, u32[]{:S(2)}, u32[]{:S(2)}) %collective-permute-start.3) | collective-permute-done | bytes 4128 | tf_op jit(solution)/shard_map/ppermute | solution.py:350
  165.1 72.4 %front.3 = (bf16[4,4,256,2048]{3,2,1,0:T(8,128)(2,1)}, bf16[4,4,256,2048]{3,2,1,0:T(8,128)(2,1)}, bf16[4,4,256,2048]{3,2,1,0:T(8,128)(2,1)}, bf16[4,4,256,2048]{...) custom-call(s32[1]{0:T(128)} %bitcast.refs_0_.me_ref, ...), custom_call_target="tpu_custom_call" | custom-call | flops 51539607552 | bytes 109051904 | tf_op jit(solution)/shard_map/front/pallas_call | solution.py:123
  239.5 41.1 %front.4 = (bf16[4,4,256,2048]{3,2,1,0:T(8,128)(2,1)}, bf16[4,4,256,2048]{3,2,1,0:T(8,128)(2,1)}, bf16[4,4,256,2048]{3,2,1,0:T(8,128)(2,1)}, bf16[4,4,256,2048]{...) custom-call(s32[1]{0:T(128)} %bitcast.refs_0_.me_ref, ...), custom_call_target="tpu_custom_call", output_to_operand_aliasing={{0}: (11, {}), {1}: (12, {}), {2}: (13, {}), {3}: (14, {}),... | custom-call | flops 25769803776 | bytes 67108864 | tf_op jit(solution)/shard_map/front/pallas_call | solution.py:123
  280.6 52.4 %attend.2 = (bf16[4,2,256,2048]{3,2,1,0:T(8,128)(2,1)}, bf16[4,4,256,2048]{3,2,1,0:T(8,128)(2,1)}, f32[4,16,1,1024]{3,2,1,0:T(1,128)}) custom-call(s32[1]{0:T(128)} %bitcast.refs_0_.me_ref, bf16[4,4,256,2048]{3,2,1,0:T(8,128)(2,1)} %get-tuple-element.111.q_ref.refs_2_, bf16[4,4,256,2048]{3,2,1,0:T(8,128)(2,1)} %get-tuple-element.112.k_ref.refs_3_, ...), custom_call_target="tpu_custom_call" | custom-call | flops 25769803776 | bytes 41943040 | tf_op jit(solution)/shard_map/attend/pallas_call | solution.py:177
  335.0 40.8 %front.5 = (bf16[4,4,256,2048]{3,2,1,0:T(8,128)(2,1)}, bf16[4,4,256,2048]{3,2,1,0:T(8,128)(2,1)}, bf16[4,4,256,2048]{3,2,1,0:T(8,128)(2,1)}, bf16[4,4,256,2048]{...) custom-call(s32[1]{0:T(128)} %bitcast.refs_0_.me_ref, ...), custom_call_target="tpu_custom_call", output_to_operand_aliasing={{0}: (11, {}), {1}: (12, {}), {2}: (13, {}), {3}: (14, {}),... | custom-call | flops 25769803776 | bytes 67108864 | tf_op jit(solution)/shard_map/front/pallas_call | solution.py:123
  375.9 52.5 %attend.3 = (bf16[4,2,256,2048]{3,2,1,0:T(8,128)(2,1)}, bf16[4,4,256,2048]{3,2,1,0:T(8,128)(2,1)}, f32[4,16,1,1024]{3,2,1,0:T(1,128)}) custom-call(s32[1]{0:T(128)} %bitcast.refs_0_.me_ref, bf16[4,4,256,2048]{3,2,1,0:T(8,128)(2,1)} %get-tuple-element.121.q_ref, ...), custom_call_target="tpu_custom_call", output_to_operand_aliasing={{1}: (4, {}), {2}: (5, {})} | custom-call | flops 25769803776 | bytes 41943040 | tf_op jit(solution)/shard_map/attend/pallas_call | solution.py:177
  428.4 41.3 %fusion = bf16[4096,2048]{1,0:T(8,128)(2,1)S(1)} fusion(bf16[4,4,256,2048]{3,2,1,0:T(8,128)(2,1)} %get-tuple-element.120.x_ref, bf16[4096,2048]{1,0:T(8,128)(2,1)} %bitcast.139, bf16[2048,2048]{1,0:T(8,128)(2,1)} %param.17), kind=kOutput, calls=%fused_computation.1 | convolution fusion | flops 34384904192 | bytes 58720256 | tf_op jit(solution)/shard_map/dot_general | solution.py:23
  489.4 23.8 %convolution_convert_fusion.1 = bf16[2048,2048]{1,0:T(8,128)(2,1)} fusion(bf16[2048,2048]{1,0:T(8,128)(2,1)} %bitcast.134, bf16[2048,2048]{1,0:T(8,128)(2,1)} %param.17), kind=kOutput, calls=%fused_computation.3 | convolution fusion | flops 17184063488 | bytes 25165824 | tf_op jit(solution)/shard_map/dot_general | solution.py:27
  513.2 79.6 %attend_back.2 = (bf16[4,2,256,2048]{3,2,1,0:T(8,128)(2,1)}, bf16[4,2,256,2048]{3,2,1,0:T(8,128)(2,1)}, bf16[4,4,256,2048]{3,2,1,0:T(8,128)(2,1)}) custom-call(bf16[4,4,256,2048]{3,2,1,0:T(8,128)(2,1)} %get-tuple-element.121.q_ref, bf16[4,4,256,2048]{3,2,1,0:T(8,128)(2,1)} %get-tuple-element.122.k_ref, bf16[4,4,256,2048]{3,2,1,0:T(8,128)(2,1)} %get-tuple-element.123.v_ref, ...), custom_call_target="tpu_custom_call" | custom-call | flops 60129542144 | bytes 58720256 | tf_op jit(solution)/shard_map/attend_back/pallas_call | solution.py:241
  625.1 22.2 %convolution_convert_fusion = bf16[2048,2048]{1,0:T(8,128)(2,1)} fusion(bf16[2048,2048]{1,0:T(8,128)(2,1)S(1)} %bitcast.71, bf16[2048,2048]{1,0:T(8,128)(2,1)} %param.17), kind=kOutput, calls=%fused_computation.2 | convolution fusion | flops 17184063488 | bytes 25165824 | tf_op jit(solution)/shard_map/dot_general | solution.py:27
  650.2 79.6 %attend_back.3 = (bf16[4,2,256,2048]{3,2,1,0:T(8,128)(2,1)}, bf16[4,2,256,2048]{3,2,1,0:T(8,128)(2,1)}, bf16[4,4,256,2048]{3,2,1,0:T(8,128)(2,1)}) custom-call(bf16[4,4,256,2048]{3,2,1,0:T(8,128)(2,1)} %get-tuple-element.121.q_ref, bf16[4,4,256,2048]{3,2,1,0:T(8,128)(2,1)} %get-tuple-element.122.k_ref, ...), custom_call_target="tpu_custom_call", output_to_operand_aliasing={{2}: (5, {})} | custom-call | flops 60129542144 | bytes 58720256 | tf_op jit(solution)/shard_map/attend_back/pallas_call | solution.py:241
  729.8 15.1 fusion.11
  745.3 10.6 fusion.17
  758.8 84.1 %tail.2 = (bf16[4,4,256,2048]{3,2,1,0:T(8,128)(2,1)}, bf16[4,4,256,2048]{3,2,1,0:T(8,128)(2,1)}, bf16[4,4,256,2048]{3,2,1,0:T(8,128)(2,1)}, f32[1,2048]{1,0:T(1,...) custom-call(bf16[4,2,256,2048]{3,2,1,0:T(8,128)(2,1)} %get-tuple-element.138.dq_ref, ...), custom_call_target="tpu_custom_call" | custom-call | flops 51539607552 | bytes 125829120 | tf_op jit(solution)/shard_map/tail/pallas_call | solution.py:319
  848.5 83.8 %tail.3 = (bf16[4,4,256,2048]{3,2,1,0:T(8,128)(2,1)}, bf16[4,4,256,2048]{3,2,1,0:T(8,128)(2,1)}, bf16[4,4,256,2048]{3,2,1,0:T(8,128)(2,1)}, f32[1,2048]{1,0:T(1,...) custom-call(bf16[4,2,256,2048]{3,2,1,0:T(8,128)(2,1)} %get-tuple-elemen, ...), custom_call_target="tpu_custom_call", output_to_operand_aliasing={{0}: (15, {}), {1}: (16, {}), {2}: (17, {})} | custom-call | flops 51539607552 | bytes 125829120 | tf_op jit(solution)/shard_map/tail/pallas_call | solution.py:319
  938.1 15.2 fusion.9
  957.5 13.7 fusion.15
  980.3 23.8 %collective-permute-done.21 = bf16[1,2,256,2048]{3,2,1,0:T(8,128)(2,1)} collective-permute-done((bf16[1,2,256,2048]{3,2,1,0:T(8,128)(2,1)}, bf16[1,2,256,2048]{3,2,1,0:T(8,128)(2,1)}, u32[]{:S(2)}, u32[]{:S(2)}) %collective-permute-start.21) | collective-permute-done | bytes 2097184 | tf_op jit(solution)/shard_map/ppermute | solution.py:350
  1004.1 13.8 fusion.7
  1017.9 74.5 %collective-permute-done.22 = bf16[1,2,256,2048]{3,2,1,0:T(8,128)(2,1)} collective-permute-done((bf16[1,2,256,2048]{3,2,1,0:T(8,128)(2,1)}, bf16[1,2,256,2048]{3,2,1,0:T(8,128)(2,1)}, u32[]{:S(2)}, u32[]{:S(2)}) %collective-permute-start.22) | collective-permute-done | bytes 2097184 | tf_op jit(solution)/shard_map/ppermute | solution.py:350
  1107.8 29.5 %collective-permute-done.25 = bf16[1,2,256,2048]{3,2,1,0:T(8,128)(2,1)} collective-permute-done((bf16[1,2,256,2048]{3,2,1,0:T(8,128)(2,1)}, bf16[1,2,256,2048]{3,2,1,0:T(8,128)(2,1)}, u32[]{:S(2)}, u32[]{:S(2)}) %collective-permute-start.25) | collective-permute-done | bytes 2097184 | tf_op jit(solution)/shard_map/ppermute | solution.py:350
  1146.7 11.7 fusion.13
  1161.6 14.1 fusion.23
  1175.7 13.9 fusion.21
  1189.7 13.9 fusion.19
  1219.0 13.7 fusion.1
  1232.7 13.7 fusion.3
  1246.4 13.7 fusion.5
  1260.1 57.0 %collective-permute-done.19 = bf16[1,4,256,2048]{3,2,1,0:T(8,128)(2,1)} collective-permute-done((bf16[1,4,256,2048]{3,2,1,0:T(8,128)(2,1)}, bf16[1,4,256,2048]{3,2,1,0:T(8,128)(2,1)}, u32[]{:S(2)}, u32[]{:S(2)}) %collective-permute-start.19) | collective-permute-done | bytes 4194336 | tf_op jit(solution)/shard_map/ppermute | solution.py:350
  1326.8 81.7 %collective-permute-done.36 = f32[512,2048]{1,0:T(8,128)} collective-permute-done((f32[512,2048]{1,0:T(8,128)}, f32[512,2048]{1,0:T(8,128)}, u32[]{:S(2)}, u32[]{:S(2)}) %collective-permute-start.36) | collective-permute-done | bytes 4194336 | tf_op jit(solution)/shard_map/ppermute | solution.py:350
  1409.0 89.4 %collective-permute-done.34 = f32[512,2048]{1,0:T(8,128)} collective-permute-done((f32[512,2048]{1,0:T(8,128)}, f32[512,2048]{1,0:T(8,128)}, u32[]{:S(2)}, u32[]{:S(2)}) %collective-permute-start.34) | collective-permute-done | bytes 4194336 | tf_op jit(solution)/shard_map/ppermute | solution.py:350
  1534.0 143.4 %collective-permute-done.32 = f32[512,2048]{1,0:T(8,128)} collective-permute-done((f32[512,2048]{1,0:T(8,128)S(1)}, f32[512,2048]{1,0:T(8,128)}, u32[]{:S(2)}, u32[]{:S(2)}) %collective-permute-start.32) | collective-permute-done | bytes 4194336 | tf_op jit(solution)/shard_map/ppermute | solution.py:350
  (183 shorter events, 231.4 us)
Async XLA Ops:
  5.5 159.5 %collective-permute-start.7 = (bf16[4,256,2048]{2,1,0:T(8,128)(2,1)}, bf16[4,256,2048]{2,1,0:T(8,128)(2,1)}, u32[]{:S(2)}, u32[]{:S(2)}) collective-permute-start(bf16[4,256,2048]{2,1,0:T(8,128)(2,1)} %dynamic-slice_bitcast_fusion), channel_id=1, source_target_pairs={{0,1},{1,0},{2,3},{3,2},{4,5},{5,4},{6,7},{7,6}} | collective-permute-start | bytes 12582920 | tf_op jit(solution)/shard_map/ppermute | solution.py:350
  6.3 21.3 %collective-permute-start.2 = (s32[1,4,256]{2,1,0:T(4,128)S(1)}, s32[1,4,256]{2,1,0:T(4,128)S(1)}, u32[]{:S(2)}, u32[]{:S(2)}) collective-permute-start(s32[1,4,256]{2,1,0:T(4,128)S(1)} %get-tuple-element.100), channel_id=1, source_target_pairs={{0,2},{1,3},{2,0},{3,1},{4,6},{5,7},{6,4},{7,5}} | collective-permute-start | bytes 12296 | tf_op jit(solution)/shard_map/ppermute | solution.py:350
  14.4 223.0 %collective-permute-start.5 = (bf16[2,256,2048]{2,1,0:T(8,128)(2,1)}, bf16[2,256,2048]{2,1,0:T(8,128)(2,1)}, u32[]{:S(2)}, u32[]{:S(2)}) collective-permute-start(bf16[2,256,2048]{2,1,0:T(8,128)(2,1)} %get-tuple-element.203), channel_id=1, source_target_pairs={{0,2},{1,3},{2,0},{3,1},{4,6},{5,7},{6,4},{7,5}} | collective-permute-start | bytes 6291464 | tf_op jit(solution)/shard_map/ppermute | solution.py:350
  14.4 224.8 %collective-permute-start.6 = (bf16[2,256,2048]{2,1,0:T(8,128)(2,1)}, bf16[2,256,2048]{2,1,0:T(8,128)(2,1)}, u32[]{:S(2)}, u32[]{:S(2)}) collective-permute-start(bf16[2,256,2048]{2,1,0:T(8,128)(2,1)} %get-tuple-element.202), channel_id=1, source_target_pairs={{0,3},{1,2},{2,1},{3,0},{4,7},{5,6},{6,5},{7,4}} | collective-permute-start | bytes 6291464 | tf_op jit(solution)/shard_map/ppermute | solution.py:350
  20.8 312.2 %collective-permute-start = (bf16[2,256,2048]{2,1,0:T(8,128)(2,1)}, bf16[2,256,2048]{2,1,0:T(8,128)(2,1)}, u32[]{:S(2)}, u32[]{:S(2)}) collective-permute-start(bf16[2,256,2048]{2,1,0:T(8,128)(2,1)} %get-tuple-element.201), channel_id=1, source_target_pairs={{0,2},{1,3},{2,0},{3,1},{4,6},{5,7},{6,4},{7,5}} | collective-permute-start | bytes 6291464 | tf_op jit(solution)/shard_map/ppermute | solution.py:350
  27.6 124.0 %collective-permute-start.3 = (s32[1,4,256]{2,1,0:T(4,128)S(1)}, s32[1,4,256]{2,1,0:T(4,128)S(1)}, u32[]{:S(2)}, u32[]{:S(2)}) collective-permute-start(s32[1,4,256]{2,1,0:T(4,128)S(1)} %get-tuple-element.101), channel_id=1, source_target_pairs={{0,3},{1,2},{2,1},{3,0},{4,7},{5,6},{6,5},{7,4}} | collective-permute-start | bytes 12296 | tf_op jit(solution)/shard_map/ppermute | solution.py:350
  153.4 179.7 %collective-permute-start.1 = (bf16[2,256,2048]{2,1,0:T(8,128)(2,1)}, bf16[2,256,2048]{2,1,0:T(8,128)(2,1)}, u32[]{:S(2)}, u32[]{:S(2)}) collective-permute-start(bf16[2,256,2048]{2,1,0:T(8,128)(2,1)} %get-tuple-element.200), channel_id=1, source_target_pairs={{0,3},{1,2},{2,1},{3,0},{4,7},{5,6},{6,5},{7,4}} | collective-permute-start | bytes 6291464 | tf_op jit(solution)/shard_map/ppermute | solution.py:350
  164.9 314.7 %collective-permute-start.11 = (bf16[1,2,256,2048]{3,2,1,0:T(8,128)(2,1)}, bf16[1,2,256,2048]{3,2,1,0:T(8,128)(2,1)}, u32[]{:S(2)}, u32[]{:S(2)}) collective-permute-start(bf16[1,2,256,2048]{3,2,1,0:T(8,128)(2,1)} %get-tuple-element.194), channel_id=1, source_target_pairs={{0,1},{1,0},{2,3},{3,2},{4,5},{5,4},{6,7},{7,6}} | collective-permute-start | bytes 6291464 | tf_op jit(solution)/shard_map/ppermute | solution.py:350
  237.5 242.4 %collective-permute-start.10 = (bf16[1,2,256,2048]{3,2,1,0:T(8,128)(2,1)}, bf16[1,2,256,2048]{3,2,1,0:T(8,128)(2,1)}, u32[]{:S(2)}, u32[]{:S(2)}) collective-permute-start(bf16[1,2,256,2048]{3,2,1,0:T(8,128)(2,1)} %get-tuple-element.195), channel_id=1, source_target_pairs={{0,3},{1,2},{2,1},{3,0},{4,7},{5,6},{6,5},{7,4}} | collective-permute-start | bytes 6291464 | tf_op jit(solution)/shard_map/ppermute | solution.py:350
  239.2 240.7 %collective-permute-start.9 = (bf16[1,2,256,2048]{3,2,1,0:T(8,128)(2,1)}, bf16[1,2,256,2048]{3,2,1,0:T(8,128)(2,1)}, u32[]{:S(2)}, u32[]{:S(2)}) collective-permute-start(bf16[1,2,256,2048]{3,2,1,0:T(8,128)(2,1)} %get-tuple-element.196), channel_id=1, source_target_pairs={{0,2},{1,3},{2,0},{3,1},{4,6},{5,7},{6,4},{7,5}} | collective-permute-start | bytes 6291464 | tf_op jit(solution)/shard_map/ppermute | solution.py:350
  333.0 267.4 %collective-permute-start.14 = (bf16[1,2,256,2048]{3,2,1,0:T(8,128)(2,1)}, bf16[1,2,256,2048]{3,2,1,0:T(8,128)(2,1)}, u32[]{:S(2)}, u32[]{:S(2)}) collective-permute-start(bf16[1,2,256,2048]{3,2,1,0:T(8,128)(2,1)} %get-tuple-element.191), channel_id=1, source_target_pairs={{0,1},{1,0},{2,3},{3,2},{4,5},{5,4},{6,7},{7,6}} | collective-permute-start | bytes 6291464 | tf_op jit(solution)/shard_map/ppermute | solution.py:350
  333.1 267.4 %collective-permute-start.13 = (bf16[1,2,256,2048]{3,2,1,0:T(8,128)(2,1)}, bf16[1,2,256,2048]{3,2,1,0:T(8,128)(2,1)}, u32[]{:S(2)}, u32[]{:S(2)}) collective-permute-start(bf16[1,2,256,2048]{3,2,1,0:T(8,128)(2,1)} %get-tuple-element.192), channel_id=1, source_target_pairs={{0,3},{1,2},{2,1},{3,0},{4,7},{5,6},{6,5},{7,4}} | collective-permute-start | bytes 6291464 | tf_op jit(solution)/shard_map/ppermute | solution.py:350
  479.7 128.6 %collective-permute-start.12 = (bf16[1,2,256,2048]{3,2,1,0:T(8,128)(2,1)}, bf16[1,2,256,2048]{3,2,1,0:T(8,128)(2,1)}, u32[]{:S(2)}, u32[]{:S(2)}) collective-permute-start(bf16[1,2,256,2048]{3,2,1,0:T(8,128)(2,1)} %get-tuple-element.193), channel_id=1, source_target_pairs={{0,2},{1,3},{2,0},{3,1},{4,6},{5,7},{6,4},{7,5}} | collective-permute-start | bytes 6291464 | tf_op jit(solution)/shard_map/ppermute | solution.py:350
  620.2 27.0 %collective-permute-start.15 = (f32[512,2048]{1,0:T(8,128)}, f32[512,2048]{1,0:T(8,128)S(1)}, u32[]{:S(2)}, u32[]{:S(2)}) collective-permute-start(f32[512,2048]{1,0:T(8,128)} %convolution_add_fusion.2), channel_id=1, source_target_pairs={{0,1},{1,0},{2,3},{3,2},{4,5},{5,4},{6,7},{7,6}} | collective-permute-start | bytes 12582920 | tf_op jit(solution)/shard_map/ppermute | solution.py:350
  955.3 48.8 %collective-permute-start.21 = (bf16[1,2,256,2048]{3,2,1,0:T(8,128)(2,1)}, bf16[1,2,256,2048]{3,2,1,0:T(8,128)(2,1)}, u32[]{:S(2)}, u32[]{:S(2)}) collective-permute-start(bf16[1,2,256,2048]{3,2,1,0:T(8,128)(2,1)} %get-tuple-element.153), channel_id=1, source_target_pairs={{0,2},{1,3},{2,0},{3,1},{4,6},{5,7},{6,4},{7,5}} | collective-permute-start | bytes 6291464 | tf_op jit(solution)/shard_map/ppermute | solution.py:350
  971.2 133.4 %collective-permute-start.24 = (bf16[1,2,256,2048]{3,2,1,0:T(8,128)(2,1)}, bf16[1,2,256,2048]{3,2,1,0:T(8,128)(2,1)}, u32[]{:S(2)}, u32[]{:S(2)}) collective-permute-start(bf16[1,2,256,2048]{3,2,1,0:T(8,128)(2,1)} %get-tuple-element.161), channel_id=1, source_target_pairs={{0,2},{1,3},{2,0},{3,1},{4,6},{5,7},{6,4},{7,5}} | collective-permute-start | bytes 6291464 | tf_op jit(solution)/shard_map/ppermute | solution.py:350
  973.4 119.0 %collective-permute-start.22 = (bf16[1,2,256,2048]{3,2,1,0:T(8,128)(2,1)}, bf16[1,2,256,2048]{3,2,1,0:T(8,128)(2,1)}, u32[]{:S(2)}, u32[]{:S(2)}) collective-permute-start(bf16[1,2,256,2048]{3,2,1,0:T(8,128)(2,1)} %get-tuple-element.175), channel_id=1, source_target_pairs={{0,3},{1,2},{2,1},{3,0},{4,7},{5,6},{6,5},{7,4}} | collective-permute-start | bytes 6291464 | tf_op jit(solution)/shard_map/ppermute | solution.py:350
  973.5 127.5 %collective-permute-start.23 = (bf16[1,2,256,2048]{3,2,1,0:T(8,128)(2,1)}, bf16[1,2,256,2048]{3,2,1,0:T(8,128)(2,1)}, u32[]{:S(2)}, u32[]{:S(2)}) collective-permute-start(bf16[1,2,256,2048]{3,2,1,0:T(8,128)(2,1)} %get-tuple-element.176), channel_id=1, source_target_pairs={{0,1},{1,0},{2,3},{3,2},{4,5},{5,4},{6,7},{7,6}} | collective-permute-start | bytes 6291464 | tf_op jit(solution)/shard_map/ppermute | solution.py:350
  978.6 158.8 %collective-permute-start.25 = (bf16[1,2,256,2048]{3,2,1,0:T(8,128)(2,1)}, bf16[1,2,256,2048]{3,2,1,0:T(8,128)(2,1)}, u32[]{:S(2)}, u32[]{:S(2)}) collective-permute-start(bf16[1,2,256,2048]{3,2,1,0:T(8,128)(2,1)} %get-tuple-element.177), channel_id=1, source_target_pairs={{0,3},{1,2},{2,1},{3,0},{4,7},{5,6},{6,5},{7,4}} | collective-permute-start | bytes 6291464 | tf_op jit(solution)/shard_map/ppermute | solution.py:350
  1004.1 137.9 %collective-permute-start.26 = (bf16[1,2,256,2048]{3,2,1,0:T(8,128)(2,1)S(1)}, bf16[1,2,256,2048]{3,2,1,0:T(8,128)(2,1)}, u32[]{:S(2)}, u32[]{:S(2)}) collective-permute-start(bf16[1,2,256,2048]{3,2,1,0:T(8,128)(2,1)S(1)} %get-tuple-element.178), channel_id=1, source_target_pairs={{0,1},{1,0},{2,3},{3,2},{4,5},{5,4},{6,7},{7,6}} | collective-permute-start | bytes 6291464 | tf_op jit(solution)/shard_map/ppermute | solution.py:350
  1092.4 66.0 %collective-permute-start.18 = (f32[512,2048]{1,0:T(8,128)}, f32[512,2048]{1,0:T(8,128)S(1)}, u32[]{:S(2)}, u32[]{:S(2)}) collective-permute-start(f32[512,2048]{1,0:T(8,128)} %fusion.7), channel_id=1, source_target_pairs={{0,1},{1,0},{2,3},{3,2},{4,5},{5,4},{6,7},{7,6}} | collective-permute-start | bytes 12582920 | tf_op jit(solution)/shard_map/ppermute | solution.py:350
  1101.0 225.3 %collective-permute-start.8 = (bf16[1,4,256,2048]{3,2,1,0:T(8,128)(2,1)}, bf16[1,4,256,2048]{3,2,1,0:T(8,128)(2,1)}, u32[]{:S(2)}, u32[]{:S(2)}) collective-permute-start(bf16[1,4,256,2048]{3,2,1,0:T(8,128)(2,1)} %get-tuple-element.127), channel_id=1, source_target_pairs={{0,2},{1,3},{2,0},{3,1},{4,6},{5,7},{6,4},{7,5}} | collective-permute-start | bytes 12582920 | tf_op jit(solution)/shard_map/ppermute | solution.py:350
  1104.6 128.1 %collective-permute-start.20 = (bf16[1,4,256,2048]{3,2,1,0:T(8,128)(2,1)}, bf16[1,4,256,2048]{3,2,1,0:T(8,128)(2,1)}, u32[]{:S(2)}, u32[]{:S(2)}) collective-permute-start(bf16[1,4,256,2048]{3,2,1,0:T(8,128)(2,1)} %get-tuple-element.172), channel_id=1, source_target_pairs={{0,1},{1,0},{2,3},{3,2},{4,5},{5,4},{6,7},{7,6}} | collective-permute-start | bytes 12582920 | tf_op jit(solution)/shard_map/ppermute | solution.py:350
  1137.3 179.8 %collective-permute-start.19 = (bf16[1,4,256,2048]{3,2,1,0:T(8,128)(2,1)}, bf16[1,4,256,2048]{3,2,1,0:T(8,128)(2,1)}, u32[]{:S(2)}, u32[]{:S(2)}) collective-permute-start(bf16[1,4,256,2048]{3,2,1,0:T(8,128)(2,1)} %get-tuple-element.170), channel_id=1, source_target_pairs={{0,3},{1,2},{2,1},{3,0},{4,7},{5,6},{6,5},{7,4}} | collective-permute-start | bytes 12582920 | tf_op jit(solution)/shard_map/ppermute | solution.py:350
  1142.0 266.6 %collective-permute-start.36 = (f32[512,2048]{1,0:T(8,128)}, f32[512,2048]{1,0:T(8,128)}, u32[]{:S(2)}, u32[]{:S(2)}) collective-permute-start(f32[512,2048]{1,0:T(8,128)} %add.54), channel_id=1, source_target_pairs={{0,2},{1,3},{2,0},{3,1},{4,6},{5,7},{6,4},{7,5}} | collective-permute-start | bytes 12582920 | tf_op jit(solution)/shard_map/ppermute | solution.py:350
  1158.4 340.1 %collective-permute-start.34 = (f32[512,2048]{1,0:T(8,128)}, f32[512,2048]{1,0:T(8,128)}, u32[]{:S(2)}, u32[]{:S(2)}) collective-permute-start(f32[512,2048]{1,0:T(8,128)} %add.55), channel_id=1, source_target_pairs={{0,2},{1,3},{2,0},{3,1},{4,6},{5,7},{6,4},{7,5}} | collective-permute-start | bytes 12582920 | tf_op jit(solution)/shard_map/ppermute | solution.py:350
  1232.7 265.7 %collective-permute-start.35 = (f32[512,2048]{1,0:T(8,128)}, f32[512,2048]{1,0:T(8,128)}, u32[]{:S(2)}, u32[]{:S(2)}) collective-permute-start(f32[512,2048]{1,0:T(8,128)} %convolution_add_fusion), channel_id=1, source_target_pairs={{0,1},{1,0},{2,3},{3,2},{4,5},{5,4},{6,7},{7,6}} | collective-permute-start | bytes 12582920 | tf_op jit(solution)/shard_map/ppermute | solution.py:350
  1317.1 209.9 %collective-permute-start.33 = (f32[512,2048]{1,0:T(8,128)}, f32[512,2048]{1,0:T(8,128)}, u32[]{:S(2)}, u32[]{:S(2)}) collective-permute-start(f32[512,2048]{1,0:T(8,128)} %fusion.1), channel_id=1, source_target_pairs={{0,1},{1,0},{2,3},{3,2},{4,5},{5,4},{6,7},{7,6}} | collective-permute-start | bytes 12582920 | tf_op jit(solution)/shard_map/ppermute | solution.py:350
  1326.3 358.0 %collective-permute-start.30 = (f32[512,2048]{1,0:T(8,128)S(1)}, f32[512,2048]{1,0:T(8,128)}, u32[]{:S(2)}, u32[]{:S(2)}) collective-permute-start(f32[512,2048]{1,0:T(8,128)S(1)} %copy-done.4), channel_id=1, source_target_pairs={{0,2},{1,3},{2,0},{3,1},{4,6},{5,7},{6,4},{7,5}} | collective-permute-start | bytes 12582920 | tf_op jit(solution)/shard_map/ppermute | solution.py:350
  1408.5 268.9 %collective-permute-start.32 = (f32[512,2048]{1,0:T(8,128)S(1)}, f32[512,2048]{1,0:T(8,128)}, u32[]{:S(2)}, u32[]{:S(2)}) collective-permute-start(f32[512,2048]{1,0:T(8,128)S(1)} %copy-done.5), channel_id=1, source_target_pairs={{0,2},{1,3},{2,0},{3,1},{4,6},{5,7},{6,4},{7,5}} | collective-permute-start | bytes 12582920 | tf_op jit(solution)/shard_map/ppermute | solution.py:350
  1498.4 35.6 %collective-permute-start.31 = (f32[512,2048]{1,0:T(8,128)}, f32[512,2048]{1,0:T(8,128)}, u32[]{:S(2)}, u32[]{:S(2)}) collective-permute-start(f32[512,2048]{1,0:T(8,128)} %fusion.3), channel_id=1, source_target_pairs={{0,1},{1,0},{2,3},{3,2},{4,5},{5,4},{6,7},{7,6}} | collective-permute-start | bytes 12582920 | tf_op jit(solution)/shard_map/ppermute | solution.py:350
  1498.4 185.9 %collective-permute-start.29 = (f32[512,2048]{1,0:T(8,128)}, f32[512,2048]{1,0:T(8,128)}, u32[]{:S(2)}, u32[]{:S(2)}) collective-permute-start(f32[512,2048]{1,0:T(8,128)} %fusion.5), channel_id=1, source_target_pairs={{0,1},{1,0},{2,3},{3,2},{4,5},{5,4},{6,7},{7,6}} | collective-permute-start | bytes 12582920 | tf_op jit(solution)/shard_map/ppermute | solution.py:350
  (34 other events, 1017.1 us)

commit v5 on v4

--- a/solution.py
+++ b/solution.py
@@ -387,7 +387,7 @@
                 late = [after(g, prev) for g in rights]
                 given = to_peer(part(2, late), 1)
                 mine = lax.optimization_barrier(part(3, late))
-                return mine, given, got
+                return lax.optimization_barrier(mine + given), got
 
             return rest, far
 
@@ -397,11 +397,14 @@
             pos4 = lax.dynamic_update_slice_in_dim(pos4, got, me ^ bits, axis=0)
         x4 = x_loc.reshape(shape4)
         x_parts = []
-        x_near = piece(x4, 1, 0, n_seq)[0]
-        x4 = after(x4, x_near)
         for c in range(N_CHUNK):
-            x_parts.append([piece(x4, bits, c * step, step)[0] for bits in (2, 3)])
-            x4 = after(x4, *x_parts[-1])
+            x_parts.append([])
+            for bits in (2, 3):
+                x_parts[-1].append(piece(x4, bits, c * step, step)[0])
+                x4 = after(x4, *x_parts[-1])
+            if c == 0:
+                x_near = piece(x4, 1, 0, n_seq)[0]
+                x4 = after(x4, x_near)
         x_far = [[to_peer(p, bits) for p, bits in zip(x_parts[c], (2, 3))] for c in range(N_CHUNK)]
         dy4 = after(grad_y.reshape(shape4), *x_parts[1])
         x_near = to_peer(x_near, 1)
@@ -454,6 +457,8 @@
         for rest in (w_q, w_k, w_v, w_o):
             sums.append(rest(prev))
             prev = sums[-1][0]
+        g_wq, g_wv, g_wo = (sums[n][0] + sums[n][1] for n in (0, 2, 3))
+        g_wk = after(sums[1][0], g_wq, g_wv, g_wo) + sums[1][1]
         for bits, got in zip(far_bits, y_got):
             y = put(y, after(got, prev), bits, 0)
         for c in range(N_CHUNK):
@@ -461,9 +466,8 @@
                 gx = put(gx, got, bits, c * step)
         gains = gains + to_peer(gains, 1)
         gains = lax.dynamic_slice_in_dim(gains, me * (d_model // n_sp), d_model // n_sp, axis=1)
-        total = lambda terms: terms[0] + terms[1] + terms[2]
         join = lambda arr: arr.reshape(x_loc.shape)
-        return (join(y), join(gx), gains[0], *map(total, sums), gains[1], gains[2])
+        return (join(y), join(gx), gains[0], g_wq, g_wk, g_wv, g_wo, gains[1], gains[2])
 
     seq_spec = P('dp', 'sp', None)
     mat_rep = P(None, None)

time: 1700 us -> 1800 us (1.059)
  waiting for transfers between devices: 625 us -> 742 us
    ppermute x37, waiting for transfers between devices: 625 us -> 742 us  [to_peer(): return lax.ppermute(value, 'sp', [(i, i ^ bits) for i in range(n_sp)])]
  transfers between devices with their start and end apart: 37 -> 37, of which waited for: 10 -> 8; matrix products, arithmetic and copies ran while one was open for 22% -> 17% of each run, Pallas kernels for 20% -> 19%
where the time goes in v5:
time: 1800 us
  waiting for transfers between devices  742 us (41%)
  Pallas kernels  586 us (33%)
  matrix products  297 us (16%)
  local copies, waits for them, and re-layouts  88.3 us (5%)
  other arithmetic  56.3 us (3%)
  starting transfers between devices  25.6 us (1%)
    ppermute x37, waiting for transfers between devices, to_peer(): return lax.ppermute(value, 'sp', [(i, i ^ bits) for i in range(n_sp)])  742 us
    dot_general x20, matrix products, dot_tn(): lax.dot_general(a, b, (((0,), (0,)), ((), ())), preferred_element_type=F32)  209 us
    pallas_call x2, Pallas kernels, tail(): pl.pallas_call(tail_kernel, grid=(n_piece, n_seq), in_specs=[loc] * 2 + [...  168 us
    pallas_call x2, Pallas kernels, attend_back(): pl.pallas_call(attend_back_kernel, grid=(n_seq, n_heads // heads), in_spe...  159 us
    pallas_call x3, Pallas kernels, front(): pl.pallas_call(front_own_kernel if own else front_kernel, grid_spec=pltpu...  154 us
    pallas_call x2, Pallas kernels, attend(): pl.pallas_call(attend_kernel, grid_spec=pltpu.PrefetchScalarGridSpec(num_...  105 us
    dot_general x2, matrix products, dot_nt(): lax.dot_general(a, b, (((1,), (1,)), ((), ())), preferred_element_type=F32)  46 us
    dynamic_update_slice x15, local copies, waits for them, and re-layouts, put(): return lax.dynamic_update_slice(buf, got, (me ^ bits, seq0, 0, 0))  42.9 us
  transfers between devices with their start and end apart: 37, of which 8 were waited for; matrix products, arithmetic and copies ran while one was open for 17% of the time, Pallas kernels for 19%

profile of v5, /device:TPU:0, one launch (start us, length us, event | category | flops | bytes accessed | tf_op | source)
XLA Modules:
  0.0 1796.9 jit_solution(11962355710715782037)
XLA Ops:
  23.6 9.2 constant_dynamic-slice_fusion.8
  34.7 72.2 %collective-permute-done.2 = s32[1,4,256]{2,1,0:T(4,128)S(1)} collective-permute-done((s32[1,4,256]{2,1,0:T(4,128)S(1)}, s32[1,4,256]{2,1,0:T(4,128)S(1)}, u32[]{:S(2)}, u32[]{:S(2)}) %collective-permute-start.2) | collective-permute-done | bytes 4128 | tf_op jit(solution)/shard_map/ppermute | solution.py:350
  107.4 44.1 %collective-permute-done.3 = s32[1,4,256]{2,1,0:T(4,128)S(1)} collective-permute-done((s32[1,4,256]{2,1,0:T(4,128)S(1)}, s32[1,4,256]{2,1,0:T(4,128)S(1)}, u32[]{:S(2)}, u32[]{:S(2)}) %collective-permute-start.3) | collective-permute-done | bytes 4128 | tf_op jit(solution)/shard_map/ppermute | solution.py:350
  165.5 72.6 %front.3 = (bf16[4,4,256,2048]{3,2,1,0:T(8,128)(2,1)}, bf16[4,4,256,2048]{3,2,1,0:T(8,128)(2,1)}, bf16[4,4,256,2048]{3,2,1,0:T(8,128)(2,1)}, bf16[4,4,256,2048]{...) custom-call(s32[1]{0:T(128)} %bitcast.refs_0_.me_ref, ...), custom_call_target="tpu_custom_call" | custom-call | flops 51539607552 | bytes 109051904 | tf_op jit(solution)/shard_map/front/pallas_call | solution.py:123
  240.2 40.8 %front.4 = (bf16[4,4,256,2048]{3,2,1,0:T(8,128)(2,1)}, bf16[4,4,256,2048]{3,2,1,0:T(8,128)(2,1)}, bf16[4,4,256,2048]{3,2,1,0:T(8,128)(2,1)}, bf16[4,4,256,2048]{...) custom-call(s32[1]{0:T(128)} %bitcast.refs_0_.me_ref, ...), custom_call_target="tpu_custom_call", output_to_operand_aliasing={{0}: (11, {}), {1}: (12, {}), {2}: (13, {}), {3}: (14, {}),... | custom-call | flops 25769803776 | bytes 67108864 | tf_op jit(solution)/shard_map/front/pallas_call | solution.py:123
  281.0 52.5 %attend.2 = (bf16[4,2,256,2048]{3,2,1,0:T(8,128)(2,1)}, bf16[4,4,256,2048]{3,2,1,0:T(8,128)(2,1)}, f32[4,16,1,1024]{3,2,1,0:T(1,128)}) custom-call(s32[1]{0:T(128)} %bitcast.refs_0_.me_ref, bf16[4,4,256,2048]{3,2,1,0:T(8,128)(2,1)} %get-tuple-element.116.q_ref.refs_2_, bf16[4,4,256,2048]{3,2,1,0:T(8,128)(2,1)} %get-tuple-element.117.k_ref.refs_3_, ...), custom_call_target="tpu_custom_call" | custom-call | flops 25769803776 | bytes 41943040 | tf_op jit(solution)/shard_map/attend/pallas_call | solution.py:177
  334.3 40.9 %front.5 = (bf16[4,4,256,2048]{3,2,1,0:T(8,128)(2,1)}, bf16[4,4,256,2048]{3,2,1,0:T(8,128)(2,1)}, bf16[4,4,256,2048]{3,2,1,0:T(8,128)(2,1)}, bf16[4,4,256,2048]{...) custom-call(s32[1]{0:T(128)} %bitcast.refs_0_.me_ref, ...), custom_call_target="tpu_custom_call", output_to_operand_aliasing={{0}: (11, {}), {1}: (12, {}), {2}: (13, {}), {3}: (14, {}),... | custom-call | flops 25769803776 | bytes 67108864 | tf_op jit(solution)/shard_map/front/pallas_call | solution.py:123
  375.2 52.6 %attend.3 = (bf16[4,2,256,2048]{3,2,1,0:T(8,128)(2,1)}, bf16[4,4,256,2048]{3,2,1,0:T(8,128)(2,1)}, f32[4,16,1,1024]{3,2,1,0:T(1,128)}) custom-call(s32[1]{0:T(128)} %bitcast.refs_0_.me_ref, bf16[4,4,256,2048]{3,2,1,0:T(8,128)(2,1)} %get-tuple-element.126.q_ref, ...), custom_call_target="tpu_custom_call", output_to_operand_aliasing={{1}: (4, {}), {2}: (5, {})} | custom-call | flops 25769803776 | bytes 41943040 | tf_op jit(solution)/shard_map/attend/pallas_call | solution.py:177
  427.7 41.5 %fusion = bf16[4096,2048]{1,0:T(8,128)(2,1)S(1)} fusion(bf16[4,4,256,2048]{3,2,1,0:T(8,128)(2,1)} %get-tuple-element.125.x_ref, bf16[4096,2048]{1,0:T(8,128)(2,1)} %bitcast.147, bf16[2048,2048]{1,0:T(8,128)(2,1)} %param.17), kind=kOutput, calls=%fused_computation.1 | convolution fusion | flops 34384904192 | bytes 58720256 | tf_op jit(solution)/shard_map/dot_general | solution.py:23
  486.5 23.7 %convolution_convert_fusion.1 = bf16[2048,2048]{1,0:T(8,128)(2,1)} fusion(bf16[2048,2048]{1,0:T(8,128)(2,1)} %bitcast.140, bf16[2048,2048]{1,0:T(8,128)(2,1)} %param.17), kind=kOutput, calls=%fused_computation.3 | convolution fusion | flops 17184063488 | bytes 25165824 | tf_op jit(solution)/shard_map/dot_general | solution.py:27
  510.2 79.4 %attend_back.2 = (bf16[4,2,256,2048]{3,2,1,0:T(8,128)(2,1)}, bf16[4,2,256,2048]{3,2,1,0:T(8,128)(2,1)}, bf16[4,4,256,2048]{3,2,1,0:T(8,128)(2,1)}) custom-call(bf16[4,4,256,2048]{3,2,1,0:T(8,128)(2,1)} %get-tuple-element.126.q_ref, bf16[4,4,256,2048]{3,2,1,0:T(8,128)(2,1)} %get-tuple-element.127.k_ref, bf16[4,4,256,2048]{3,2,1,0:T(8,128)(2,1)} %get-tuple-element.128.v_ref, ...), custom_call_target="tpu_custom_call" | custom-call | flops 60129542144 | bytes 58720256 | tf_op jit(solution)/shard_map/attend_back/pallas_call | solution.py:241
  621.9 22.2 %convolution_convert_fusion = bf16[2048,2048]{1,0:T(8,128)(2,1)} fusion(bf16[2048,2048]{1,0:T(8,128)(2,1)S(1)} %bitcast.71, bf16[2048,2048]{1,0:T(8,128)(2,1)} %param.17), kind=kOutput, calls=%fused_computation.2 | convolution fusion | flops 17184063488 | bytes 25165824 | tf_op jit(solution)/shard_map/dot_general | solution.py:27
  646.8 79.8 %attend_back.3 = (bf16[4,2,256,2048]{3,2,1,0:T(8,128)(2,1)}, bf16[4,2,256,2048]{3,2,1,0:T(8,128)(2,1)}, bf16[4,4,256,2048]{3,2,1,0:T(8,128)(2,1)}) custom-call(bf16[4,4,256,2048]{3,2,1,0:T(8,128)(2,1)} %get-tuple-element.126.q_ref, bf16[4,4,256,2048]{3,2,1,0:T(8,128)(2,1)} %get-tuple-element.127.k_ref, ...), custom_call_target="tpu_custom_call", output_to_operand_aliasing={{2}: (5, {})} | custom-call | flops 60129542144 | bytes 58720256 | tf_op jit(solution)/shard_map/attend_back/pallas_call | solution.py:241
  726.6 15.1 fusion.11
  742.2 10.6 fusion.17
  755.7 83.8 %tail.2 = (bf16[4,4,256,2048]{3,2,1,0:T(8,128)(2,1)}, bf16[4,4,256,2048]{3,2,1,0:T(8,128)(2,1)}, bf16[4,4,256,2048]{3,2,1,0:T(8,128)(2,1)}, f32[1,2048]{1,0:T(1,...) custom-call(bf16[4,2,256,2048]{3,2,1,0:T(8,128)(2,1)} %get-tuple-element.143.dq_ref, ...), custom_call_target="tpu_custom_call" | custom-call | flops 51539607552 | bytes 125829120 | tf_op jit(solution)/shard_map/tail/pallas_call | solution.py:319
  845.2 83.9 %tail.3 = (bf16[4,4,256,2048]{3,2,1,0:T(8,128)(2,1)}, bf16[4,4,256,2048]{3,2,1,0:T(8,128)(2,1)}, bf16[4,4,256,2048]{3,2,1,0:T(8,128)(2,1)}, f32[1,2048]{1,0:T(1,...) custom-call(bf16[4,2,256,2048]{3,2,1,0:T(8,128)(2,1)} %get-tuple-elemen, ...), custom_call_target="tpu_custom_call", output_to_operand_aliasing={{0}: (15, {}), {1}: (16, {}), {2}: (17, {})} | custom-call | flops 51539607552 | bytes 125829120 | tf_op jit(solution)/shard_map/tail/pallas_call | solution.py:319
  935.5 15.1 fusion.9
  950.6 12.1 fusion.15
  965.6 13.7 fusion.7
  979.8 11.7 fusion.13
  994.2 13.7 fusion.5
  1008.0 11.8 fusion.23
  1022.6 13.7 fusion.3
  1036.8 11.7 fusion.21
  1051.3 13.8 fusion.1
  1069.6 11.7 fusion.19
  1093.1 112.1 %collective-permute-done.25 = bf16[1,2,256,2048]{3,2,1,0:T(8,128)(2,1)} collective-permute-done((bf16[1,2,256,2048]{3,2,1,0:T(8,128)(2,1)}, bf16[1,2,256,2048]{3,2,1,0:T(8,128)(2,1)}, u32[]{:S(2)}, u32[]{:S(2)}) %collective-permute-start.25) | collective-permute-done | bytes 2097184 | tf_op jit(solution)/shard_map/ppermute | solution.py:350
  1214.0 79.7 %collective-permute-done.26 = bf16[1,2,256,2048]{3,2,1,0:T(8,128)(2,1)} collective-permute-done((bf16[1,2,256,2048]{3,2,1,0:T(8,128)(2,1)}, bf16[1,2,256,2048]{3,2,1,0:T(8,128)(2,1)}, u32[]{:S(2)}, u32[]{:S(2)}) %collective-permute-start.26) | collective-permute-done | bytes 2097184 | tf_op jit(solution)/shard_map/ppermute | solution.py:350
  1303.6 124.9 %collective-permute-done.29 = bf16[1,2,256,2048]{3,2,1,0:T(8,128)(2,1)} collective-permute-done((bf16[1,2,256,2048]{3,2,1,0:T(8,128)(2,1)}, bf16[1,2,256,2048]{3,2,1,0:T(8,128)(2,1)}, u32[]{:S(2)}, u32[]{:S(2)}) %collective-permute-start.29) | collective-permute-done | bytes 2097184 | tf_op jit(solution)/shard_map/ppermute | solution.py:350
  1470.0 231.9 %collective-permute-done.35 = f32[512,2048]{1,0:T(8,128)} collective-permute-done((f32[512,2048]{1,0:T(8,128)S(1)}, f32[512,2048]{1,0:T(8,128)}, u32[]{:S(2)}, u32[]{:S(2)}) %collective-permute-start.35) | collective-permute-done | bytes 4194336 | tf_op jit(solution)/shard_map/ppermute | solution.py:350
  1715.8 75.7 %collective-permute-done.36 = f32[512,2048]{1,0:T(8,128)} collective-permute-done((f32[512,2048]{1,0:T(8,128)}, f32[512,2048]{1,0:T(8,128)}, u32[]{:S(2)}, u32[]{:S(2)}) %collective-permute-start.36) | collective-permute-done | bytes 4194336 | tf_op jit(solution)/shard_map/ppermute | solution.py:350
  (214 shorter events, 216.8 us)
Async XLA Ops:
  11.8 153.6 %collective-permute-start.7 = (bf16[4,256,2048]{2,1,0:T(8,128)(2,1)}, bf16[4,256,2048]{2,1,0:T(8,128)(2,1)}, u32[]{:S(2)}, u32[]{:S(2)}) collective-permute-start(bf16[4,256,2048]{2,1,0:T(8,128)(2,1)} %dynamic-slice_bitcast_fusion), channel_id=1, source_target_pairs={{0,1},{1,0},{2,3},{3,2},{4,5},{5,4},{6,7},{7,6}} | collective-permute-start | bytes 12582920 | tf_op jit(solution)/shard_map/ppermute | solution.py:350
  12.6 225.4 %collective-permute-start.6 = (bf16[2,256,2048]{2,1,0:T(8,128)(2,1)}, bf16[2,256,2048]{2,1,0:T(8,128)(2,1)}, u32[]{:S(2)}, u32[]{:S(2)}) collective-permute-start(bf16[2,256,2048]{2,1,0:T(8,128)(2,1)} %dynamic-slice_bitcast_fusion.3), channel_id=1, source_target_pairs={{0,3},{1,2},{2,1},{3,0},{4,7},{5,6},{6,5},{7,4}} | collective-permute-start | bytes 6291464 | tf_op jit(solution)/shard_map/ppermute | solution.py:350
  15.2 223.6 %collective-permute-start.5 = (bf16[2,256,2048]{2,1,0:T(8,128)(2,1)}, bf16[2,256,2048]{2,1,0:T(8,128)(2,1)}, u32[]{:S(2)}, u32[]{:S(2)}) collective-permute-start(bf16[2,256,2048]{2,1,0:T(8,128)(2,1)} %dynamic-slice_bitcast_fusion.4), channel_id=1, source_target_pairs={{0,2},{1,3},{2,0},{3,1},{4,6},{5,7},{6,4},{7,5}} | collective-permute-start | bytes 6291464 | tf_op jit(solution)/shard_map/ppermute | solution.py:350
  15.3 91.6 %collective-permute-start.2 = (s32[1,4,256]{2,1,0:T(4,128)S(1)}, s32[1,4,256]{2,1,0:T(4,128)S(1)}, u32[]{:S(2)}, u32[]{:S(2)}) collective-permute-start(s32[1,4,256]{2,1,0:T(4,128)S(1)} %get-tuple-element.105), channel_id=1, source_target_pairs={{0,2},{1,3},{2,0},{3,1},{4,6},{5,7},{6,4},{7,5}} | collective-permute-start | bytes 12296 | tf_op jit(solution)/shard_map/ppermute | solution.py:350
  23.6 309.8 %collective-permute-start.1 = (bf16[2,256,2048]{2,1,0:T(8,128)(2,1)}, bf16[2,256,2048]{2,1,0:T(8,128)(2,1)}, u32[]{:S(2)}, u32[]{:S(2)}) collective-permute-start(bf16[2,256,2048]{2,1,0:T(8,128)(2,1)} %dynamic-slice_bitcast_fusion.1), channel_id=1, source_target_pairs={{0,3},{1,2},{2,1},{3,0},{4,7},{5,6},{6,5},{7,4}} | collective-permute-start | bytes 6291464 | tf_op jit(solution)/shard_map/ppermute | solution.py:350
  106.9 44.7 %collective-permute-start.3 = (s32[1,4,256]{2,1,0:T(4,128)S(1)}, s32[1,4,256]{2,1,0:T(4,128)S(1)}, u32[]{:S(2)}, u32[]{:S(2)}) collective-permute-start(s32[1,4,256]{2,1,0:T(4,128)S(1)} %get-tuple-element.106), channel_id=1, source_target_pairs={{0,3},{1,2},{2,1},{3,0},{4,7},{5,6},{6,5},{7,4}} | collective-permute-start | bytes 12296 | tf_op jit(solution)/shard_map/ppermute | solution.py:350
  152.7 180.8 %collective-permute-start = (bf16[2,256,2048]{2,1,0:T(8,128)(2,1)}, bf16[2,256,2048]{2,1,0:T(8,128)(2,1)}, u32[]{:S(2)}, u32[]{:S(2)}) collective-permute-start(bf16[2,256,2048]{2,1,0:T(8,128)(2,1)} %dynamic-slice_bitcast_fusion.2), channel_id=1, source_target_pairs={{0,2},{1,3},{2,0},{3,1},{4,6},{5,7},{6,4},{7,5}} | collective-permute-start | bytes 6291464 | tf_op jit(solution)/shard_map/ppermute | solution.py:350
  165.4 308.7 %collective-permute-start.11 = (bf16[1,2,256,2048]{3,2,1,0:T(8,128)(2,1)}, bf16[1,2,256,2048]{3,2,1,0:T(8,128)(2,1)}, u32[]{:S(2)}, u32[]{:S(2)}) collective-permute-start(bf16[1,2,256,2048]{3,2,1,0:T(8,128)(2,1)} %get-tuple-element.200), channel_id=1, source_target_pairs={{0,1},{1,0},{2,3},{3,2},{4,5},{5,4},{6,7},{7,6}} | collective-permute-start | bytes 6291464 | tf_op jit(solution)/shard_map/ppermute | solution.py:350
  238.1 237.4 %collective-permute-start.10 = (bf16[1,2,256,2048]{3,2,1,0:T(8,128)(2,1)}, bf16[1,2,256,2048]{3,2,1,0:T(8,128)(2,1)}, u32[]{:S(2)}, u32[]{:S(2)}) collective-permute-start(bf16[1,2,256,2048]{3,2,1,0:T(8,128)(2,1)} %get-tuple-element.201), channel_id=1, source_target_pairs={{0,3},{1,2},{2,1},{3,0},{4,7},{5,6},{6,5},{7,4}} | collective-permute-start | bytes 6291464 | tf_op jit(solution)/shard_map/ppermute | solution.py:350
  238.8 236.6 %collective-permute-start.9 = (bf16[1,2,256,2048]{3,2,1,0:T(8,128)(2,1)}, bf16[1,2,256,2048]{3,2,1,0:T(8,128)(2,1)}, u32[]{:S(2)}, u32[]{:S(2)}) collective-permute-start(bf16[1,2,256,2048]{3,2,1,0:T(8,128)(2,1)} %get-tuple-element.202), channel_id=1, source_target_pairs={{0,2},{1,3},{2,0},{3,1},{4,6},{5,7},{6,4},{7,5}} | collective-permute-start | bytes 6291464 | tf_op jit(solution)/shard_map/ppermute | solution.py:350
  333.5 263.7 %collective-permute-start.14 = (bf16[1,2,256,2048]{3,2,1,0:T(8,128)(2,1)}, bf16[1,2,256,2048]{3,2,1,0:T(8,128)(2,1)}, u32[]{:S(2)}, u32[]{:S(2)}) collective-permute-start(bf16[1,2,256,2048]{3,2,1,0:T(8,128)(2,1)} %get-tuple-element.197), channel_id=1, source_target_pairs={{0,1},{1,0},{2,3},{3,2},{4,5},{5,4},{6,7},{7,6}} | collective-permute-start | bytes 6291464 | tf_op jit(solution)/shard_map/ppermute | solution.py:350
  333.5 263.7 %collective-permute-start.13 = (bf16[1,2,256,2048]{3,2,1,0:T(8,128)(2,1)}, bf16[1,2,256,2048]{3,2,1,0:T(8,128)(2,1)}, u32[]{:S(2)}, u32[]{:S(2)}) collective-permute-start(bf16[1,2,256,2048]{3,2,1,0:T(8,128)(2,1)} %get-tuple-element.198), channel_id=1, source_target_pairs={{0,3},{1,2},{2,1},{3,0},{4,7},{5,6},{6,5},{7,4}} | collective-permute-start | bytes 6291464 | tf_op jit(solution)/shard_map/ppermute | solution.py:350
  474.1 130.9 %collective-permute-start.12 = (bf16[1,2,256,2048]{3,2,1,0:T(8,128)(2,1)}, bf16[1,2,256,2048]{3,2,1,0:T(8,128)(2,1)}, u32[]{:S(2)}, u32[]{:S(2)}) collective-permute-start(bf16[1,2,256,2048]{3,2,1,0:T(8,128)(2,1)} %get-tuple-element.199), channel_id=1, source_target_pairs={{0,2},{1,3},{2,0},{3,1},{4,6},{5,7},{6,4},{7,5}} | collective-permute-start | bytes 6291464 | tf_op jit(solution)/shard_map/ppermute | solution.py:350
  617.0 27.1 %collective-permute-start.15 = (f32[512,2048]{1,0:T(8,128)}, f32[512,2048]{1,0:T(8,128)S(1)}, u32[]{:S(2)}, u32[]{:S(2)}) collective-permute-start(f32[512,2048]{1,0:T(8,128)} %convolution_add_fusion.2), channel_id=1, source_target_pairs={{0,1},{1,0},{2,3},{3,2},{4,5},{5,4},{6,7},{7,6}} | collective-permute-start | bytes 12582920 | tf_op jit(solution)/shard_map/ppermute | solution.py:350
  950.6 12.2 collective-permute-start.17
  979.3 12.2 collective-permute-start.18
  1036.3 12.2 collective-permute-start.20
  1065.1 16.2 collective-permute-start.21
  1066.6 363.1 %collective-permute-start.34 = (f32[512,2048]{1,0:T(8,128)}, f32[512,2048]{1,0:T(8,128)}, u32[]{:S(2)}, u32[]{:S(2)}) collective-permute-start(f32[512,2048]{1,0:T(8,128)} %add.55), channel_id=1, source_target_pairs={{0,2},{1,3},{2,0},{3,1},{4,6},{5,7},{6,4},{7,5}} | collective-permute-start | bytes 12582920 | tf_op jit(solution)/shard_map/ppermute | solution.py:350
  1067.3 138.0 %collective-permute-start.25 = (bf16[1,2,256,2048]{3,2,1,0:T(8,128)(2,1)}, bf16[1,2,256,2048]{3,2,1,0:T(8,128)(2,1)}, u32[]{:S(2)}, u32[]{:S(2)}) collective-permute-start(bf16[1,2,256,2048]{3,2,1,0:T(8,128)(2,1)} %get-tuple-element.158), channel_id=1, source_target_pairs={{0,2},{1,3},{2,0},{3,1},{4,6},{5,7},{6,4},{7,5}} | collective-permute-start | bytes 6291464 | tf_op jit(solution)/shard_map/ppermute | solution.py:350
  1068.6 227.7 %collective-permute-start.28 = (bf16[1,2,256,2048]{3,2,1,0:T(8,128)(2,1)}, bf16[1,2,256,2048]{3,2,1,0:T(8,128)(2,1)}, u32[]{:S(2)}, u32[]{:S(2)}) collective-permute-start(bf16[1,2,256,2048]{3,2,1,0:T(8,128)(2,1)} %get-tuple-element.166), channel_id=1, source_target_pairs={{0,2},{1,3},{2,0},{3,1},{4,6},{5,7},{6,4},{7,5}} | collective-permute-start | bytes 6291464 | tf_op jit(solution)/shard_map/ppermute | solution.py:350
  1069.3 224.3 %collective-permute-start.26 = (bf16[1,2,256,2048]{3,2,1,0:T(8,128)(2,1)}, bf16[1,2,256,2048]{3,2,1,0:T(8,128)(2,1)}, u32[]{:S(2)}, u32[]{:S(2)}) collective-permute-start(bf16[1,2,256,2048]{3,2,1,0:T(8,128)(2,1)} %get-tuple-element.180), channel_id=1, source_target_pairs={{0,3},{1,2},{2,1},{3,0},{4,7},{5,6},{6,5},{7,4}} | collective-permute-start | bytes 6291464 | tf_op jit(solution)/shard_map/ppermute | solution.py:350
  1093.1 201.9 %collective-permute-start.27 = (bf16[1,2,256,2048]{3,2,1,0:T(8,128)(2,1)S(1)}, bf16[1,2,256,2048]{3,2,1,0:T(8,128)(2,1)S(1)}, u32[]{:S(2)}, u32[]{:S(2)}) collective-permute-start(bf16[1,2,256,2048]{3,2,1,0:T(8,128)(2,1)S(1)} %copy-done.9), channel_id=1, source_target_pairs={{0,1},{1,0},{2,3},{3,2},{4,5},{5,4},{6,7},{7,6}} | collective-permute-start | bytes 6291464 | tf_op jit(solution)/shard_map/ppermute | solution.py:350
  1205.3 225.3 %collective-permute-start.33 = (f32[512,2048]{1,0:T(8,128)}, f32[512,2048]{1,0:T(8,128)}, u32[]{:S(2)}, u32[]{:S(2)}) collective-permute-start(f32[512,2048]{1,0:T(8,128)} %add.56), channel_id=1, source_target_pairs={{0,2},{1,3},{2,0},{3,1},{4,6},{5,7},{6,4},{7,5}} | collective-permute-start | bytes 12582920 | tf_op jit(solution)/shard_map/ppermute | solution.py:350
  1293.6 146.0 %collective-permute-start.22 = (f32[512,2048]{1,0:T(8,128)}, f32[512,2048]{1,0:T(8,128)}, u32[]{:S(2)}, u32[]{:S(2)}) collective-permute-start(f32[512,2048]{1,0:T(8,128)} %convolution_add_fusion), channel_id=1, source_target_pairs={{0,1},{1,0},{2,3},{3,2},{4,5},{5,4},{6,7},{7,6}} | collective-permute-start | bytes 12582920 | tf_op jit(solution)/shard_map/ppermute | solution.py:350
  1295.0 133.5 %collective-permute-start.29 = (bf16[1,2,256,2048]{3,2,1,0:T(8,128)(2,1)}, bf16[1,2,256,2048]{3,2,1,0:T(8,128)(2,1)}, u32[]{:S(2)}, u32[]{:S(2)}) collective-permute-start(bf16[1,2,256,2048]{3,2,1,0:T(8,128)(2,1)} %get-tuple-element.182), channel_id=1, source_target_pairs={{0,3},{1,2},{2,1},{3,0},{4,7},{5,6},{6,5},{7,4}} | collective-permute-start | bytes 6291464 | tf_op jit(solution)/shard_map/ppermute | solution.py:350
  1296.3 133.2 %collective-permute-start.30 = (bf16[1,2,256,2048]{3,2,1,0:T(8,128)(2,1)S(1)}, bf16[1,2,256,2048]{3,2,1,0:T(8,128)(2,1)}, u32[]{:S(2)}, u32[]{:S(2)}) collective-permute-start(bf16[1,2,256,2048]{3,2,1,0:T(8,128)(2,1)S(1)} %copy-done.8), channel_id=1, source_target_pairs={{0,1},{1,0},{2,3},{3,2},{4,5},{5,4},{6,7},{7,6}} | collective-permute-start | bytes 6291464 | tf_op jit(solution)/shard_map/ppermute | solution.py:350
  1428.4 278.7 %collective-permute-start.8 = (bf16[1,4,256,2048]{3,2,1,0:T(8,128)(2,1)}, bf16[1,4,256,2048]{3,2,1,0:T(8,128)(2,1)}, u32[]{:S(2)}, u32[]{:S(2)}) collective-permute-start(bf16[1,4,256,2048]{3,2,1,0:T(8,128)(2,1)} %get-tuple-element.132), channel_id=1, source_target_pairs={{0,2},{1,3},{2,0},{3,1},{4,6},{5,7},{6,4},{7,5}} | collective-permute-start | bytes 12582920 | tf_op jit(solution)/shard_map/ppermute | solution.py:350
  1429.5 277.6 %collective-permute-start.24 = (bf16[1,4,256,2048]{3,2,1,0:T(8,128)(2,1)}, bf16[1,4,256,2048]{3,2,1,0:T(8,128)(2,1)}, u32[]{:S(2)}, u32[]{:S(2)}) collective-permute-start(bf16[1,4,256,2048]{3,2,1,0:T(8,128)(2,1)} %get-tuple-element.177), channel_id=1, source_target_pairs={{0,1},{1,0},{2,3},{3,2},{4,5},{5,4},{6,7},{7,6}} | collective-permute-start | bytes 12582920 | tf_op jit(solution)/shard_map/ppermute | solution.py:350
  1429.7 277.5 %collective-permute-start.23 = (bf16[1,4,256,2048]{3,2,1,0:T(8,128)(2,1)}, bf16[1,4,256,2048]{3,2,1,0:T(8,128)(2,1)}, u32[]{:S(2)}, u32[]{:S(2)}) collective-permute-start(bf16[1,4,256,2048]{3,2,1,0:T(8,128)(2,1)} %get-tuple-element.175), channel_id=1, source_target_pairs={{0,3},{1,2},{2,1},{3,0},{4,7},{5,6},{6,5},{7,4}} | collective-permute-start | bytes 12582920 | tf_op jit(solution)/shard_map/ppermute | solution.py:350
  1430.6 271.4 %collective-permute-start.35 = (f32[512,2048]{1,0:T(8,128)S(1)}, f32[512,2048]{1,0:T(8,128)}, u32[]{:S(2)}, u32[]{:S(2)}) collective-permute-start(f32[512,2048]{1,0:T(8,128)S(1)} %copy-done.7), channel_id=1, source_target_pairs={{0,2},{1,3},{2,0},{3,1},{4,6},{5,7},{6,4},{7,5}} | collective-permute-start | bytes 12582920 | tf_op jit(solution)/shard_map/ppermute | solution.py:350
  1439.6 351.9 %collective-permute-start.36 = (f32[512,2048]{1,0:T(8,128)}, f32[512,2048]{1,0:T(8,128)}, u32[]{:S(2)}, u32[]{:S(2)}) collective-permute-start(f32[512,2048]{1,0:T(8,128)} %add.57), channel_id=1, source_target_pairs={{0,2},{1,3},{2,0},{3,1},{4,6},{5,7},{6,4},{7,5}} | collective-permute-start | bytes 12582920 | tf_op jit(solution)/shard_map/ppermute | solution.py:350
  (45 other events, 2276.7 us)
